TPU v7x, 32 devices: a whole 2x2x4 slice. The times are simulated.
32 devices in a mesh: dp: 4 (over z), expert: 2 (over core), tensor: 4 (over y, x).
Axes of the slice: x: 2, y: 2, z: 4, core: 2. Of those that a mesh axis runs over, the one named last changes fastest.
Arguments:
- tokens: bfloat16 [2048, 1536], P(('dp', 'expert')), may hold values from -6 to 6
- gain_attn: float32 [1536], replicated, may hold values from 0.5 to 1.5
- w_query: bfloat16 [1536, 1536], P(None, 'tensor'), may hold values from -0.15625 to 0.15625
- key_projection: bfloat16 [1536, 512], P(None, 'tensor'), may hold values from -0.15625 to 0.15625
- value_projection: bfloat16 [1536, 512], P(None, 'tensor'), may hold values from -0.15625 to 0.15625
- w_out: bfloat16 [1536, 1536], P('tensor'), may hold values from -0.625 to 0.625
- gain_moe: float32 [1536], replicated, may hold values from 0.5 to 1.5
- w_router: bfloat16 [1536, 40], replicated, may hold values from -0.15625 to 0.15625
- w_gate: bfloat16 [40, 1536, 512], P('expert', None, 'tensor'), may hold values from -0.15625 to 0.15625
- w_up: bfloat16 [40, 1536, 512], P('expert', None, 'tensor'), may hold values from -0.15625 to 0.15625
- w_down: bfloat16 [40, 512, 1536], P('expert', 'tensor'), may hold values from -0.5 to 0.5
- routes: int32 [2048, 8], P(('dp', 'expert')), may hold values from 0 to 39, all different within a row; in each aligned block of 256 rows (0 to 255, 256 to 511, ...) at most 64 rows name the same one
- cotangent: bfloat16 [2048, 1536], P(('dp', 'expert')), may hold values from -6 to 6
Outputs:
- output: bfloat16 [2048, 1536], P(('dp', 'expert'))
- input_grad: bfloat16 [2048, 1536], P(('dp', 'expert'))
- gain_attn_grad: float32 [1536], P(('dp', 'expert'))
- query_grad: float32 [1536, 1536], P(('dp', 'expert'), 'tensor')
- key_grad: float32 [1536, 512], P(('dp', 'expert'), 'tensor')
- value_grad: float32 [1536, 512], P(('dp', 'expert'), 'tensor')
- out_grad: float32 [1536, 1536], P('tensor', ('dp', 'expert'))
- gain_moe_grad: float32 [1536], P(('dp', 'expert'))
- router_grad: float32 [1536, 40], P(('dp', 'expert'))
- gate_grad: float32 [40, 1536, 512], P('expert', 'dp', 'tensor')
- up_grad: float32 [40, 1536, 512], P('expert', 'dp', 'tensor')
- down_grad: float32 [40, 512, 1536], P('expert', 'tensor', 'dp')
Inputs may be any that keep to these rules, and one draw needn't show every extreme that they name: `routes`: each row names 8 different experts. Within the rows of one sequence (aligned blocks of 256 rows) no expert is named by more than 64 rows, and in every draw some expert is named by exactly 64 rows of some block.
All inputs are finite; a program needn't handle non-finite values.
Results may differ from a plain program's by a relative error of at most 0.023.
Values may be sent and summed in bfloat16 or wider, within the bound.
A program may use at most 256 MiB of HBM per device.

v0:
```python
import math

import jax
import jax.numpy as jnp
from jax import lax
from jax.sharding import PartitionSpec as P

HEAD_SIZE = 64
SEQUENCE_LENGTH = 256
CAP = 64


EPSILON = 1e-06
ROPE_BASE = 10000.0
BLOCK_ROWS = 512


def split_up(x, dim, count):
    dims = x.shape
    tiles = x.reshape(*dims[:dim], count, dims[dim] // count, *dims[dim + 1 :])
    return jnp.moveaxis(tiles, dim, 0)


def sum_at_owner(x, axis, dim):
    tiles = split_up(x, dim, lax.axis_size(axis))
    arrived = lax.all_to_all(tiles, axis, split_axis=0, concat_axis=0, tiled=True)
    return arrived.astype(jnp.float32).sum(axis=0)


def side_by_side(arrays, axis, dim, along):
    both = jnp.concatenate(arrays, axis=along)
    filled, at, outs = (sum_at_owner(both, axis, dim), 0, [])
    for a in arrays:
        outs.append(lax.slice_in_dim(filled, at, at + a.shape[along], axis=along))
        at += a.shape[along]
    return tuple(outs)


def sent_together(arrays, axis, dim, along):
    widths = [math.prod(a.shape[along:]) for a in arrays]
    both = jnp.concatenate(
        [a.reshape(*a.shape[:along], w) for a, w in zip(arrays, widths)], axis=along
    )
    filled = sum_at_owner(both, axis, dim)
    tiles = jnp.split(filled, [sum(widths[:k]) for k in range(1, len(widths))], axis=along)
    return tuple(
        (b.reshape(*filled.shape[:along], *a.shape[along:]) for a, b in zip(arrays, tiles))
    )


def rms_scale(hidden):
    return lax.rsqrt(jnp.mean(hidden * hidden, axis=-1, keepdims=True) + EPSILON)


def norm_back(hidden, scaling, gain_vec, grad_out):
    weighted = grad_out * gain_vec
    gain_grad = jnp.sum(grad_out * hidden * scaling, axis=0)
    inner_mean = jnp.mean(weighted * hidden, axis=-1, keepdims=True)
    return (scaling * weighted - hidden * (scaling * scaling * scaling) * inner_mean, gain_grad)


def rope_tables(positions, head_dim):
    half_dim = head_dim // 2
    frequency = jnp.exp(
        jnp.arange(half_dim, dtype=jnp.float32) * (-2.0 * math.log(ROPE_BASE) / head_dim)
    )
    angles = positions[:, None] * frequency[None, :]
    return (jnp.cos(angles), jnp.sin(angles))


def apply_rotary(vectors, cosine_table, sine_component):
    half_dim = vectors.shape[-1] // 2
    first_half = vectors[..., :half_dim]
    second_half = vectors[..., half_dim:]
    cos_rows = cosine_table[:, None, :]
    sin_rows = sine_component[:, None, :]
    return jnp.concatenate(
        [
            first_half * cos_rows - second_half * sin_rows,
            first_half * sin_rows + second_half * cos_rows,
        ],
        axis=-1,
    )


def slot_table(route_ids, expert_count, capacity):
    number_of_rows, top_count = route_ids.shape
    flat_ids = route_ids.reshape(-1)
    one_hot = (flat_ids[:, None] == jnp.arange(expert_count, dtype=jnp.int32)[None, :]).astype(
        jnp.int32
    )
    earlier = jnp.cumsum(one_hot, axis=0) - one_hot
    slot_ids = jnp.sum(earlier * one_hot, axis=1)
    slot_where = flat_ids * capacity + slot_ids
    pick_ids = jnp.arange(number_of_rows * top_count, dtype=jnp.int32)
    token_of = (
        jnp.full((expert_count * capacity,), number_of_rows, jnp.int32)
        .at[slot_where]
        .set(pick_ids // top_count)
    )
    pick_of = (
        jnp.full((expert_count * capacity,), number_of_rows * top_count, jnp.int32)
        .at[slot_where]
        .set(pick_ids)
    )
    return (slot_where, token_of, pick_of)


def block_scores(query_rows, key_rows, query_group_width):
    block_len = query_rows.shape[0]
    key_count, kv_heads, head_dim = key_rows.shape
    grouped = query_rows.reshape(block_len, kv_heads, query_group_width, head_dim)
    scores = jnp.einsum(
        "qhgd,khd->hgqk", grouped, key_rows, preferred_element_type=jnp.float32
    ) * head_dim ** (-0.5)
    row_pos = jnp.arange(block_len, dtype=jnp.int32)[:, None]
    col_pos = jnp.arange(key_count, dtype=jnp.int32)[None, :]
    return (jnp.where(col_pos <= row_pos, scores, -1e30), grouped)


def sequence_forward(query_rows, key_rows, value_rows, query_group_width):
    length, kv_heads, head_dim = key_rows.shape
    block_len = min(BLOCK_ROWS, length)
    scores, grouped = block_scores(query_rows, key_rows, query_group_width)
    largest = jnp.max(scores, axis=-1, keepdims=True)
    log_total = largest + jnp.log(jnp.sum(jnp.exp(scores - largest), axis=-1, keepdims=True))
    weights = jnp.exp(scores - log_total).astype(jnp.bfloat16)
    attended = jnp.einsum("hgqk,khd->qhgd", weights, value_rows, preferred_element_type=jnp.float32)
    outputs = attended.reshape(block_len, -1, head_dim).astype(jnp.bfloat16)
    return (outputs, log_total)


def sequence_backward(
    query_rows, key_rows, value_rows, attended, log_total, d_attended, query_group_width
):
    length, kv_heads, head_dim = key_rows.shape
    block_len = min(BLOCK_ROWS, length)
    scale_factor = head_dim ** (-0.5)
    key_gradient = jnp.zeros((length, kv_heads, head_dim), jnp.float32)
    value_gradient = jnp.zeros((length, kv_heads, head_dim), jnp.float32)
    scores, grouped = block_scores(query_rows, key_rows, query_group_width)
    weights = jnp.exp(scores - log_total)
    d_grouped = d_attended.reshape(block_len, kv_heads, query_group_width, head_dim)
    o_grouped = attended.reshape(block_len, kv_heads, query_group_width, head_dim)
    delta = jnp.sum(d_grouped.astype(jnp.float32) * o_grouped.astype(jnp.float32), axis=-1)
    delta = jnp.transpose(delta, (1, 2, 0))[..., None]
    d_weights = jnp.einsum(
        "qhgd,khd->hgqk", d_grouped, value_rows, preferred_element_type=jnp.float32
    )
    d_scores = (weights * (d_weights - delta)).astype(jnp.bfloat16)
    block_query = (
        jnp.einsum("hgqk,khd->qhgd", d_scores, key_rows, preferred_element_type=jnp.float32)
        * scale_factor
    )
    query_parts = block_query.reshape(block_len, -1, head_dim)
    key_gradient = key_gradient.at[:block_len].add(
        jnp.einsum("hgqk,qhgd->khd", d_scores, grouped, preferred_element_type=jnp.float32)
        * scale_factor
    )
    value_gradient = value_gradient.at[:block_len].add(
        jnp.einsum(
            "hgqk,qhgd->khd",
            weights.astype(jnp.bfloat16),
            d_grouped,
            preferred_element_type=jnp.float32,
        )
    )
    return (query_parts, key_gradient, value_gradient)


def local(
    tokens,
    gain_attn,
    w_query,
    key_projection,
    value_projection,
    w_out,
    gain_moe,
    w_router,
    w_gate,
    w_up,
    w_down,
    routes,
    cotangent,
):
    number_of_rows, model_width = tokens.shape
    head_dim = HEAD_SIZE
    query_heads = w_query.shape[1] // head_dim
    kv_heads = key_projection.shape[1] // head_dim
    query_group_width = query_heads // kv_heads
    expert_count = w_router.shape[1]
    local_experts = w_gate.shape[0]
    source_count = expert_count // local_experts
    capacity = CAP
    top_count = routes.shape[1]
    resid = tokens.astype(jnp.float32)
    scale_one = rms_scale(resid)
    first_normalized = (resid * scale_one * gain_attn).astype(jnp.bfloat16)
    positions = (jnp.arange(number_of_rows, dtype=jnp.int32) % SEQUENCE_LENGTH).astype(jnp.float32)
    cosine_table, sine_component = rope_tables(positions, head_dim)
    q_lin = jnp.dot(first_normalized, w_query, preferred_element_type=jnp.float32).reshape(
        number_of_rows, query_heads, head_dim
    )
    linear_key = jnp.dot(
        first_normalized, key_projection, preferred_element_type=jnp.float32
    ).reshape(number_of_rows, kv_heads, head_dim)
    value_reduced = (
        jnp.dot(first_normalized, value_projection, preferred_element_type=jnp.float32)
        .astype(jnp.bfloat16)
        .reshape(number_of_rows, kv_heads, head_dim)
    )
    q_rot = apply_rotary(q_lin, cosine_table, sine_component).astype(jnp.bfloat16)
    rotated_key = apply_rotary(linear_key, cosine_table, sine_component).astype(jnp.bfloat16)
    attended, log_total = sequence_forward(q_rot, rotated_key, value_reduced, query_group_width)
    flat_att = attended.reshape(number_of_rows, query_heads * head_dim)
    attn_part = jnp.dot(flat_att, w_out, preferred_element_type=jnp.float32)
    hidden1 = resid + lax.psum(attn_part.astype(jnp.bfloat16), "tensor").astype(jnp.float32)
    scale_two = rms_scale(hidden1)
    normed2 = (hidden1 * scale_two * gain_moe).astype(jnp.bfloat16)
    logits = jnp.dot(normed2, w_router, preferred_element_type=jnp.float32)
    chosen = jnp.take_along_axis(logits, routes, axis=1)
    gate_probs = jax.nn.softmax(chosen, axis=-1)
    slot_where, token_of, pick_of = slot_table(routes, expert_count, capacity)
    normed_pad = jnp.concatenate([normed2, jnp.zeros((1, model_width), jnp.bfloat16)], axis=0)
    outgoing = normed_pad[token_of].reshape(expert_count, capacity, model_width)
    received = lax.all_to_all(outgoing, "expert", split_axis=0, concat_axis=0, tiled=True)
    arrived = received.reshape(source_count, local_experts, capacity, model_width)
    gate_pre = jnp.einsum("secd,edh->sech", arrived, w_gate, preferred_element_type=jnp.float32)
    up_pre = jnp.einsum("secd,edh->sech", arrived, w_up, preferred_element_type=jnp.float32)
    sig_gate = jax.nn.sigmoid(gate_pre)
    activated = gate_pre * sig_gate
    hid_low = (activated * up_pre).astype(jnp.bfloat16)
    expert_out = jnp.einsum(
        "sech,ehd->secd", hid_low, w_down, preferred_element_type=jnp.float32
    ).astype(jnp.bfloat16)
    returned = lax.all_to_all(
        expert_out.reshape(expert_count, capacity, model_width),
        "expert",
        split_axis=0,
        concat_axis=0,
        tiled=True,
    )
    picked = returned.reshape(expert_count * capacity, model_width)[slot_where].reshape(
        number_of_rows, top_count, model_width
    )
    moe_part = jnp.zeros((number_of_rows, model_width), jnp.float32)
    for choice_index in range(top_count):
        moe_part = (
            moe_part
            + picked[:, choice_index].astype(jnp.float32)
            * gate_probs[:, choice_index : choice_index + 1]
        )
    moe_out = lax.psum(moe_part.astype(jnp.bfloat16), "tensor").astype(jnp.float32)
    output = (hidden1 + moe_out).astype(jnp.bfloat16)
    grad = cotangent.astype(jnp.float32)
    gate_dot = jnp.einsum("rjd,rd->rj", picked, cotangent, preferred_element_type=jnp.float32)
    grad_pad = jnp.concatenate([cotangent, jnp.zeros((1, model_width), jnp.bfloat16)], axis=0)
    gate_pad = jnp.concatenate([gate_probs.reshape(-1), jnp.zeros((1,), jnp.float32)], axis=0)
    sent_grad = (grad_pad[token_of].astype(jnp.float32) * gate_pad[pick_of][:, None]).astype(
        jnp.bfloat16
    )
    sent_grad = sent_grad.reshape(expert_count, capacity, model_width)
    grad_received = lax.all_to_all(sent_grad, "expert", split_axis=0, concat_axis=0, tiled=True)
    arrived_grad = grad_received.reshape(source_count, local_experts, capacity, model_width)
    d_hid = jnp.einsum("secd,ehd->sech", arrived_grad, w_down, preferred_element_type=jnp.float32)
    down_local = jnp.einsum(
        "sech,secd->ehd", hid_low, arrived_grad, preferred_element_type=jnp.float32
    )
    d_gate = (d_hid * up_pre * sig_gate * (1.0 + gate_pre * (1.0 - sig_gate))).astype(jnp.bfloat16)
    d_up = (d_hid * activated).astype(jnp.bfloat16)
    gate_local = jnp.einsum("secd,sech->edh", arrived, d_gate, preferred_element_type=jnp.float32)
    up_local = jnp.einsum("secd,sech->edh", arrived, d_up, preferred_element_type=jnp.float32)
    back_rows = jnp.einsum("sech,edh->secd", d_gate, w_gate, preferred_element_type=jnp.float32)
    back_rows = (
        back_rows + jnp.einsum("sech,edh->secd", d_up, w_up, preferred_element_type=jnp.float32)
    ).astype(jnp.bfloat16)
    came_back = lax.all_to_all(
        back_rows.reshape(expert_count, capacity, model_width),
        "expert",
        split_axis=0,
        concat_axis=0,
        tiled=True,
    )
    back_picked = came_back.reshape(expert_count * capacity, model_width)[slot_where].reshape(
        number_of_rows, top_count, model_width
    )
    back_part = jnp.zeros((number_of_rows, model_width), jnp.float32)
    for choice_index in range(top_count):
        back_part = back_part + back_picked[:, choice_index].astype(jnp.float32)
    back_total, dgate = (
        lax.psum(back_part.astype(jnp.bfloat16), "tensor").astype(jnp.float32),
        lax.psum(gate_dot.astype(jnp.bfloat16), "tensor").astype(jnp.float32),
    )
    inner_sum = jnp.sum(gate_probs * dgate, axis=1, keepdims=True)
    d_chosen = gate_probs * (dgate - inner_sum)
    matches = routes[:, :, None] == jnp.arange(expert_count, dtype=jnp.int32)[None, None, :]
    d_logits = jnp.sum(jnp.where(matches, d_chosen[:, :, None], 0.0), axis=1).astype(jnp.bfloat16)
    router_local = jnp.dot(normed2.T, d_logits, preferred_element_type=jnp.float32)
    d_normed2 = back_total + jnp.dot(d_logits, w_router.T, preferred_element_type=jnp.float32)
    d_hidden_part, gain_moe_local = norm_back(hidden1, scale_two, gain_moe, d_normed2)
    d_hidden1 = grad + d_hidden_part
    d_mixed = d_hidden1.astype(jnp.bfloat16)
    out_local = jnp.dot(flat_att.T, d_mixed, preferred_element_type=jnp.float32)
    d_att = (
        jnp.dot(d_mixed, w_out.T, preferred_element_type=jnp.float32)
        .astype(jnp.bfloat16)
        .reshape(number_of_rows, query_heads, head_dim)
    )
    dq_rot, rotated_key_gradient, dv_rows = sequence_backward(
        q_rot, rotated_key, value_reduced, attended, log_total, d_att, query_group_width
    )
    d_query = (
        apply_rotary(dq_rot, cosine_table, -sine_component)
        .astype(jnp.bfloat16)
        .reshape(number_of_rows, query_heads * head_dim)
    )
    key_gradient = (
        apply_rotary(rotated_key_gradient, cosine_table, -sine_component)
        .astype(jnp.bfloat16)
        .reshape(number_of_rows, kv_heads * head_dim)
    )
    value_gradient = dv_rows.astype(jnp.bfloat16).reshape(number_of_rows, kv_heads * head_dim)
    query_local = jnp.dot(first_normalized.T, d_query, preferred_element_type=jnp.float32)
    key_local = jnp.dot(first_normalized.T, key_gradient, preferred_element_type=jnp.float32)
    value_local = jnp.dot(first_normalized.T, value_gradient, preferred_element_type=jnp.float32)
    d_normed_part = jnp.dot(d_query, w_query.T, preferred_element_type=jnp.float32)
    d_normed_part = d_normed_part + jnp.dot(
        key_gradient, key_projection.T, preferred_element_type=jnp.float32
    )
    d_normed_part = d_normed_part + jnp.dot(
        value_gradient, value_projection.T, preferred_element_type=jnp.float32
    )
    d_normed1 = lax.psum(d_normed_part.astype(jnp.bfloat16), "tensor").astype(jnp.float32)
    d_resid_part, gain_attn_local = norm_back(resid, scale_one, gain_attn, d_normed1)
    input_grad = (d_hidden1 + d_resid_part).astype(jnp.bfloat16)
    gate_grad, up_grad, down_grad = (
        lax.psum_scatter(
            gate_local.astype(jnp.bfloat16), "dp", scatter_dimension=1, tiled=True
        ).astype(jnp.float32),
        lax.psum_scatter(
            up_local.astype(jnp.bfloat16), "dp", scatter_dimension=1, tiled=True
        ).astype(jnp.float32),
        lax.psum_scatter(
            down_local.astype(jnp.bfloat16), "dp", scatter_dimension=2, tiled=True
        ).astype(jnp.float32),
    )
    query_grad, key_grad, value_grad, out_grad, router_grad, gain_attn_grad, gain_moe_grad = (
        *side_by_side(
            (
                query_local.astype(jnp.bfloat16),
                key_local.astype(jnp.bfloat16),
                value_local.astype(jnp.bfloat16),
            ),
            ("dp", "expert"),
            0,
            1,
        ),
        sum_at_owner(out_local.astype(jnp.bfloat16), ("dp", "expert"), 1),
        *sent_together(
            (
                router_local.astype(jnp.bfloat16),
                gain_attn_local.astype(jnp.bfloat16),
                gain_moe_local.astype(jnp.bfloat16),
            ),
            ("dp", "expert"),
            0,
            1,
        ),
    )
    return (
        output,
        input_grad,
        gain_attn_grad,
        query_grad,
        key_grad,
        value_grad,
        out_grad,
        gain_moe_grad,
        router_grad,
        gate_grad,
        up_grad,
        down_grad,
    )


def solution(mesh):
    placed = (
        P(("dp", "expert"), None),
        P(),
        P(None, "tensor"),
        P(None, "tensor"),
        P(None, "tensor"),
        P("tensor", None),
        P(),
        P(),
        P("expert", None, "tensor"),
        P("expert", None, "tensor"),
        P("expert", "tensor", None),
        P(("dp", "expert"), None),
        P(("dp", "expert"), None),
    )
    return jax.shard_map(
        local,
        mesh=mesh,
        in_specs=placed,
        out_specs=(
            P(("dp", "expert"), None),
            P(("dp", "expert"), None),
            P(("dp", "expert")),
            P(("dp", "expert"), "tensor"),
            P(("dp", "expert"), "tensor"),
            P(("dp", "expert"), "tensor"),
            P("tensor", ("dp", "expert")),
            P(("dp", "expert")),
            P(("dp", "expert"), None),
            P("expert", "dp", "tensor"),
            P("expert", "dp", "tensor"),
            P("expert", "tensor", "dp"),
        ),
        check_vma=False,
    )
```

profile of v0, /device:TPU:0, one launch (start us, length us, event | category | flops | bytes accessed | tf_op | source)
XLA Modules:
  0.0 966.7 jit_solution(1960256116302737873)
XLA Ops:
  18.8 11.3 %reduce-window.6 = s32[40,16,128]{2,1,0:T(8,128)S(1)} reduce-window(s32[40,16,128]{2,1,0:T(8,128)S(1)} %fusion.73, s32[]{:T(128)} %constant.139.clone.1), window={size=1x1x128 pad=0_0x0_0x127_0}, to_apply=%region_5.6 | reduce-window | flops 10403840 | bytes 655364 | tf_op jit(solution)/shard_map/reduce-window
  31.1 8.1 scatter_custom_fusion.1
  39.2 8.1 scatter_custom_fusion
  48.5 9.6 gather_fusion.2
  59.3 10.2 %all-reduce.7.cloned.1.call-done = bf16[256,1536]{1,0:T(8,128)(2,1)} async-done(((bf16[256,1536]{1,0:T(8,128)(2,1)}), bf16[256,1536]{1,0:T(8,128)(2,1)}) %all-reduce.7.cloned.1.call-update) | async-done | bytes 786448 | tf_op jit(solution)/shard_map/psum | solution.py:217
  73.7 16.8 %gather_fusion.5 = f32[2048]{0:T(1024)S(1)} fusion(f32[256,40]{0,1:T(8,128)S(1)} %fusion.111, s32[2048]{0:T(1024)S(1)} %reshape.509), kind=kCustom, calls=%fused_computation.5 | custom fusion | bytes 32768 | tf_op jit(solution)/shard_map/jit(take_along_axis)/gather | solution.py:221
  91.3 9.6 gather_fusion
  100.8 12.1 %all_to_all.35 = bf16[40,64,1536]{2,1,0:T(8,128)(2,1)S(1)} all-to-all(bf16[40,64,1536]{2,1,0:T(8,128)(2,1)} %bitcast.259), channel_id=1, replica_groups=mesh['dp'=4,'expert'=2,'tensor'=4] {'expert'}, dimensions={0} | all-to-all | bytes 15728640 | tf_op jit(solution)/shard_map/all_to_all | solution.py:226
  112.9 8.3 fusion.50
  134.0 17.9 %all_to_all.36 = bf16[40,64,1536]{2,1,0:T(8,128)(2,1)} all-to-all(bf16[40,64,1536]{2,1,0:T(8,128)(2,1)} %bitcast.260), channel_id=1, replica_groups=mesh['dp'=4,'expert'=2,'tensor'=4] {'expert'}, dimensions={0} | all-to-all | bytes 15728640 | tf_op jit(solution)/shard_map/all_to_all | solution.py:236
  152.0 17.6 %gather_fusion.1 = bf16[2048,1536]{1,0:T(8,128)(2,1)} fusion(bf16[2560,1536]{1,0:T(8,128)(2,1)} %bitcast.249, s32[2048]{0:T(1024)S(1)} %copy-done.50), kind=kCustom, calls=%fused_computation.1 | custom fusion | bytes 12591104 | tf_op jit(solution)/shard_map/gather | solution.py:243
  175.8 9.3 psum.38
  186.1 13.6 %gather_fusion.3 = f32[2560]{0:T(1024)S(1)} fusion(f32[2049]{0:T(1024)S(1)} %pad_maximum_fusion.7, s32[3072]{0:T(1024)S(1)} %copy-done.51), kind=kCustom, calls=%fused_computation.3 | custom fusion | bytes 30720 | tf_op jit(solution)/shard_map/gather | solution.py:259
  199.8 7.7 fusion
  214.3 31.4 %fusion.106 = (bf16[256,1,1536]{2,1,0:T(2,128)(2,1)}, bf16[256,1,1536]{2,1,0:T(2,128)(2,1)}, bf16[256,1,1536]{2,1,0:T(2,128)(2,1)}, bf16[256,1,1536]{2,1,0:T(2,1...) fusion(bf16[256,8,1536]{2,1,0:T(8,128)(2,1)} %bitcast.254), kind=kLoop, calls=%fused_computation.204 | loop fusion | bytes 12582912 | tf_op jit(solution)/shard_map/slice | solution.py:250
  245.7 8.5 multiply_convert_fusion.1
  254.2 11.4 %fusion.4 = f32[20,2,64,1536]{3,2,1,0:T(8,128)} fusion(bf16[2,20,64,128]{3,2,0,1:T(8,128)(2,1)S(1)} %get-tuple-element.77, bf16[20,1536,128]{2,1,0:T(8,128)(2,1)} %param.29), kind=kOutput, calls=%fused_computation.18 | convolution fusion | flops 1006632960 | bytes 24248320 | tf_op jit(solution)/shard_map/sech,edh->secd/dot_general | solution.py:273
  265.6 13.2 %fusion.18 = bf16[2,20,64,1536]{3,2,0,1:T(8,128)(2,1)} fusion(f32[20,2,64,1536]{3,2,1,0:T(8,128)} %fusion.4, bf16[2,20,64,128]{3,2,0,1:T(8,128)(2,1)S(1)} %get-tuple-element.76, bf16[20,1536,128]{2,1,0:T(8,128)(2,1)} %param.30), kind=kOutput, calls=%fused_computation.31 | convolution fusion | flops 1014497280 | bytes 32112640 | tf_op jit(solution)/shard_map/sech,edh->secd/dot_general | solution.py:275
  282.5 11.5 %all_to_all.37 = bf16[40,64,1536]{2,1,0:T(8,128)(2,1)} all-to-all(bf16[40,64,1536]{2,1,0:T(8,128)(2,1)S(1)} %bitcast.261), channel_id=1, replica_groups=mesh['dp'=4,'expert'=2,'tensor'=4] {'expert'}, dimensions={0} | all-to-all | bytes 15728640 | tf_op jit(solution)/shard_map/all_to_all | solution.py:277
  294.0 17.6 %gather_fusion.4 = bf16[2048,1536]{1,0:T(8,128)(2,1)} fusion(bf16[2560,1536]{1,0:T(8,128)(2,1)} %bitcast.248, s32[2048]{0:T(1024)S(1)} %copy-done.50), kind=kCustom, calls=%fused_computation.4 | custom fusion | bytes 12591104 | tf_op jit(solution)/shard_map/gather | solution.py:284
  311.6 30.3 %fusion.105 = (bf16[256,1,1536]{2,1,0:T(2,128)(2,1)S(1)}, bf16[256,1,1536]{2,1,0:T(2,128)(2,1)S(1)}, bf16[256,1,1536]{2,1,0:T(2,128)(2,1)S(1)}, bf16[256,1,1536]...) fusion(bf16[256,8,1536]{2,1,0:T(8,128)(2,1)} %bitcast.255), kind=kLoop, calls=%fused_computation.203 | loop fusion | bytes 12582912 | tf_op jit(solution)/shard_map/slice | solution.py:289
  352.7 40.2 %all-reduce.9.cloned.1.call-done = bf16[256,1536]{1,0:T(8,128)(2,1)} async-done(((bf16[256,1536]{1,0:T(8,128)(2,1)}), bf16[256,1536]{1,0:T(8,128)(2,1)}) %all-reduce.9.cloned.1.call-update) | async-done | bytes 786448 | tf_op jit(solution)/shard_map/psum | solution.py:291
  408.2 8.6 bitcast_convert_fusion
  416.7 12.3 %copy.320 = bf16[20,128,1536]{1,0,2:T(8,128)(2,1)} copy(bf16[20,128,1536]{2,1,0:T(8,128)(2,1)} %bitcast_convert_fusion) | data formatting | bytes 15728640
  429.0 9.0 copy.398
  439.1 8.7 bitcast_convert_fusion.1
  448.9 8.6 bitcast_convert_fusion.2
  483.7 9.2 all-to-all-done.4
  506.1 50.0 %all-to-all-done.6 = bf16[8,384,192]{1,2,0:T(8,128)(2,1)} async-done(((bf16[8,384,192]{1,2,0:T(8,128)(2,1)}), bf16[8,384,192]{1,2,0:T(8,128)(2,1)}, u32[]{:S(2)}, u32[]{:S(2)}) %all-to-all-start.6) | async-done | bytes 1179680 | tf_op jit(solution)/shard_map/all_to_all | solution.py:26
  569.4 91.0 %all-to-all-done.5 = bf16[8,192,640]{2,1,0:T(8,128)(2,1)} async-done(((bf16[8,192,640]{2,1,0:T(8,128)(2,1)}), bf16[8,192,640]{2,1,0:T(8,128)(2,1)}, u32[]{:S(2)}, u32[]{:S(2)}) %all-to-all-start.5) | async-done | bytes 1966112 | tf_op jit(solution)/shard_map/all_to_all | solution.py:26
  674.4 142.2 %reduce-scatter.8.cloned.1.call-done = bf16[20,384,128]{2,1,0:T(8,128)(2,1)} async-done(((bf16[20,1536,128]{2,1,0:T(8,128)(2,1)}), bf16[20,384,128]{2,1,0:T(8,128)(2,1)}) %reduce-scatter.8.cloned.1.call-update) | async-done | bytes 1966096 | tf_op jit(solution)/shard_map/reduce_scatter | solution.py:340
  820.5 135.0 %reduce-scatter.6.cloned.1.call-done = bf16[20,384,128]{2,1,0:T(8,128)(2,1)} async-done(((bf16[20,1536,128]{2,1,0:T(8,128)(2,1)}), bf16[20,384,128]{2,1,0:T(8,128)(2,1)}) %reduce-scatter.6.cloned.1.call-update) | async-done | bytes 1966096 | tf_op jit(solution)/shard_map/reduce_scatter | solution.py:337
  (262 shorter events, 152.5 us)
Async XLA Ops:
  7.2 9.2 copy-start
  7.2 62.2 %all-reduce.7.cloned.1.call-start = ((), (), s32[]{:S(2)}) async-start(), calls=%async_computation.10 | async-start | bytes 1572864 | tf_op jit(solution)/shard_map/psum | solution.py:217
  58.1 14.1 %copy-start.52 = (f32[1536]{0:T(1024)S(1)}, f32[1536]{0:T(1024)}, u32[]{:S(2)}) copy-start(f32[1536]{0:T(1024)} %param.27) | copy-start | bytes 18436
  90.7 10.2 %copy-start.56 = (f32[256]{0:T(256)}, f32[256]{0:T(256)S(1)}, u32[]{:S(2)}) copy-start(f32[256]{0:T(256)S(1)} %fusion.95) | copy-start | bytes 3076
  100.8 20.4 %slice-start = ((s8[7864320]{0:T(1024)(128)(4,1)}), s8[4194304]{0:T(1024)(128)(4,1)S(1)}, s32[]{:S(2)}) async-start(s8[7864320]{0:T(1024)(128)(4,1)} %bitcast.264), calls=%async_computation.16 | async-start | bytes 8388608
  112.9 8.3 copy-start.1
  112.9 8.4 slice-start.1
  124.6 5.7 copy-start.16
  134.0 17.9 %copy-start.50 = (s32[2048]{0:T(1024)S(1)}, s32[2048]{0:T(1024)}, u32[]{:S(2)}) copy-start(s32[2048]{0:T(1024)} %broadcast_clamp_fusion) | copy-start | bytes 24580
  152.0 17.6 %copy-start.20 = (bf16[256,1536]{1,0:T(8,128)(2,1)S(1)}, bf16[256,1536]{1,0:T(8,128)(2,1)}, u32[]{:S(2)}) copy-start(bf16[256,1536]{1,0:T(8,128)(2,1)} %param.33) | copy-start | bytes 2359300
  169.6 15.6 %copy-start.57 = (f32[256]{0:T(256)S(1)}, f32[256]{0:T(256)}, u32[]{:S(2)}) copy-start(f32[256]{0:T(256)} %copy-done.56) | copy-start | bytes 3076
  169.6 15.6 %copy-start.61 = (f32[256]{0:T(256)S(1)}, f32[256]{0:T(256)}, u32[]{:S(2)}) copy-start(f32[256]{0:T(256)} %fusion.85) | copy-start | bytes 3076
  169.6 16.5 %copy-start.51 = (s32[3072]{0:T(1024)S(1)}, s32[3072]{0:T(1024)}, u32[]{:S(2)}) copy-start(s32[3072]{0:T(1024)} %pad_clamp_fusion) | copy-start | bytes 36868
  207.5 38.2 %all-to-all-start.2 = ((bf16[40,64,1536]{2,1,0:T(8,128)(2,1)}), bf16[40,64,1536]{2,1,0:T(8,128)(2,1)}, u32[]{:S(2)}, u32[]{:S(2)}) async-start(bf16[40,64,1536]{2,1,0:T(8,128)(2,1)} %fusion), calls=%async_computation.2 | async-start | bytes 15728640 | tf_op jit(solution)/shard_map/all_to_all | solution.py:263
  214.2 178.7 %all-reduce.9.cloned.1.call-start = ((), (), s32[]{:S(2)}) async-start(), calls=%async_computation.11 | async-start | bytes 1572864 | tf_op jit(solution)/shard_map/psum | solution.py:291
  254.2 11.4 %copy-start.12 = (bf16[2,20,64,128]{3,2,0,1:T(8,128)(2,1)}, bf16[2,20,64,128]{3,2,0,1:T(8,128)(2,1)S(1)}, u32[]{:S(2)}) copy-start(bf16[2,20,64,128]{3,2,0,1:T(8,128)(2,1)S(1)} %get-tuple-element.77) | copy-start | bytes 1966084
  254.2 11.4 %copy-start.14 = (bf16[2,20,64,128]{3,2,0,1:T(8,128)(2,1)}, bf16[2,20,64,128]{3,2,0,1:T(8,128)(2,1)S(1)}, u32[]{:S(2)}) copy-start(bf16[2,20,64,128]{3,2,0,1:T(8,128)(2,1)S(1)} %get-tuple-element.76) | copy-start | bytes 1966084
  344.1 124.9 %all-reduce.11.cloned.1.call-start = ((), (), s32[]{:S(2)}) async-start(), calls=%async_computation.15 | async-start | bytes 3145728 | tf_op jit(solution)/shard_map/psum | solution.py:253
  345.0 47.9 %copy-start.3 = (bf16[256,1536]{1,0:T(8,128)(2,1)S(1)}, bf16[256,1536]{1,0:T(8,128)(2,1)}, u32[]{:S(2)}) copy-start(bf16[256,1536]{1,0:T(8,128)(2,1)} %param.21) | copy-start | bytes 2359300
  345.0 47.9 %copy-start.11 = (bf16[256,1536]{1,0:T(8,128)(2,1)S(1)}, bf16[256,1536]{1,0:T(8,128)(2,1)}, u32[]{:S(2)}) copy-start(bf16[256,1536]{1,0:T(8,128)(2,1)} %all-reduce.7.cloned.1.call-done) | copy-start | bytes 2359300
  345.0 47.9 %copy-start.53 = (f32[1536]{0:T(1024)S(1)}, f32[1536]{0:T(1024)}, u32[]{:S(2)}) copy-start(f32[1536]{0:T(1024)} %param.27) | copy-start | bytes 18436
  345.0 47.9 %copy-start.59 = (f32[256]{0:T(256)S(1)}, f32[256]{0:T(256)}, u32[]{:S(2)}) copy-start(f32[256]{0:T(256)} %copy-done.58) | copy-start | bytes 3076
  352.7 42.8 %copy-start.62 = (f32[256]{0:T(256)S(1)}, f32[256]{0:T(256)}, u32[]{:S(2)}) copy-start(f32[256]{0:T(256)} %get-tuple-element.105) | copy-start | bytes 3076
  408.1 256.9 %reduce-scatter.10.cloned.1.call-start = ((), (), s32[]{:S(2)}) async-start(), calls=%async_computation.14 | async-start | bytes 9830400
  438.1 378.6 %reduce-scatter.8.cloned.1.call-start = ((), (), s32[]{:S(2)}) async-start(), calls=%async_computation.13 | async-start | bytes 9830400 | tf_op jit(solution)/shard_map/reduce_scatter | solution.py:340
  447.9 507.7 %reduce-scatter.6.cloned.1.call-start = ((), (), s32[]{:S(2)}) async-start(), calls=%async_computation.12 | async-start | bytes 9830400 | tf_op jit(solution)/shard_map/reduce_scatter | solution.py:337
  457.6 11.4 %copy-start.49 = (f32[1536]{0:T(1024)S(1)}, f32[1536]{0:T(1024)}, u32[]{:S(2)}) copy-start(f32[1536]{0:T(1024)} %param.22) | copy-start | bytes 18436
  459.7 19.1 %copy-start.7 = (f32[256,1536]{1,0:T(8,128)S(1)}, f32[256,1536]{1,0:T(8,128)}, u32[]{:S(2)}) copy-start(f32[256,1536]{1,0:T(8,128)} %copy-done.6) | copy-start | bytes 4718596
  474.2 18.7 %all-to-all-start.4 = ((bf16[8,192,42]{1,2,0:T(8,128)(2,1)}), bf16[8,192,42]{1,2,0:T(8,128)(2,1)}, u32[]{:S(2)}, u32[]{:S(2)}) async-start(bf16[8,192,42]{1,2,0:T(8,128)(2,1)} %pad_maximum_fusion.3), calls=%async_computation.4 | async-start | bytes 393216 | tf_op jit(solution)/shard_map/all_to_all | solution.py:26
  483.7 13.9 %copy-start.55 = (f32[256]{0:T(256)S(1)}, f32[256]{0:T(256)}, u32[]{:S(2)}) copy-start(f32[256]{0:T(256)} %copy-done.54) | copy-start | bytes 3076
  492.9 63.3 %all-to-all-start.6 = ((bf16[8,384,192]{1,2,0:T(8,128)(2,1)}), bf16[8,384,192]{1,2,0:T(8,128)(2,1)}, u32[]{:S(2)}, u32[]{:S(2)}) async-start(bf16[8,384,192]{1,2,0:T(8,128)(2,1)} %bitcast.266), calls=%async_computation.6 | async-start | bytes 2359296 | tf_op jit(solution)/shard_map/all_to_all | solution.py:26
  556.1 104.2 %all-to-all-start.5 = ((bf16[8,192,640]{2,1,0:T(8,128)(2,1)}), bf16[8,192,640]{2,1,0:T(8,128)(2,1)}, u32[]{:S(2)}, u32[]{:S(2)}) async-start(bf16[8,192,640]{2,1,0:T(8,128)(2,1)} %bitcast.263), calls=%async_computation.5 | async-start | bytes 3932160 | tf_op jit(solution)/shard_map/all_to_all | solution.py:26
  (44 other events, 84.5 us)
Sparse Core Ops, SparseCore 0:
  18.0 51.4 all-reduce.6
  344.2 48.6 all-reduce.8
  408.2 60.7 all-reduce.10
  471.2 193.7 reduce-scatter.9
  667.1 149.4 reduce-scatter.7
  818.8 136.7 reduce-scatter.5
where the time goes:
time: 976 us; the launch traced here: 967 us
  waiting for transfers between devices  484 us (50%)
  local copies, waits for them, and re-layouts  226 us (23%)
  matrix products  103 us (11%)
  other arithmetic  65.5 us (7%)
  blocking collectives  50.9 us (5%)
  starting transfers between devices  21.6 us (2%)
  between operations  15.5 us (2%)
    all_to_all x3, waiting for transfers between devices, sum_at_owner(): lax.all_to_all(tiles, axis, split_axis=0, concat_axis=0, tiled=True)  150 us
    reduce_scatter x1, waiting for transfers between devices, local(): lax.psum_scatter(up_local.astype(jnp.bfloat16), 'dp', scatter_dimension=1...  142 us
    reduce_scatter x1, waiting for transfers between devices, local(): lax.psum_scatter(gate_local.astype(jnp.bfloat16), 'dp', scatter_dimension...  135 us
    psum x1, waiting for transfers between devices, local(): lax.psum(back_part.astype(jnp.bfloat16), 'tensor').astype(jnp.float32)  40.2 us
    unnamed x137, local copies, waits for them, and re-layouts  36.2 us
    slice x1, local copies, waits for them, and re-layouts, local(): picked[:, choice_index].astype(jnp.float32)  31.4 us
    slice x1, local copies, waits for them, and re-layouts, local(): back_part = back_part + back_picked[:, choice_index].astype(jnp.float32)  30.3 us
  transfers between devices with their start and end apart: 10, of which 9 were waited for; matrix products, arithmetic and copies ran while one was open for 18% of the time, Pallas kernels for 0%

commit v1 on v0

--- a/solution.py
+++ b/solution.py
@@ -3,6 +3,8 @@
 import jax
 import jax.numpy as jnp
 from jax import lax
+from jax.experimental import pallas as pl
+from jax.experimental.pallas import tpu as pltpu
 from jax.sharding import PartitionSpec as P
 
 HEAD_SIZE = 64
@@ -168,7 +170,7 @@
     return (query_parts, key_gradient, value_gradient)
 
 
-def local(
+def reduce_plan(
     tokens,
     gain_attn,
     w_query,
@@ -383,6 +385,332 @@
     )
 
 
+GATHER_ROWS = 4096
+CHUNK = 512
+ALL = ("dp", "expert", "tensor")
+SEQ = ("dp", "expert")
+
+
+def dot(a, b):
+    return jnp.dot(a, b, preferred_element_type=jnp.float32)
+
+
+def dot_nt(a, b):
+    return lax.dot_general(a, b, (((1,), (1,)), ((), ())), preferred_element_type=jnp.float32)
+
+
+def expert_kernel(
+    plane_ref,
+    x_ref,
+    g_ref,
+    xt_ref,
+    gt_ref,
+    gates_ref,
+    wg_ref,
+    wu_ref,
+    wd_ref,
+    gate_grad_ref,
+    up_grad_ref,
+    down_grad_ref,
+    moe_ref,
+    back_ref,
+    dgate_ref,
+    hid_buf,
+    dgate_buf,
+    dup_buf,
+    down_buf,
+    moe_acc,
+    back_acc,
+    dg_acc,
+):
+    step = pl.program_id(0)
+    rows = x_ref.shape[0]
+    width = wg_ref.shape[2]
+    plane_rows = moe_ref.shape[0]
+    plane = plane_ref[0]
+
+    @pl.when(step == 0)
+    def _():
+        moe_acc[...] = jnp.zeros_like(moe_acc)
+        back_acc[...] = jnp.zeros_like(back_acc)
+        dg_acc[...] = jnp.zeros_like(dg_acc)
+
+    k_pos = lax.broadcasted_iota(jnp.int32, (128, 2 * width), 0)
+    l_pos = lax.broadcasted_iota(jnp.int32, (128, 2 * width), 1)
+    pick = jnp.where(k_pos % 64 == 2 * step + l_pos // width, 1.0, 0.0).astype(jnp.bfloat16)
+    wd_pair = wd_ref[...].reshape(2 * width, wd_ref.shape[2])
+
+    def chunk_step(chunk, _):
+        at = pl.ds(pl.multiple_of(chunk * CHUNK, CHUNK), CHUNK)
+        x = x_ref[at, :]
+        gate_pair = dot(gates_ref[at, :], pick)
+        dh_pair = dot_nt(g_ref[at, :], wd_pair)
+        for k in range(2):
+            both = dot(x, jnp.concatenate([wg_ref[k], wu_ref[k]], axis=1))
+            gate_pre, up_pre = both[:, :width], both[:, width:]
+            lanes = slice(k * width, (k + 1) * width)
+            gate = gate_pair[:, lanes]
+            dh = dh_pair[:, lanes]
+            sig = jax.nn.sigmoid(gate_pre)
+            act = gate_pre * sig
+            hid = act * up_pre
+            ghid = hid * gate
+            d_hid = dh * gate
+            dgp = d_hid * up_pre * sig * (1.0 + gate_pre * (1.0 - sig))
+            dup = d_hid * act
+            hid_buf[at, lanes] = ghid.astype(jnp.bfloat16)
+            dgate_buf[at, lanes] = dgp.astype(jnp.bfloat16)
+            dup_buf[at, lanes] = dup.astype(jnp.bfloat16)
+
+            @pl.when(chunk == plane)
+            def _():
+                down_buf[:, lanes] = hid * dh
+
+        return 0
+
+    lax.fori_loop(0, rows // CHUNK, chunk_step, 0)
+    own = pl.ds(pl.multiple_of(plane * plane_rows, plane_rows), plane_rows)
+    moe_acc[...] += dot(hid_buf[own, :], wd_pair)
+    for k in range(2):
+        lanes = slice(k * width, (k + 1) * width)
+        back_acc[...] += dot_nt(dgate_buf[own, lanes], wg_ref[k]) + dot_nt(dup_buf[own, lanes], wu_ref[k])
+        row_sum = jnp.sum(down_buf[:, lanes], axis=1, keepdims=True)
+        lane_of = lax.broadcasted_iota(jnp.int32, dg_acc.shape, 1)
+        dg_acc[...] += jnp.where(lane_of == 2 * step + k, row_sum, 0.0)
+    gate_both = dot(xt_ref[...], dgate_buf[...])
+    up_both = dot(xt_ref[...], dup_buf[...])
+    down_both = dot(gt_ref[...], hid_buf[...]).T
+    for k in range(2):
+        lanes = slice(k * width, (k + 1) * width)
+        gate_grad_ref[k] = gate_both[:, lanes]
+        up_grad_ref[k] = up_both[:, lanes]
+        down_grad_ref[k] = down_both[lanes, :]
+
+    @pl.when(step == pl.num_programs(0) - 1)
+    def _():
+        moe_ref[...] = moe_acc[...].astype(jnp.bfloat16)
+        back_ref[...] = back_acc[...].astype(jnp.bfloat16)
+        dgate_ref[...] = dg_acc[...]
+
+
+def experts(plane, x_all, g_all, x_cols, g_cols, gates, w_gate, w_up, w_down, plane_rows):
+    rows, model = x_all.shape
+    count, _, width = w_gate.shape
+    block = x_cols.shape[0]
+    whole = lambda shape: pl.BlockSpec(shape, lambda i, p: (0,) * len(shape), pipeline_mode=pl.Buffered(1))
+    by_pair = lambda shape: pl.BlockSpec((2,) + shape, lambda i, p: (i, 0, 0))
+    return pl.pallas_call(
+        expert_kernel,
+        grid_spec=pltpu.PrefetchScalarGridSpec(
+            num_scalar_prefetch=1,
+            grid=(count // 2,),
+            in_specs=[
+                whole((rows, model)),
+                whole((rows, model)),
+                whole((block, rows)),
+                whole((block, rows)),
+                whole((rows, 128)),
+                by_pair((model, width)),
+                by_pair((model, width)),
+                by_pair((width, model)),
+            ],
+            out_specs=[
+                by_pair((block, width)),
+                by_pair((block, width)),
+                by_pair((width, block)),
+                whole((plane_rows, model)),
+                whole((plane_rows, model)),
+                whole((plane_rows, 128)),
+            ],
+            scratch_shapes=[
+                pltpu.VMEM((rows, 2 * width), jnp.bfloat16),
+                pltpu.VMEM((rows, 2 * width), jnp.bfloat16),
+                pltpu.VMEM((rows, 2 * width), jnp.bfloat16),
+                pltpu.VMEM((plane_rows, 2 * width), jnp.float32),
+                pltpu.VMEM((plane_rows, model), jnp.float32),
+                pltpu.VMEM((plane_rows, model), jnp.float32),
+                pltpu.VMEM((plane_rows, 128), jnp.float32),
+            ],
+        ),
+        out_shape=[
+            jax.ShapeDtypeStruct((count, block, width), jnp.float32),
+            jax.ShapeDtypeStruct((count, block, width), jnp.float32),
+            jax.ShapeDtypeStruct((count, width, block), jnp.float32),
+            jax.ShapeDtypeStruct((plane_rows, model), jnp.bfloat16),
+            jax.ShapeDtypeStruct((plane_rows, model), jnp.bfloat16),
+            jax.ShapeDtypeStruct((plane_rows, 128), jnp.float32),
+        ],
+        compiler_params=pltpu.CompilerParams(vmem_limit_bytes=60 * 2**20),
+        name="experts",
+    )(plane, x_all, g_all, x_cols, g_cols, gates, w_gate, w_up, w_down)
+
+
+def dense_gates(logits, routes):
+    expert_ids = jnp.arange(logits.shape[1], dtype=jnp.int32)[None, :]
+    chosen = routes[:, 0:1] == expert_ids
+    for j in range(1, routes.shape[1]):
+        chosen = chosen | (routes[:, j : j + 1] == expert_ids)
+    top = jnp.max(jnp.where(chosen, logits, -jnp.inf), axis=1, keepdims=True)
+    weight = jnp.where(chosen, jnp.exp(jnp.where(chosen, logits - top, 0.0)), 0.0)
+    return weight / jnp.sum(weight, axis=1, keepdims=True)
+
+
+def gather_plan(
+    tokens,
+    gain_attn,
+    w_query,
+    key_projection,
+    value_projection,
+    w_out,
+    gain_moe,
+    w_router,
+    w_gate,
+    w_up,
+    w_down,
+    routes,
+    cotangent,
+):
+    number_of_rows, model_width = tokens.shape
+    head_dim = HEAD_SIZE
+    query_heads = w_query.shape[1] // head_dim
+    kv_heads = key_projection.shape[1] // head_dim
+    query_group_width = query_heads // kv_heads
+    expert_count = w_router.shape[1]
+    local_experts = w_gate.shape[0]
+    dp, ex, tp = lax.axis_size("dp"), lax.axis_size("expert"), lax.axis_size("tensor")
+    z, core, t = lax.axis_index("dp"), lax.axis_index("expert"), lax.axis_index("tensor")
+    own_rows = number_of_rows // tp
+    plane_rows = number_of_rows * ex
+    mine = lambda a: lax.dynamic_slice_in_dim(a, t * own_rows, own_rows, axis=0)
+
+    g_all = lax.all_gather(cotangent, SEQ, axis=0, tiled=True)
+    routes_all = lax.all_gather(routes, SEQ, axis=0, tiled=True)
+    resid = tokens.astype(jnp.float32)
+    scale_one = rms_scale(resid)
+    normed1 = (resid * scale_one * gain_attn).astype(jnp.bfloat16)
+    n1_cols = lax.all_to_all(
+        split_up(normed1, 1, dp * ex), SEQ, split_axis=0, concat_axis=0, tiled=True
+    ).reshape(dp * ex * number_of_rows, -1)
+    positions = (jnp.arange(number_of_rows, dtype=jnp.int32) % SEQUENCE_LENGTH).astype(jnp.float32)
+    cosine_table, sine_component = rope_tables(positions, head_dim)
+    q_lin = dot(normed1, w_query).reshape(number_of_rows, query_heads, head_dim)
+    k_lin = dot(normed1, key_projection).reshape(number_of_rows, kv_heads, head_dim)
+    v_low = (
+        dot(normed1, value_projection)
+        .astype(jnp.bfloat16)
+        .reshape(number_of_rows, kv_heads, head_dim)
+    )
+    q_rot = apply_rotary(q_lin, cosine_table, sine_component).astype(jnp.bfloat16)
+    k_rot = apply_rotary(k_lin, cosine_table, sine_component).astype(jnp.bfloat16)
+    attended, log_total = sequence_forward(q_rot, k_rot, v_low, query_group_width)
+    flat_att = attended.reshape(number_of_rows, query_heads * head_dim)
+    att_all = lax.all_gather(flat_att, SEQ, axis=0, tiled=True)
+    attn_part = dot(flat_att, w_out).astype(jnp.bfloat16)
+    resid_own = mine(tokens).astype(jnp.float32)
+    hidden1 = resid_own + lax.psum_scatter(
+        attn_part, "tensor", scatter_dimension=0, tiled=True
+    ).astype(jnp.float32)
+    scale_two = rms_scale(hidden1)
+    normed2 = (hidden1 * scale_two * gain_moe).astype(jnp.bfloat16)
+    x_all = lax.all_gather(normed2, ALL, axis=0, tiled=True)
+
+    gates = dense_gates(dot(x_all, w_router), routes_all)
+    gates_own = lax.dynamic_slice_in_dim(gates, core * local_experts, local_experts, axis=1)
+    high = gates_own.astype(jnp.bfloat16)
+    low = (gates_own - high.astype(jnp.float32)).astype(jnp.bfloat16)
+    pad = jnp.zeros((gates.shape[0], 64 - local_experts), jnp.bfloat16)
+    gate_pack = jnp.concatenate([high, pad, low, pad], axis=1)
+    block = model_width // dp
+    x_cols = lax.dynamic_slice_in_dim(x_all, z * block, block, axis=1).T
+    g_cols = lax.dynamic_slice_in_dim(g_all, z * block, block, axis=1).T
+    plane = z.astype(jnp.int32).reshape(1)
+    gate_grad, up_grad, down_grad, moe_part, back_part, dgate_part = experts(
+        plane, x_all, g_all, x_cols, g_cols, gate_pack, w_gate, w_up, w_down, plane_rows
+    )
+
+    dgate_part = dgate_part[:, :local_experts]
+    wide = jnp.zeros((plane_rows, expert_count), jnp.float32)
+    wide = lax.dynamic_update_slice_in_dim(wide, dgate_part, core * local_experts, axis=1)
+    pair = ("expert", "tensor")
+    back = lax.psum_scatter(back_part, pair, scatter_dimension=0, tiled=True).astype(jnp.float32)
+    moe = lax.psum_scatter(moe_part, pair, scatter_dimension=0, tiled=True).astype(jnp.float32)
+    dgate = lax.psum_scatter(wide, pair, scatter_dimension=0, tiled=True)
+    output_own = (hidden1 + moe).astype(jnp.bfloat16)
+    output = lax.all_gather(output_own, "tensor", axis=0, tiled=True)
+
+    first = ((z * ex + core) * tp + t) * own_rows
+    gates_mine = lax.dynamic_slice_in_dim(gates, first, own_rows, axis=0)
+    inner_sum = jnp.sum(gates_mine * dgate, axis=1, keepdims=True)
+    d_logits = (gates_mine * (dgate - inner_sum)).astype(jnp.bfloat16)
+    d_logits_all = lax.all_gather(d_logits, ALL, axis=0, tiled=True)
+    part = model_width // (dp * ex)
+    seq = z * ex + core
+    x_part = lax.dynamic_slice_in_dim(x_all, seq * part, part, axis=1)
+    router_grad = dot(x_part.T, d_logits_all)
+    d_normed2 = back + dot(d_logits, w_router.T)
+    grad_own = mine(cotangent).astype(jnp.float32)
+    d_hidden_part, gain_moe_local = norm_back(hidden1, scale_two, gain_moe, d_normed2)
+    d_hidden1 = grad_own + d_hidden_part
+    d_mixed_own = d_hidden1.astype(jnp.bfloat16)
+    d_mixed = lax.all_gather(d_mixed_own, "tensor", axis=0, tiled=True)
+    da_cols = lax.all_to_all(
+        split_up(d_mixed, 1, dp * ex), SEQ, split_axis=0, concat_axis=0, tiled=True
+    ).reshape(dp * ex * number_of_rows, -1)
+    out_grad = dot(att_all.T, da_cols)
+    d_att = (
+        dot_nt(d_mixed, w_out)
+        .astype(jnp.bfloat16)
+        .reshape(number_of_rows, query_heads, head_dim)
+    )
+    dq_rot, dk_rot, dv_rows = sequence_backward(
+        q_rot, k_rot, v_low, attended, log_total, d_att, query_group_width
+    )
+    d_query = (
+        apply_rotary(dq_rot, cosine_table, -sine_component)
+        .astype(jnp.bfloat16)
+        .reshape(number_of_rows, query_heads * head_dim)
+    )
+    d_key = (
+        apply_rotary(dk_rot, cosine_table, -sine_component)
+        .astype(jnp.bfloat16)
+        .reshape(number_of_rows, kv_heads * head_dim)
+    )
+    d_value = dv_rows.astype(jnp.bfloat16).reshape(number_of_rows, kv_heads * head_dim)
+    d_qkv = jnp.concatenate([d_query, d_key, d_value], axis=1)
+    d_qkv_all = lax.all_gather(d_qkv, SEQ, axis=0, tiled=True)
+    qkv_grad = dot(n1_cols.T, d_qkv_all)
+    q_width, k_width = d_query.shape[1], d_key.shape[1]
+    query_grad = qkv_grad[:, :q_width]
+    key_grad = qkv_grad[:, q_width : q_width + k_width]
+    value_grad = qkv_grad[:, q_width + k_width :]
+    w_qkv = jnp.concatenate([w_query, key_projection, value_projection], axis=1)
+    d_normed_part = dot_nt(d_qkv, w_qkv).astype(jnp.bfloat16)
+    d_normed1 = lax.psum_scatter(
+        d_normed_part, "tensor", scatter_dimension=0, tiled=True
+    ).astype(jnp.float32)
+    d_resid_part, gain_attn_local = norm_back(resid_own, mine(scale_one), gain_attn, d_normed1)
+    input_own = (d_hidden1 + d_resid_part).astype(jnp.bfloat16)
+    input_grad = lax.all_gather(input_own, "tensor", axis=0, tiled=True)
+    gains = jnp.stack([gain_attn_local, gain_moe_local], axis=0)
+    gains_all = lax.all_gather(gains, ALL, axis=0, tiled=False)
+    gains_sum = gains_all.reshape(-1, 2, model_width).sum(axis=0)
+    gains_mine = lax.dynamic_slice_in_dim(gains_sum, seq * part, part, axis=1)
+    return (
+        output,
+        input_grad,
+        gains_mine[0],
+        query_grad,
+        key_grad,
+        value_grad,
+        out_grad,
+        gains_mine[1],
+        router_grad,
+        gate_grad,
+        up_grad,
+        down_grad,
+    )
+
+
 def solution(mesh):
     placed = (
         P(("dp", "expert"), None),
@@ -399,8 +727,10 @@
         P(("dp", "expert"), None),
         P(("dp", "expert"), None),
     )
+    sequences = mesh.shape["dp"] * mesh.shape["expert"]
+    few = sequences * SEQUENCE_LENGTH <= GATHER_ROWS and mesh.shape["tensor"] == 4
     return jax.shard_map(
-        local,
+        gather_plan if few else reduce_plan,
         mesh=mesh,
         in_specs=placed,
         out_specs=(

time: 976 us -> 715 us (0.73)
  waiting for transfers between devices: 484 us -> 249 us
  local copies, waits for them, and re-layouts: 226 us -> 38.3 us
  blocking collectives: 50.9 us -> 196 us
  Pallas kernels: 0 us -> 144 us
  matrix products: 103 us -> 31.2 us
  other arithmetic: 65.5 us -> 30.9 us
  starting transfers between devices: 21.6 us -> 8.57 us
    all_gather x0 -> x6, blocking collectives: none -> 196 us  [the longest x1 75 us: gather_plan(): d_logits_all = lax.all_gather(d_logits, ALL, axis=0, tiled=True)]
    pallas_call x0 -> x1, Pallas kernels: none -> 144 us  [experts(): pl.pallas_call(expert_kernel, grid_spec=pltpu.PrefetchScalarGridSpec(num_...]
    reduce_scatter x2 -> x5, waiting for transfers between devices: 277 us -> 135 us  [the longest x1 39.9 us: gather_plan(): lax.psum_scatter(back_part, pair, scatter_dimension=0, tiled=True)]
    all_to_all x4 -> x2, waiting for transfers between devices: 150 us -> 37.3 us  [the longest x1 37.3 us: gather_plan(): lax.all_to_all(split_up(normed1, 1, dp * ex), SEQ, split_axis=0, concat_a...]
    gather x10 -> x0, local copies, waits for them, and re-layouts: 85.2 us -> none  [the longest x1 17.6 us: local(): returned.reshape(expert_count * capacity, model_width)[slot_where]]
    all_gather x0 -> x4, waiting for transfers between devices: none -> 74.4 us  [the longest x1 59.2 us: gather_plan(): x_all = lax.all_gather(normed2, ALL, axis=0, tiled=True)]
    dot_general x25 -> x11, matrix products: 99.9 us -> 28 us  [the longest x9 25 us: dot(): return jnp.dot(a, b, preferred_element_type=jnp.float32)]
    slice x5 -> x4, local copies, waits for them, and re-layouts: 63.7 us -> 3.47 us  [the longest x1 1.4 us: gather_plan(): gains_mine[1]]
  transfers between devices with their start and end apart: 10 -> 11, of which waited for: 9 -> 7; matrix products, arithmetic and copies ran while one was open for 18% -> 7% of each run, Pallas kernels for 0% -> 0%
where the time goes in v1:
time: 715 us; the launch traced here: 714 us
  waiting for transfers between devices  249 us (35%)
  blocking collectives  196 us (27%)
  Pallas kernels  144 us (20%)
  local copies, waits for them, and re-layouts  38.3 us (5%)
  matrix products  31.2 us (4%)
  other arithmetic  30.9 us (4%)
  between operations  16.1 us (2%)
  starting transfers between devices  8.57 us (1%)
    pallas_call x1, Pallas kernels, experts(): pl.pallas_call(expert_kernel, grid_spec=pltpu.PrefetchScalarGridSpec(num_...  144 us
    all_gather x1, blocking collectives, gather_plan(): d_logits_all = lax.all_gather(d_logits, ALL, axis=0, tiled=True)  75 us
    all_gather x1, blocking collectives, gather_plan(): gains_all = lax.all_gather(gains, ALL, axis=0, tiled=False)  66.5 us
    all_gather x1, waiting for transfers between devices, gather_plan(): x_all = lax.all_gather(normed2, ALL, axis=0, tiled=True)  59.2 us
    reduce_scatter x1, waiting for transfers between devices, gather_plan(): lax.psum_scatter(back_part, pair, scatter_dimension=0, tiled=True)  39.9 us
    reduce_scatter x1, waiting for transfers between devices, gather_plan(): lax.psum_scatter(moe_part, pair, scatter_dimension=0, tiled=True)  38.3 us
    all_to_all x1, waiting for transfers between devices, gather_plan(): lax.all_to_all(split_up(normed1, 1, dp * ex), SEQ, split_axis=0, concat_a...  37.3 us
    reduce_scatter x1, waiting for transfers between devices, gather_plan(): dgate = lax.psum_scatter(wide, pair, scatter_dimension=0, tiled=True)  30.6 us
  transfers between devices with their start and end apart: 11, of which 7 were waited for; matrix products, arithmetic and copies ran while one was open for 7% of the time, Pallas kernels for 0%

profile of v1, /device:TPU:0, one launch (start us, length us, event | category | flops | bytes accessed | tf_op | source)
XLA Modules:
  0.0 713.6 jit_solution(4844799019787545115)
XLA Ops:
  11.5 1.8 fusion.49
  21.4 2.3 copy.130
  23.8 26.5 %reduce-scatter.16.cloned.1.call-done = bf16[64,1536]{1,0:T(8,128)(2,1)} async-done(((bf16[256,1536]{1,0:T(8,128)(2,1)}), bf16[64,1536]{1,0:T(8,128)(2,1)}) %reduce-scatter.16.cloned.1.call-update) | async-done | bytes 196624 | tf_op jit(solution)/shard_map/reduce_scatter | solution.py:610
  54.3 22.0 %all_gather.35 = s32[2048,8]{0,1:T(8,128)S(1)} all-gather(s32[256,8]{0,1:T(8,128)S(1)} %copy-done.40), channel_id=1, replica_groups=mesh['dp'=4,'expert'=2,'tensor'=4] {'dp','expert'}, dimensions={0}, use_global_device_ids=true | all-gather | bytes 73728 | tf_op jit(solution)/shard_map/all_gather | solution.py:587
  77.0 15.2 %all-gather.10.cloned.1.call-done = bf16[2048,1536]{0,1:T(8,128)(2,1)} async-done(((bf16[256,1536]{0,1:T(8,128)(2,1)}), bf16[2048,1536]{0,1:T(8,128)(2,1)}) %all-gather.10.cloned.1.call-update) | async-done | bytes 6291472 | tf_op jit(solution)/shard_map/all_gather | solution.py:586
  92.2 8.7 %copy.134.g_ref = bf16[2048,1536]{1,0:T(8,128)(2,1)} copy(bf16[2048,1536]{0,1:T(8,128)(2,1)} %all-gather.10.cloned.1.call-done) | data formatting | bytes 12582912 | tf_op jit(solution)/shard_map/all_gather | solution.py:586
  100.9 2.8 dynamic-slice_bitcast_fusion.gt_ref
  103.7 59.2 %all-gather.8.cloned.1.call-done.x_ref = bf16[2048,1536]{1,0:T(8,128)(2,1)} async-done(((bf16[64,1536]{1,0:T(8,128)(2,1)}), bf16[2048,1536]{1,0:T(8,128)(2,1)}) %all-gather.8.cloned.1.call-update) | async-done | bytes 6291472 | tf_op jit(solution)/shard_map/all_gather | solution.py:615
  162.9 7.6 %select_reduce_fusion = (f32[2048]{0:T(1024)S(1)}, f32[2048,40]{1,0:T(8,128)S(1)}) fusion(s32[2048]{0:T(1024)S(1)} %bitcast.146, s32[2048]{0:T(1024)} %bitcast.149, s32[2048]{0:T(1024)} %bitcast.152, s32[2048]{0:T(1024)} %bitcast.155, s32[2048]{0:T(1024)} %bitcast.158, s32[2048]{0:T(1024)} %bitcast.161, s32[2048]{0:T(1024)} %bitcast.164, ...), kind=kOutput, calls=%fused_computation.34 | convolution fusion | flops 253048832 | bytes 6815744 | tf_op jit(solution)/shard_map/dot_general | solution.py:395
  170.6 3.7 fusion.24
  174.3 4.7 fusion.23
  179.0 2.7 constant_dynamic-slice_fusion.1
  181.7 2.6 copy.168
  184.3 2.1 subtract_convert_fusion
  187.9 143.6 %experts.1 = (f32[20,384,128]{2,1,0:T(8,128)}, f32[20,384,128]{2,1,0:T(8,128)}, f32[20,128,384]{2,1,0:T(8,128)}, bf16[512,1536]{1,0:T(8,128)(2,1)}, bf16[512,1536]{1,0:T(8,128)(2,1)}, /*index=5*/f32[512,128]{1,0:T(8,128)}) custom-call(s32[1]{0:T(128)} %bitcast.12.plane_ref, bf16[2048,1536]{1,0:T(8,128)(2,1)} %all-gather.8.cloned.1.call-done.x_ref, ...), custom_call_target="tpu_custom_call" | custom-call | tf_op jit(solution)/shard_map/experts/pallas_call | solution.py:502
  336.0 30.6 %reduce-scatter.14.cloned.1.call-done = f32[64,40]{1,0:T(8,128)} async-done(((f32[512,40]{1,0:T(8,128)}), f32[64,40]{1,0:T(8,128)}) %reduce-scatter.14.cloned.1.call-update) | async-done | bytes 10256 | tf_op jit(solution)/shard_map/reduce_scatter | solution.py:637
  368.3 39.9 %reduce-scatter.20.cloned.1.call-done = bf16[64,1536]{1,0:T(8,128)(2,1)} async-done(((bf16[512,1536]{1,0:T(8,128)(2,1)}), bf16[64,1536]{1,0:T(8,128)(2,1)}) %reduce-scatter.20.cloned.1.call-update) | async-done | bytes 196624 | tf_op jit(solution)/shard_map/reduce_scatter | solution.py:635
  408.2 2.7 multiply_reduce_fusion
  411.5 38.3 %reduce-scatter.18.cloned.1.call-done = bf16[64,1536]{1,0:T(8,128)(2,1)} async-done(((bf16[512,1536]{1,0:T(8,128)(2,1)}), bf16[64,1536]{1,0:T(8,128)(2,1)}) %reduce-scatter.18.cloned.1.call-update) | async-done | bytes 196624 | tf_op jit(solution)/shard_map/reduce_scatter | solution.py:636
  449.8 2.3 fusion.43
  452.0 11.4 %all_gather.37 = bf16[256,1536]{1,0:T(8,128)(2,1)S(1)} all-gather(bf16[64,1536]{1,0:T(8,128)(2,1)S(1)} %get-tuple-element.94), channel_id=1, replica_groups=mesh['dp'=4,'expert'=2,'tensor'=4] {'tensor'}, dimensions={0}, use_global_device_ids=true | all-gather | bytes 983040 | tf_op jit(solution)/shard_map/all_gather | solution.py:655
  474.0 1.8 pad_maximum_fusion.1
  475.8 4.6 all-to-all-start
  481.6 37.3 %all-to-all-done = bf16[8,256,192]{1,2,0:T(8,128)(2,1)S(1)} async-done(((bf16[8,256,192]{1,2,0:T(8,128)(2,1)}), bf16[8,256,192]{1,2,0:T(8,128)(2,1)S(1)}, u32[]{:S(2)}, u32[]{:S(2)}) %all-to-all-start) | async-done | bytes 786464 | tf_op jit(solution)/shard_map/all_to_all | solution.py:591
  518.9 3.5 all-to-all-start.1
  524.8 75.0 %all-gather.2 = bf16[32,64,40]{1,2,0:T(8,128)(2,1)S(1)} all-gather(bf16[1,64,40]{1,2,0:T(8,128)(2,1)S(1)} %copy.148), channel_id=1, replica_groups=mesh['dp'=4,'expert'=2,'tensor'=4] {'dp','expert','tensor'}, dimensions={0}, use_global_device_ids=true | all-gather | bytes 168960 | tf_op jit(solution)/shard_map/all_gather | solution.py:645
  600.1 2.5 fusion.14
  602.7 10.5 %all_gather.36 = bf16[256,1536]{1,0:T(8,128)(2,1)S(1)} all-gather(bf16[64,1536]{1,0:T(8,128)(2,1)} %get-tuple-element.98), channel_id=1, replica_groups=mesh['dp'=4,'expert'=2,'tensor'=4] {'tensor'}, dimensions={0}, use_global_device_ids=true | all-gather | bytes 983040 | tf_op jit(solution)/shard_map/all_gather | solution.py:639
  614.2 3.0 fusion.51
  618.9 66.5 %all-gather.1 = f32[32,2,1536]{2,1,0:T(2,128)S(1)} all-gather(f32[1,2,1536]{2,1,0:T(2,128)S(1)} %maximum_bitcast_fusion.3), channel_id=2, replica_groups=mesh['dp'=4,'expert'=2,'tensor'=4] {'dp','expert','tensor'}, dimensions={0}, use_global_device_ids=true | all-gather | bytes 405504 | tf_op jit(solution)/shard_map/all_gather | solution.py:695
  687.9 10.8 %all_gather.38 = bf16[256,1536]{1,0:T(8,128)(2,1)S(1)} all-gather(bf16[64,1536]{1,0:T(8,128)(2,1)S(1)} %fusion.28), channel_id=1, replica_groups=mesh['dp'=4,'expert'=2,'tensor'=4] {'tensor'}, dimensions={0}, use_global_device_ids=true | all-gather | bytes 983040 | tf_op jit(solution)/shard_map/all_gather | solution.py:693
  700.1 3.0 fusion.50
  (169 shorter events, 48.2 us)
Async XLA Ops:
  8.0 11.8 %copy-start = (bf16[384,1536]{1,0:T(8,128)(2,1)S(1)}, bf16[384,1536]{1,0:T(8,128)(2,1)}, u32[]{:S(2)}) copy-start(bf16[384,1536]{1,0:T(8,128)(2,1)} %param.26) | copy-start | bytes 3538948
  8.0 2.4 copy-start.31
  8.0 42.3 %reduce-scatter.16.cloned.1.call-start = ((), (), s32[]{:S(2)}) async-start(), calls=%async_computation.12 | async-start | bytes 983040 | tf_op jit(solution)/shard_map/reduce_scatter | solution.py:610
  9.6 2.0 copy-start.7
  17.3 2.5 copy-start.24
  21.3 29.1 %copy-start.1 = (bf16[256,1536]{1,0:T(8,128)(2,1)S(1)}, bf16[256,1536]{1,0:T(8,128)(2,1)}, u32[]{:S(2)}) copy-start(bf16[256,1536]{1,0:T(8,128)(2,1)} %param.21) | copy-start | bytes 2359300
  21.3 31.3 %copy-start.30 = (f32[1536]{0:T(1024)S(1)}, f32[1536]{0:T(1024)}, u32[]{:S(2)}) copy-start(f32[1536]{0:T(1024)} %param.27) | copy-start | bytes 18436
  21.3 33.0 %copy-start.40 = (s32[256,8]{0,1:T(8,128)S(1)}, s32[256,8]{0,1:T(8,128)}, u32[]{:S(2)}) copy-start(s32[256,8]{0,1:T(8,128)} %param.32) | copy-start | bytes 24580
  21.3 70.9 %all-gather.10.cloned.1.call-start = ((), (), s32[]{:S(2)}) async-start(), calls=%async_computation.8 | async-start | bytes 7077888 | tf_op jit(solution)/shard_map/all_gather | solution.py:586
  23.7 139.2 %all-gather.8.cloned.1.call-start = ((), (), s32[]{:S(2)}) async-start(), calls=%async_computation.7 | async-start | bytes 6488064 | tf_op jit(solution)/shard_map/all_gather | solution.py:615
  54.3 312.3 %reduce-scatter.14.cloned.1.call-start = ((), (), s32[]{:S(2)}) async-start(), calls=%async_computation.9 | async-start | bytes 294912 | tf_op jit(solution)/shard_map/reduce_scatter | solution.py:637
  162.9 7.6 %copy-start.33 = (s32[2048,1]{0,1:T(1,128)S(1)}, s32[2048,1]{0,1:T(1,128)}, u32[]{:S(2)}) copy-start(s32[2048,1]{0,1:T(1,128)} %get-tuple-element.111) | copy-start | bytes 24580
  162.9 7.6 %copy-start.34 = (s32[2048,1]{0,1:T(1,128)S(1)}, s32[2048,1]{0,1:T(1,128)}, u32[]{:S(2)}) copy-start(s32[2048,1]{0,1:T(1,128)} %get-tuple-element.112) | copy-start | bytes 24580
  162.9 7.6 %copy-start.35 = (s32[2048,1]{0,1:T(1,128)S(1)}, s32[2048,1]{0,1:T(1,128)}, u32[]{:S(2)}) copy-start(s32[2048,1]{0,1:T(1,128)} %get-tuple-element.113) | copy-start | bytes 24580
  162.9 7.6 %copy-start.36 = (s32[2048,1]{0,1:T(1,128)S(1)}, s32[2048,1]{0,1:T(1,128)}, u32[]{:S(2)}) copy-start(s32[2048,1]{0,1:T(1,128)} %get-tuple-element.114) | copy-start | bytes 24580
  162.9 7.7 %copy-start.37 = (s32[2048,1]{0,1:T(1,128)S(1)}, s32[2048,1]{0,1:T(1,128)}, u32[]{:S(2)}) copy-start(s32[2048,1]{0,1:T(1,128)} %get-tuple-element.115) | copy-start | bytes 24580
  162.9 7.7 %copy-start.38 = (s32[2048,1]{0,1:T(1,128)S(1)}, s32[2048,1]{0,1:T(1,128)}, u32[]{:S(2)}) copy-start(s32[2048,1]{0,1:T(1,128)} %get-tuple-element.116) | copy-start | bytes 24580
  334.0 74.2 %reduce-scatter.20.cloned.1.call-start = ((), (), s32[]{:S(2)}) async-start(), calls=%async_computation.14 | async-start | bytes 1769472 | tf_op jit(solution)/shard_map/reduce_scatter | solution.py:635
  334.8 115.0 %reduce-scatter.18.cloned.1.call-start = ((), (), s32[]{:S(2)}) async-start(), calls=%async_computation.13 | async-start | bytes 1769472 | tf_op jit(solution)/shard_map/reduce_scatter | solution.py:636
  335.4 278.8 %all-gather.14.cloned.1.call-start = ((), (), s32[]{:S(2)}) async-start(), calls=%async_computation.11 | async-start | bytes 1769472 | tf_op jit(solution)/shard_map/all_gather | solution.py:607
  335.9 281.3 %reduce-scatter.22.cloned.1.call-start = ((), (), s32[]{:S(2)}) async-start(), calls=%async_computation.15 | async-start | bytes 983040 | tf_op jit(solution)/shard_map/reduce_scatter | solution.py:688
  467.3 2.6 copy-start.16
  467.3 2.6 copy-start.18
  468.4 1.9 copy-start.27
  473.9 6.6 copy-start.5
  473.9 226.1 %all-gather.12.cloned.1.call-start = ((), (), s32[]{:S(2)}) async-start(), calls=%async_computation.10 | async-start | bytes 2949120 | tf_op jit(solution)/shard_map/all_gather | solution.py:680
  475.8 43.1 %all-to-all-start = ((bf16[8,256,192]{1,2,0:T(8,128)(2,1)}), bf16[8,256,192]{1,2,0:T(8,128)(2,1)S(1)}, u32[]{:S(2)}, u32[]{:S(2)}) async-start(bf16[8,256,192]{1,2,0:T(8,128)(2,1)} %bitcast.46), calls=%async_computation.1 | async-start | bytes 1572864 | tf_op jit(solution)/shard_map/all_to_all | solution.py:591
  518.9 94.2 %all-to-all-start.1 = ((bf16[8,256,192]{1,2,0:T(8,128)(2,1)}), bf16[8,256,192]{1,2,0:T(8,128)(2,1)S(1)}, u32[]{:S(2)}, u32[]{:S(2)}) async-start(bf16[8,256,192]{1,2,0:T(8,128)(2,1)} %bitcast.49), calls=%async_computation.2 | async-start | bytes 1572864 | tf_op jit(solution)/shard_map/all_to_all | solution.py:656
  524.7 77.9 %copy-start.39 = (f32[1536]{0:T(1024)S(1)}, f32[1536]{0:T(1024)}, u32[]{:S(2)}) copy-start(f32[1536]{0:T(1024)} %get-tuple-element.88) | copy-start | bytes 18436
  614.1 3.1 copy-start.32
  614.1 3.1 copy-start.43
  614.1 72.6 %copy-start.6 = (f32[64,1536]{1,0:T(8,128)S(1)}, f32[64,1536]{1,0:T(8,128)}, u32[]{:S(2)}) copy-start(f32[64,1536]{1,0:T(8,128)} %get-tuple-element.95) | copy-start | bytes 1179652
  (23 other events, 26.0 us)
Sparse Core Ops, SparseCore 0:
  21.4 28.8 reduce-scatter.15
  334.2 32.3 reduce-scatter.13
  369.9 38.3 reduce-scatter.19
  411.4 38.3 reduce-scatter.17
  474.1 26.1 reduce-scatter.21
Sparse Core Ops, SparseCore 1:
  24.0 68.2 all-gather.9
  95.5 67.3 all-gather.7
  337.4 25.6 all-gather.13
  476.3 47.8 all-gather.11

commit v2 on v0

--- a/solution.py
+++ b/solution.py
@@ -1,8 +1,11 @@
+import functools
 import math
 
 import jax
 import jax.numpy as jnp
 from jax import lax
+from jax.experimental import pallas as pl
+from jax.experimental.pallas import tpu as pltpu
 from jax.sharding import PartitionSpec as P
 
 HEAD_SIZE = 64
@@ -168,7 +171,7 @@
     return (query_parts, key_gradient, value_gradient)
 
 
-def local(
+def reduce_plan(
     tokens,
     gain_attn,
     w_query,
@@ -383,6 +386,953 @@
     )
 
 
+GATHER_ROWS = 4096
+MESH = pl.DeviceIdType.MESH
+VMEM = pl.BlockSpec(memory_space=pltpu.VMEM)
+ANY = pl.BlockSpec(memory_space=pl.ANY)
+EXTRA = 128
+VMEM_LIMIT = 60 * 2**20
+F32, BF16 = jnp.float32, jnp.bfloat16
+
+
+def dot(a, b):
+    return jnp.dot(a, b, preferred_element_type=F32)
+
+
+def dot_nt(a, b):
+    return lax.dot_general(a, b, (((1,), (1,)), ((), ())), preferred_element_type=F32)
+
+
+def dot_tn(a, b):
+    return lax.dot_general(a, b, (((0,), (0,)), ((), ())), preferred_element_type=F32)
+
+
+def ds(index, size):
+    return pl.ds(pl.multiple_of(index * size, size), size)
+
+
+class Peers:
+    def __init__(self, dp, tp, send_sem, recv_sem):
+        self.z, self.c, self.t = (lax.axis_index(a) for a in ("dp", "expert", "tensor"))
+        self.dp, self.tp = dp, tp
+        self.send_sem, self.recv_sem = send_sem, recv_sem
+        self.used = 0
+        self.open = []
+
+    def tensor(self, k):
+        return (self.z, self.c, lax.rem(self.t + k, self.tp))
+
+    def plane(self, k):
+        return (lax.rem(self.z + k, self.dp), self.c, self.t)
+
+    def partner(self):
+        return (self.z, 1 - self.c, self.t)
+
+    def greet(self):
+        barrier = pltpu.get_barrier_semaphore()
+        everyone = [self.tensor(k) for k in range(1, self.tp)]
+        everyone += [self.plane(k) for k in range(1, self.dp)] + [self.partner()]
+        for peer in everyone:
+            pl.semaphore_signal(barrier, inc=1, device_id=peer, device_id_type=MESH)
+        pl.semaphore_wait(barrier, len(everyone))
+
+    def number(self, count):
+        first = self.used
+        self.used += count
+        return first
+
+    def make(self, src, dst, number, device):
+        return pltpu.make_async_remote_copy(
+            src_ref=src,
+            dst_ref=dst,
+            send_sem=self.send_sem.at[number],
+            recv_sem=self.recv_sem.at[number],
+            device_id=device,
+            device_id_type=MESH,
+        )
+
+    def to(self, src, dst, device):
+        copy = self.make(src, dst, self.number(1), device)
+        copy.start()
+        self.open.append(copy)
+        return copy
+
+    def keep(self, src, dst, sem):
+        copy = pltpu.make_async_copy(src, dst, sem)
+        copy.start()
+        return copy
+
+    def drain(self):
+        for copy in self.open:
+            copy.wait_send()
+
+
+def arrived(copies):
+    for copy in copies:
+        copy.wait_recv()
+
+
+def rotate(u, rope_ref, sign):
+    width = u.shape[1]
+    tiles = []
+    for at in range(0, width, 128):
+        v = u[:, at : at + 128]
+        side = pltpu.roll(v, 96, 1) * rope_ref[1] + pltpu.roll(v, 32, 1) * rope_ref[2]
+        tiles.append(v * rope_ref[0] + sign * side)
+    return tiles[0] if len(tiles) == 1 else jnp.concatenate(tiles, axis=1)
+
+
+def inverse_rms(u):
+    return lax.rsqrt(jnp.mean(u * u, axis=-1, keepdims=True) + EPSILON)
+
+
+def causal(length):
+    row = lax.broadcasted_iota(jnp.int32, (length, length), 0)
+    col = lax.broadcasted_iota(jnp.int32, (length, length), 1)
+    return col <= row
+
+
+def forward_kernel(
+    dp,
+    tp,
+    tok_ref,
+    cot_ref,
+    routes_ref,
+    ga_ref,
+    gm_ref,
+    wq_ref,
+    wk_ref,
+    wv_ref,
+    wo_ref,
+    rope_ref,
+    x_ref,
+    g_ref,
+    gz_ref,
+    h1_ref,
+    n1_ref,
+    qkv_ref,
+    att_ref,
+    lse_ref,
+    part_buf,
+    rs_buf,
+    send_sem,
+    recv_sem,
+):
+    net = Peers(dp, tp, send_sem, recv_sem)
+    z, c, t = net.z, net.c, net.t
+    length, model = tok_ref.shape
+    own = length // tp
+    q_width, kv_width = wq_ref.shape[1], wk_ref.shape[1]
+    group = q_width // kv_width
+    net.greet()
+    seq_rows = ds(c, length)
+    got_g = [net.to(cot_ref, g_ref.at[seq_rows], net.partner())]
+    for k in range(1, dp):
+        got_g.append(net.to(cot_ref.at[ds(t, own)], gz_ref.at[dp - 1 - k], net.plane(k)))
+    g_ref[seq_rows, :] = cot_ref[...]
+
+    resid = tok_ref[...].astype(F32)
+    n1 = (resid * inverse_rms(resid) * ga_ref[...]).astype(BF16)
+    n1_ref[...] = n1
+    qkv_ref[:, :q_width] = rotate(dot(n1, wq_ref[...]), rope_ref, 1.0).astype(BF16)
+    qkv_ref[:, q_width : q_width + kv_width] = rotate(dot(n1, wk_ref[...]), rope_ref, 1.0).astype(BF16)
+    qkv_ref[:, q_width + kv_width :] = dot(n1, wv_ref[...]).astype(BF16)
+
+    seen = causal(length)
+    lane = lax.broadcasted_iota(jnp.int32, lse_ref.shape, 1)
+    lse_all = jnp.zeros(lse_ref.shape, F32)
+    scale = HEAD_SIZE ** (-0.5)
+    for h in range(q_width // HEAD_SIZE):
+        kv = h // group
+        at_k = q_width + kv * HEAD_SIZE
+        at_v = q_width + kv_width + kv * HEAD_SIZE
+        q = qkv_ref[:, h * HEAD_SIZE : (h + 1) * HEAD_SIZE]
+        key = qkv_ref[:, at_k : at_k + HEAD_SIZE]
+        val = qkv_ref[:, at_v : at_v + HEAD_SIZE]
+        s = jnp.where(seen, dot_nt(q, key) * scale, -1e30)
+        top = jnp.max(s, axis=-1, keepdims=True)
+        lse = top + jnp.log(jnp.sum(jnp.exp(s - top), axis=-1, keepdims=True))
+        prob = jnp.exp(s - lse).astype(BF16)
+        att_ref[:, h * HEAD_SIZE : (h + 1) * HEAD_SIZE] = dot(prob, val).astype(BF16)
+        lse_all = jnp.where(lane == h, lse, lse_all)
+    lse_ref[...] = lse_all
+    part_buf[...] = dot(att_ref[...], wo_ref[...]).astype(BF16)
+
+    got = []
+    for k in range(1, tp):
+        block = part_buf.at[ds(lax.rem(t + k, tp), own)]
+        got.append(net.to(block, rs_buf.at[k - 1], net.tensor(k)))
+    total = tok_ref[ds(t, own), :].astype(F32) + part_buf[ds(t, own), :].astype(F32)
+    picked = routes_ref[ds(t, own), :]
+    ids = lax.broadcasted_iota(jnp.int32, (own, EXTRA), 1)
+    chosen = picked[:, 0:1] == ids
+    for j in range(1, picked.shape[1]):
+        chosen = chosen | (picked[:, j : j + 1] == ids)
+    arrived(got)
+    for k in range(1, tp):
+        total = total + rs_buf[k - 1].astype(F32)
+    h1_ref[...] = total
+    n2 = (total * inverse_rms(total) * gm_ref[...]).astype(BF16)
+    mine = ds(c * tp + t, own)
+    x_ref[mine, :model] = n2
+    x_ref[mine, model:] = jnp.where(chosen, 1.0, 0.0).astype(BF16)
+    got = [net.to(x_ref.at[mine], x_ref.at[mine], net.tensor(k)) for k in range(1, tp)]
+    arrived(got)
+    got = [net.to(x_ref.at[seq_rows], x_ref.at[seq_rows], net.partner())]
+    arrived(got_g + got)
+    net.drain()
+
+
+def forward(dp, tp, tokens, cotangent, routes, ga, gm, wq, wk, wv, wo, rope):
+    length, model = tokens.shape
+    own, wide = length // tp, model + EXTRA
+    widths = wq.shape[1] + wk.shape[1] + wv.shape[1]
+    copies = 2 + (dp - 1) + 2 * (tp - 1)
+    shapes = [
+        ((2 * length, wide), BF16),
+        ((2 * length, model), BF16),
+        ((dp - 1, own, model), BF16),
+        ((own, model), F32),
+        ((length, model), BF16),
+        ((length, widths), BF16),
+        ((length, wq.shape[1]), BF16),
+        ((length, 128), F32),
+    ]
+    return pl.pallas_call(
+        functools.partial(forward_kernel, dp, tp),
+        out_shape=[jax.ShapeDtypeStruct(*s) for s in shapes],
+        in_specs=[VMEM] * 10,
+        out_specs=[VMEM] * len(shapes),
+        scratch_shapes=[
+            pltpu.VMEM((length, model), BF16),
+            pltpu.VMEM((tp - 1, own, model), BF16),
+            pltpu.SemaphoreType.DMA((copies,)),
+            pltpu.SemaphoreType.DMA((copies,)),
+        ],
+        compiler_params=pltpu.CompilerParams(
+            collective_id=0, has_side_effects=True, vmem_limit_bytes=VMEM_LIMIT
+        ),
+        name="forward",
+    )(tokens, cotangent, routes, ga, gm, wq, wk, wv, wo, rope)
+
+
+def gates_of(x_ref, wr_ref, model):
+    logits = dot(x_ref[:, :model], wr_ref[...])
+    chosen = x_ref[:, model:].astype(F32) > 0.5
+    top = jnp.max(jnp.where(chosen, logits, -jnp.inf), axis=1, keepdims=True)
+    weight = jnp.where(chosen, jnp.exp(jnp.where(chosen, logits - top, 0.0)), 0.0)
+    return weight / jnp.sum(weight, axis=1, keepdims=True)
+
+
+def store_split(gates, split_ref):
+    high = gates.astype(BF16)
+    split_ref[:, :EXTRA] = high
+    split_ref[:, EXTRA:] = (gates - high.astype(F32)).astype(BF16)
+
+
+def pair_of_gates(split, first, width):
+    k_pos = lax.broadcasted_iota(jnp.int32, (2 * EXTRA, 2 * width), 0)
+    l_pos = lax.broadcasted_iota(jnp.int32, (2 * EXTRA, 2 * width), 1)
+    pick = jnp.where(k_pos % EXTRA == first + l_pos // width, 1.0, 0.0).astype(BF16)
+    return dot(split, pick)
+
+
+def swiglu(both, dh, gate):
+    width = dh.shape[1]
+    gate_pre, up_pre = both[:, :width], both[:, width:]
+    sig = jax.nn.sigmoid(gate_pre)
+    act = gate_pre * sig
+    hid = act * up_pre
+    d_hid = dh * gate
+    d_gate = d_hid * up_pre * sig * (1.0 + gate_pre * (1.0 - sig))
+    return hid, (hid * gate).astype(BF16), d_gate.astype(BF16), (d_hid * act).astype(BF16)
+
+
+def plane_kernel(
+    dp,
+    tp,
+    x_ref,
+    g_ref,
+    gz_ref,
+    n1_ref,
+    wr_ref,
+    wg_ref,
+    wu_ref,
+    wd_ref,
+    xr_ref,
+    gr_ref,
+    n1c_ref,
+    moe_ref,
+    back_ref,
+    dgate_ref,
+    gates_ref,
+    ghid_ref,
+    dgp_ref,
+    dup_ref,
+    split,
+    moe_acc,
+    back_acc,
+    send_sem,
+    recv_sem,
+    keep_sem,
+):
+    step, last = pl.program_id(0), pl.num_programs(0) - 1
+    net = Peers(dp, tp, send_sem, recv_sem)
+    z, c, t = net.z, net.c, net.t
+    rows, model = g_ref.shape
+    length = rows // 2
+    own = length // tp
+    width = wg_ref.shape[2]
+    part = model // dp
+    others = range(1, dp)
+    sides = range(1, tp)
+
+    def block(plane, core, tensor):
+        return ds((plane * 2 + core) * tp + tensor, own)
+
+    def columns(index):
+        return pl.ds(pl.multiple_of(index * part, 128), part)
+
+    mine = ds(c * tp + t, own)
+    x_z = [
+        net.make(x_ref.at[mine], xr_ref.at[block(dp - k, c, t)], net.number(1), net.plane(k))
+        for k in others
+    ]
+    n1_z = [
+        net.make(
+            n1_ref.at[:, columns(lax.rem(z + k, dp))],
+            n1c_ref.at[ds((dp - k) * 2 + c, length)],
+            net.number(1),
+            net.plane(k),
+        )
+        for k in others
+    ]
+    n1_own = net.make(
+        n1_ref.at[:, columns(z)], n1c_ref.at[ds(c, length)], net.number(1), net.partner()
+    )
+    g_t = [
+        net.make(gz_ref.at[p - 1], gr_ref.at[block(p, c, t)], net.number(1), net.tensor(k))
+        for p in others
+        for k in sides
+    ]
+    x_t = [
+        net.make(
+            xr_ref.at[block(p, c, t)], xr_ref.at[block(p, c, t)], net.number(1), net.tensor(k)
+        )
+        for p in others
+        for k in sides
+    ]
+
+    def over(ref):
+        return [
+            net.make(
+                ref.at[ds(p * 2 + c, length)],
+                ref.at[ds(p * 2 + c, length)],
+                net.number(1),
+                net.partner(),
+            )
+            for p in others
+        ]
+
+    g_c, x_c, n1_c = over(gr_ref), over(xr_ref), over(n1c_ref)
+    kept = [
+        pltpu.make_async_copy(x_ref, xr_ref.at[pl.ds(0, rows)], keep_sem.at[0]),
+        pltpu.make_async_copy(g_ref, gr_ref.at[pl.ds(0, rows)], keep_sem.at[1]),
+        pltpu.make_async_copy(
+            n1_ref.at[:, columns(z)], n1c_ref.at[ds(c, length)], keep_sem.at[2]
+        ),
+    ] + [
+        pltpu.make_async_copy(gz_ref.at[p - 1], gr_ref.at[block(p, c, t)], keep_sem.at[2 + p])
+        for p in others
+    ]
+
+    def start(copies):
+        for copy in copies:
+            copy.start()
+
+    @pl.when(step == 0)
+    def _():
+        net.greet()
+        start(x_z + g_t + n1_z + [n1_own])
+        start(kept)
+        moe_acc[...] = jnp.zeros_like(moe_acc)
+        back_acc[...] = jnp.zeros_like(back_acc)
+        dgate_ref[...] = jnp.zeros_like(dgate_ref)
+        gates = gates_of(x_ref, wr_ref, model)
+        gates_ref[...] = gates
+        store_split(gates, split)
+
+    @pl.when(step == 4)
+    def _():
+        arrived(x_z)
+        start(x_t)
+
+    @pl.when(step == 6)
+    def _():
+        arrived(g_t)
+        for copy in kept:
+            copy.wait()
+        start(g_c)
+
+    @pl.when(step == 8)
+    def _():
+        arrived(n1_z)
+        start(n1_c)
+
+    first = c * (2 * pl.num_programs(0)) + 2 * step
+    gate_pair = pair_of_gates(split[...], first, width)
+    wd_pair = wd_ref[...].reshape(2 * width, model)
+    dh_pair = dot_nt(g_ref[...], wd_pair)
+    lane = lax.broadcasted_iota(jnp.int32, dgate_ref.shape, 1)
+    for k in range(2):
+        lanes = slice(k * width, (k + 1) * width)
+        w_both = jnp.concatenate([wg_ref[k], wu_ref[k]], axis=1)
+        both = dot(x_ref[:, :model], w_both)
+        dh = dh_pair[:, lanes]
+        hid, ghid, dgp, dup = swiglu(both, dh, gate_pair[:, lanes])
+        ghid_ref[:, lanes] = ghid
+        dgp_ref[:, lanes] = dgp
+        dup_ref[:, lanes] = dup
+        row_sum = jnp.sum(hid * dh, axis=1, keepdims=True)
+        dgate_ref[...] += jnp.where(lane == first + k, row_sum, 0.0)
+        back_acc[...] += dot_nt(jnp.concatenate([dgp, dup], axis=1), w_both)
+    moe_acc[...] += dot(ghid_ref[...], wd_pair)
+
+    @pl.when(step == last)
+    def _():
+        moe_ref[...] = moe_acc[...].astype(BF16)
+        back_ref[...] = back_acc[...].astype(BF16)
+        arrived(x_t)
+        start(x_c)
+        arrived(g_c + n1_c + [n1_own])
+        arrived(x_c)
+        for copy in x_z + g_t + n1_z + [n1_own] + x_t + g_c + n1_c + x_c:
+            copy.wait_send()
+
+
+def plane_experts(dp, tp, x, g, gz, n1, wr, w_gate, w_up, w_down):
+    rows, model = g.shape
+    length = rows // 2
+    count, _, width = w_gate.shape
+    all_rows = rows * dp
+    others, sides = dp - 1, tp - 1
+    copies = 2 * others + 1 + 2 * others * sides + 3 * others
+
+    def whole(a):
+        shape = a.shape
+        return pl.BlockSpec(shape, lambda i: (0,) * len(shape), pipeline_mode=pl.Buffered(1))
+
+    by_pair = lambda shape: pl.BlockSpec((2,) + shape, lambda i: (i, 0, 0))
+    saved = pl.BlockSpec((rows, 2 * width), lambda i: (0, i))
+    shapes = [
+        ((all_rows, x.shape[1]), BF16),
+        ((all_rows, model), BF16),
+        ((all_rows, model // dp), BF16),
+        ((rows, model), BF16),
+        ((rows, model), BF16),
+        ((rows, EXTRA), F32),
+        ((rows, EXTRA), F32),
+        ((rows, count * width), BF16),
+        ((rows, count * width), BF16),
+        ((rows, count * width), BF16),
+    ]
+    shapes = [jax.ShapeDtypeStruct(*s) for s in shapes]
+    return pl.pallas_call(
+        functools.partial(plane_kernel, dp, tp),
+        grid=(count // 2,),
+        out_shape=shapes,
+        in_specs=[whole(x), whole(g), whole(gz), whole(n1), whole(wr)]
+        + [by_pair((model, width)), by_pair((model, width)), by_pair((width, model))],
+        out_specs=[ANY, ANY, ANY] + [whole(s) for s in shapes[3:7]] + [saved] * 3,
+        scratch_shapes=[
+            pltpu.VMEM((rows, 2 * EXTRA), BF16),
+            pltpu.VMEM((rows, model), F32),
+            pltpu.VMEM((rows, model), F32),
+            pltpu.SemaphoreType.DMA((copies,)),
+            pltpu.SemaphoreType.DMA((copies,)),
+            pltpu.SemaphoreType.DMA((3 + others,)),
+        ],
+        compiler_params=pltpu.CompilerParams(
+            collective_id=1, has_side_effects=True, vmem_limit_bytes=VMEM_LIMIT
+        ),
+        name="plane_experts",
+    )(x, g, gz, n1, wr, w_gate, w_up, w_down)
+
+
+def backward_kernel(
+    dp,
+    tp,
+    back_ref,
+    moe_ref,
+    dgate_ref,
+    gates_ref,
+    h1_ref,
+    tok_ref,
+    cot_ref,
+    ga_ref,
+    gm_ref,
+    wr_ref,
+    wq_ref,
+    wk_ref,
+    wv_ref,
+    wo_ref,
+    qkv_ref,
+    att_ref,
+    lse_ref,
+    rope_ref,
+    out_ref,
+    in_ref,
+    att_all,
+    da_cols,
+    d_all,
+    gains_ref,
+    pair_b,
+    pair_m,
+    pair_d,
+    sum_b,
+    sum_m,
+    sum_d,
+    rs_b,
+    rs_m,
+    rs_d,
+    da_buf,
+    dl_buf,
+    d_buf,
+    do_buf,
+    part_buf,
+    rs_3,
+    gain_buf,
+    gain_t,
+    gain_z,
+    gain_zs,
+    gain_c,
+    send_sem,
+    recv_sem,
+    keep_sem,
+):
+    net = Peers(dp, tp, send_sem, recv_sem)
+    z, c, t = net.z, net.c, net.t
+    length, model = tok_ref.shape
+    own = length // tp
+    part = model // dp
+    q_width, kv_width = wq_ref.shape[1], wk_ref.shape[1]
+    group = q_width // kv_width
+    others, sides = range(1, dp), range(1, tp)
+    mine = ds(t, own)
+    here, there = ds(c, length), ds(1 - c, length)
+
+    def columns(index):
+        return pl.ds(pl.multiple_of(index * part, 128), part)
+
+    def to_sides(ref, into):
+        return [
+            net.to(ref.at[ds(lax.rem(t + k, tp), own)], into.at[k - 1], net.tensor(k))
+            for k in sides
+        ]
+
+    def share(ref):
+        return [net.to(ref.at[mine], ref.at[mine], net.tensor(k)) for k in sides]
+
+    def on_to_partner(ref):
+        rows = [ds(p * 2 + c, length) for p in others]
+        return [net.to(ref.at[r], ref.at[r], net.partner()) for r in rows]
+
+    net.greet()
+    got_b = [
+        net.to(back_ref.at[there], pair_b, net.partner()),
+        net.to(dgate_ref.at[there], pair_d, net.partner()),
+    ]
+    got_m = [net.to(moe_ref.at[there], pair_m, net.partner())]
+    att_z = [net.to(att_ref, att_all.at[ds((dp - k) * 2 + c, length)], net.plane(k)) for k in others]
+    att_own = net.to(att_ref, att_all.at[here], net.partner())
+    kept = [net.keep(att_ref, att_all.at[here], keep_sem.at[0])]
+    arrived(got_b)
+    sum_b[...] = (back_ref[here, :].astype(F32) + pair_b[...].astype(F32)).astype(BF16)
+    sum_d[...] = dgate_ref[here, :] + pair_d[...]
+    got_b = to_sides(sum_b, rs_b) + to_sides(sum_d, rs_d)
+    arrived(got_m)
+    sum_m[...] = (moe_ref[here, :].astype(F32) + pair_m[...].astype(F32)).astype(BF16)
+    arrived(got_b)
+    d_n2 = sum_b[mine, :].astype(F32)
+    dgate = sum_d[mine, :]
+    for k in sides:
+        d_n2 = d_n2 + rs_b[k - 1].astype(F32)
+        dgate = dgate + rs_d[k - 1]
+    gates = gates_ref[ds(c * tp + t, own), :]
+    d_logits = gates * (dgate - jnp.sum(gates * dgate, axis=1, keepdims=True))
+    dl_buf[mine, :] = d_logits.astype(BF16)
+    d_n2 = d_n2 + dot_nt(d_logits.astype(BF16), wr_ref[...])
+    h1 = h1_ref[...]
+    r2 = inverse_rms(h1)
+    weighted = d_n2 * gm_ref[...]
+    inner = jnp.mean(weighted * h1, axis=-1, keepdims=True)
+    gain_buf[...] = jnp.zeros_like(gain_buf)
+    gain_buf[1:2, :] = jnp.sum(d_n2 * h1 * r2, axis=0, keepdims=True)
+    d_h1 = cot_ref[mine, :].astype(F32) + (r2 * weighted - h1 * (r2 * r2 * r2) * inner)
+    da_buf[mine, :] = d_h1.astype(BF16)
+    got_da = share(da_buf) + share(dl_buf)
+    got_m = to_sides(sum_m, rs_m)
+    arrived(att_z)
+    att_c = on_to_partner(att_all)
+    arrived(got_da)
+    d_buf[:, q_width + 2 * kv_width :] = dl_buf[...]
+    da_z = [
+        net.to(
+            da_buf.at[:, columns(lax.rem(z + k, dp))],
+            da_cols.at[ds((dp - k) * 2 + c, length)],
+            net.plane(k),
+        )
+        for k in others
+    ]
+    da_own = net.to(da_buf.at[:, columns(z)], da_cols.at[here], net.partner())
+    kept.append(net.keep(da_buf.at[:, columns(z)], da_cols.at[here], keep_sem.at[1]))
+    do_buf[...] = dot_nt(da_buf[...], wo_ref[...]).astype(BF16)
+
+    arrived(got_m)
+    total = h1 + sum_m[mine, :].astype(F32)
+    for k in sides:
+        total = total + rs_m[k - 1].astype(F32)
+    out_ref[mine, :] = total.astype(BF16)
+    got_out = share(out_ref)
+
+    seen = causal(length)
+    scale = HEAD_SIZE ** (-0.5)
+    d_key, d_val, d_query = [], [], []
+    for kv in range(kv_width // HEAD_SIZE):
+        at_k = q_width + kv * HEAD_SIZE
+        at_v = q_width + kv_width + kv * HEAD_SIZE
+        key = qkv_ref[:, at_k : at_k + HEAD_SIZE]
+        val = qkv_ref[:, at_v : at_v + HEAD_SIZE]
+        dk = jnp.zeros((length, HEAD_SIZE), F32)
+        dv = jnp.zeros((length, HEAD_SIZE), F32)
+        for h in range(kv * group, (kv + 1) * group):
+            at = slice(h * HEAD_SIZE, (h + 1) * HEAD_SIZE)
+            q = qkv_ref[:, at]
+            d_out = do_buf[:, at]
+            s = jnp.where(seen, dot_nt(q, key) * scale, -1e30)
+            prob = jnp.exp(s - lse_ref[:, h : h + 1])
+            delta = jnp.sum(d_out.astype(F32) * att_ref[:, at].astype(F32), axis=-1, keepdims=True)
+            d_s = (prob * (dot_nt(d_out, val) - delta)).astype(BF16)
+            d_query.append(dot(d_s, key) * scale)
+            dk = dk + dot_tn(d_s, q)
+            dv = dv + dot_tn(prob.astype(BF16), d_out)
+        d_key.append(dk * scale)
+        d_val.append(dv)
+    d_buf[:, :q_width] = rotate(jnp.concatenate(d_query, axis=1), rope_ref, -1.0).astype(BF16)
+    d_buf[:, q_width : q_width + kv_width] = rotate(
+        jnp.concatenate(d_key, axis=1), rope_ref, -1.0
+    ).astype(BF16)
+    d_buf[:, q_width + kv_width : q_width + 2 * kv_width] = jnp.concatenate(d_val, axis=1).astype(BF16)
+    d_z = [net.to(d_buf, d_all.at[ds((dp - k) * 2 + c, length)], net.plane(k)) for k in others]
+    d_own = net.to(d_buf, d_all.at[here], net.partner())
+    kept.append(net.keep(d_buf, d_all.at[here], keep_sem.at[2]))
+    part_n1 = dot_nt(d_buf[:, :q_width], wq_ref[...])
+    part_n1 = part_n1 + dot_nt(d_buf[:, q_width : q_width + kv_width], wk_ref[...])
+    part_n1 = part_n1 + dot_nt(
+        d_buf[:, q_width + kv_width : q_width + 2 * kv_width], wv_ref[...]
+    )
+    part_buf[...] = part_n1.astype(BF16)
+    got_3 = to_sides(part_buf, rs_3)
+    arrived(da_z)
+    da_c = on_to_partner(da_cols)
+    arrived(got_3)
+    d_n1 = part_buf[mine, :].astype(F32)
+    for k in sides:
+        d_n1 = d_n1 + rs_3[k - 1].astype(F32)
+    resid = tok_ref[mine, :].astype(F32)
+    r1 = inverse_rms(resid)
+    weighted = d_n1 * ga_ref[...]
+    inner = jnp.mean(weighted * resid, axis=-1, keepdims=True)
+    gain_buf[0:1, :] = jnp.sum(d_n1 * resid * r1, axis=0, keepdims=True)
+    d_x = d_h1 + (r1 * weighted - resid * (r1 * r1 * r1) * inner)
+    in_ref[mine, :] = d_x.astype(BF16)
+    got_gain = [net.to(gain_buf, gain_t.at[k - 1], net.tensor(k)) for k in sides]
+    got_in = share(in_ref)
+    arrived(got_gain)
+    gain = gain_buf[...]
+    for k in sides:
+        gain = gain + gain_t[k - 1]
+    gain_zs[...] = gain
+    got_gain = [
+        net.to(gain_zs.at[:, columns(lax.rem(z + k, dp))], gain_z.at[k - 1], net.plane(k))
+        for k in others
+    ]
+    arrived(got_gain)
+    gain = gain_zs[:, columns(z)]
+    for k in others:
+        gain = gain + gain_z[k - 1]
+    gain_c[0] = gain
+    got_gain = net.to(gain_c.at[0], gain_c.at[1], net.partner())
+    arrived(d_z)
+    d_c = on_to_partner(d_all)
+    arrived([got_gain])
+    gains_ref[...] = gain + gain_c[1]
+    arrived(got_out + got_in + [att_own, da_own, d_own] + att_c + da_c + d_c)
+    for copy in kept:
+        copy.wait()
+    net.drain()
+
+
+def backward(dp, tp, *arrays):
+    back, _, _, _, _, tokens, _, _, _, _, wq, wk, wv = arrays[:13]
+    rows, model = back.shape
+    length = tokens.shape[0]
+    own, part = length // tp, model // dp
+    q_width = wq.shape[1]
+    wide = q_width + wk.shape[1] + wv.shape[1] + EXTRA
+    others, sides = dp - 1, tp - 1
+    copies = 3 + 3 * (2 * others + 1) + 2 * sides + 2 * sides + 4 * sides + sides + others + 1
+    shapes = [
+        ((length, model), BF16),
+        ((length, model), BF16),
+        ((rows * dp, q_width), BF16),
+        ((rows * dp, part), BF16),
+        ((rows * dp, wide), BF16),
+        ((8, part), F32),
+    ]
+    return pl.pallas_call(
+        functools.partial(backward_kernel, dp, tp),
+        out_shape=[jax.ShapeDtypeStruct(*s) for s in shapes],
+        in_specs=[VMEM] * len(arrays),
+        out_specs=[VMEM, VMEM, ANY, ANY, ANY, VMEM],
+        scratch_shapes=[
+            pltpu.VMEM((length, model), BF16),
+            pltpu.VMEM((length, model), BF16),
+            pltpu.VMEM((length, EXTRA), F32),
+            pltpu.VMEM((length, model), BF16),
+            pltpu.VMEM((length, model), BF16),
+            pltpu.VMEM((length, EXTRA), F32),
+            pltpu.VMEM((sides, own, model), BF16),
+            pltpu.VMEM((sides, own, model), BF16),
+            pltpu.VMEM((sides, own, EXTRA), F32),
+            pltpu.VMEM((length, model), BF16),
+            pltpu.VMEM((length, EXTRA), BF16),
+            pltpu.VMEM((length, wide), BF16),
+            pltpu.VMEM((length, q_width), BF16),
+            pltpu.VMEM((length, model), BF16),
+            pltpu.VMEM((sides, own, model), BF16),
+            pltpu.VMEM((8, model), F32),
+            pltpu.VMEM((sides, 8, model), F32),
+            pltpu.VMEM((others, 8, part), F32),
+            pltpu.VMEM((8, model), F32),
+            pltpu.VMEM((2, 8, part), F32),
+            pltpu.SemaphoreType.DMA((copies,)),
+            pltpu.SemaphoreType.DMA((copies,)),
+            pltpu.SemaphoreType.DMA((3,)),
+        ],
+        compiler_params=pltpu.CompilerParams(
+            collective_id=2, has_side_effects=True, vmem_limit_bytes=VMEM_LIMIT
+        ),
+        name="backward",
+    )(*arrays)
+
+
+def weights_kernel(
+    place_ref,
+    x_ref,
+    g_ref,
+    wr_ref,
+    att_ref,
+    da_ref,
+    n1_ref,
+    d_ref,
+    ghid_ref,
+    dgp_ref,
+    dup_ref,
+    wg_ref,
+    wu_ref,
+    wd_ref,
+    gate_grad_ref,
+    up_grad_ref,
+    down_grad_ref,
+    query_ref,
+    key_ref,
+    value_ref,
+    out_grad_ref,
+    router_ref,
+    split,
+    xt_buf,
+    gt_buf,
+    hid_buf,
+    dgate_buf,
+    dup_buf,
+    side_buf,
+):
+    step = pl.program_id(0)
+    z, c = place_ref[0], place_ref[1]
+    rows, model = g_ref.shape
+    width = wg_ref.shape[2]
+    part = xt_buf.shape[0]
+    plane_rows = ghid_ref.shape[0]
+    rest = slice(plane_rows, rows)
+
+    @pl.when(step == 0)
+    def _():
+        store_split(gates_of(x_ref, wr_ref, model), split)
+        cols = pl.ds(pl.multiple_of(z * part, 128), part)
+        xt_buf[...] = x_ref[:, cols].T
+        gt_buf[...] = g_ref[:, cols].T
+        q_width, kv_width = query_ref.shape[1], key_ref.shape[1]
+        half = query_ref.shape[0]
+        at = pl.ds(pl.multiple_of(c * half, 8), half)
+        side_buf[:, : d_ref.shape[1] - EXTRA] = dot_tn(n1_ref[...], d_ref[:, : d_ref.shape[1] - EXTRA])
+        side_buf[:, d_ref.shape[1] - EXTRA :] = dot(xt_buf[...], d_ref[:, d_ref.shape[1] - EXTRA :])
+        query_ref[...] = side_buf[at, :q_width]
+        key_ref[...] = side_buf[at, q_width : q_width + kv_width]
+        value_ref[...] = side_buf[at, q_width + kv_width : q_width + 2 * kv_width]
+        router_ref[...] = side_buf[at, d_ref.shape[1] - EXTRA :][:, : router_ref.shape[1]]
+        out_all = dot_tn(att_ref[...], da_ref[...])
+        out_grad_ref[...] = jnp.where(c == 0, out_all[:, :half], out_all[:, half:])
+
+    first = c * (2 * pl.num_programs(0)) + 2 * step
+    wd_pair = wd_ref[...].reshape(2 * width, model)
+    gate_pair = pair_of_gates(split[rest, :], first, width)
+    dh_pair = dot_nt(g_ref[rest, :], wd_pair)
+    hid_buf[:plane_rows, :] = ghid_ref[...]
+    dgate_buf[:plane_rows, :] = dgp_ref[...]
+    dup_buf[:plane_rows, :] = dup_ref[...]
+    for k in range(2):
+        lanes = slice(k * width, (k + 1) * width)
+        both = dot(x_ref[rest, :model], jnp.concatenate([wg_ref[k], wu_ref[k]], axis=1))
+        _, ghid, dgp, dup = swiglu(both, dh_pair[:, lanes], gate_pair[:, lanes])
+        hid_buf[rest, lanes] = ghid
+        dgate_buf[rest, lanes] = dgp
+        dup_buf[rest, lanes] = dup
+    gate_both = dot(xt_buf[...], dgate_buf[...])
+    up_both = dot(xt_buf[...], dup_buf[...])
+    down_both = dot(gt_buf[...], hid_buf[...]).T
+    for k in range(2):
+        lanes = slice(k * width, (k + 1) * width)
+        gate_grad_ref[k] = gate_both[:, lanes]
+        up_grad_ref[k] = up_both[:, lanes]
+        down_grad_ref[k] = down_both[lanes, :]
+
+
+def weight_grads(place, x, g, wr, att, da, n1, d, ghid, dgp, dup, w_gate, w_up, w_down, kv_width, experts):
+    rows, model = g.shape
+    count, _, width = w_gate.shape
+    part = n1.shape[1]
+    q_width, half = att.shape[1], part // 2
+
+    def whole(a):
+        shape = a.shape
+        return pl.BlockSpec(shape, lambda i, p: (0,) * len(shape), pipeline_mode=pl.Buffered(1))
+
+    by_pair = lambda shape: pl.BlockSpec((2,) + shape, lambda i, p: (i, 0, 0))
+    saved = pl.BlockSpec((ghid.shape[0], 2 * width), lambda i, p: (0, i))
+    shapes = [
+        (count, part, width),
+        (count, part, width),
+        (count, width, part),
+        (half, q_width),
+        (half, kv_width),
+        (half, kv_width),
+        (q_width, half),
+        (half, experts),
+    ]
+    shapes = [jax.ShapeDtypeStruct(s, F32) for s in shapes]
+    return pl.pallas_call(
+        weights_kernel,
+        grid_spec=pltpu.PrefetchScalarGridSpec(
+            num_scalar_prefetch=1,
+            grid=(count // 2,),
+            in_specs=[whole(a) for a in (x, g, wr, att, da, n1, d)]
+            + [saved] * 3
+            + [by_pair((model, width)), by_pair((model, width)), by_pair((width, model))],
+            out_specs=[by_pair((part, width)), by_pair((part, width)), by_pair((width, part))]
+            + [whole(s) for s in shapes[3:]],
+            scratch_shapes=[
+                pltpu.VMEM((rows, 2 * EXTRA), BF16),
+                pltpu.VMEM((part, rows), BF16),
+                pltpu.VMEM((part, rows), BF16),
+                pltpu.VMEM((rows, 2 * width), BF16),
+                pltpu.VMEM((rows, 2 * width), BF16),
+                pltpu.VMEM((rows, 2 * width), BF16),
+                pltpu.VMEM((part, d.shape[1]), F32),
+            ],
+        ),
+        out_shape=shapes,
+        compiler_params=pltpu.CompilerParams(vmem_limit_bytes=VMEM_LIMIT),
+        name="weight_grads",
+    )(place, x, g, wr, att, da, n1, d, ghid, dgp, dup, w_gate, w_up, w_down)
+
+
+def rope_rows(length):
+    positions = jnp.arange(length, dtype=F32)
+    cos, sin = rope_tables(positions, HEAD_SIZE)
+    none = jnp.zeros_like(sin)
+    double = lambda first, second: jnp.concatenate([first, second, first, second], axis=1)
+    return jnp.stack([double(cos, cos), double(-sin, none), double(none, sin)])
+
+
+def gather_plan(
+    tokens,
+    gain_attn,
+    w_query,
+    key_projection,
+    value_projection,
+    w_out,
+    gain_moe,
+    w_router,
+    w_gate,
+    w_up,
+    w_down,
+    routes,
+    cotangent,
+):
+    dp, tp = lax.axis_size("dp"), lax.axis_size("tensor")
+    experts = w_router.shape[1]
+    half = tokens.shape[1] // dp // 2
+    rope = rope_rows(tokens.shape[0])
+    ga, gm = gain_attn[None, :], gain_moe[None, :]
+    wr = jnp.pad(w_router, ((0, 0), (0, EXTRA - experts)))
+    heads = (w_query, key_projection, value_projection, w_out)
+    x, g, gz, h1, n1, qkv, att, lse = forward(
+        dp, tp, tokens, cotangent, routes, ga, gm, *heads, rope
+    )
+    x_all, g_all, n1_cols, moe, back, dgate, gates, ghid, dgp, dup = plane_experts(
+        dp, tp, x, g, gz, n1, wr, w_gate, w_up, w_down
+    )
+    output, input_grad, att_all, da_cols, d_all, gains = backward(
+        dp, tp, back, moe, dgate, gates, h1, tokens, cotangent, ga, gm, wr, *heads, qkv, att, lse, rope
+    )
+    z, core = lax.axis_index("dp"), lax.axis_index("expert")
+    place = jnp.stack([z, core]).astype(jnp.int32)
+    gate_grad, up_grad, down_grad, query_grad, key_grad, value_grad, out_grad, router_grad = weight_grads(
+        place,
+        x_all,
+        g_all,
+        wr,
+        att_all,
+        da_cols,
+        n1_cols,
+        d_all,
+        ghid,
+        dgp,
+        dup,
+        w_gate,
+        w_up,
+        w_down,
+        key_projection.shape[1],
+        experts,
+    )
+    gains = lax.dynamic_slice_in_dim(gains, core * half, half, axis=1)
+    return (
+        output,
+        input_grad,
+        gains[0],
+        query_grad,
+        key_grad,
+        value_grad,
+        out_grad,
+        gains[1],
+        router_grad,
+        gate_grad,
+        up_grad,
+        down_grad,
+    )
+
+
 def solution(mesh):
     placed = (
         P(("dp", "expert"), None),
@@ -399,8 +1349,11 @@
         P(("dp", "expert"), None),
         P(("dp", "expert"), None),
     )
+    sequences = mesh.shape["dp"] * mesh.shape["expert"]
+    few = sequences * SEQUENCE_LENGTH <= GATHER_ROWS
+    few = few and mesh.shape["tensor"] > 1 and mesh.shape["expert"] == 2
     return jax.shard_map(
-        local,
+        gather_plan if few else reduce_plan,
         mesh=mesh,
         in_specs=placed,
         out_specs=(

time: 976 us -> 304 us (0.31)
  waiting for transfers between devices: 484 us -> 0 us
  Pallas kernels: 0 us -> 288 us
  local copies, waits for them, and re-layouts: 226 us -> 11.9 us
  matrix products: 103 us -> 0 us
  other arithmetic: 65.5 us -> 2.24 us
  blocking collectives: 50.9 us -> 0 us
  starting transfers between devices: 21.6 us -> 0 us
  between operations: 15.5 us -> 0.73 us
    pallas_call x0 -> x4, Pallas kernels: none -> 288 us  [the longest x1 91.8 us: weight_grads(): pl.pallas_call(weights_kernel, grid_spec=pltpu.PrefetchScalarGridSpec(num...]
    reduce_scatter x2 -> x0, waiting for transfers between devices: 277 us -> none  [the longest x1 142 us: local(): lax.psum_scatter(up_local.astype(jnp.bfloat16), 'dp', scatter_dimension=1...]
    all_to_all x4 -> x0, waiting for transfers between devices: 150 us -> none  [the longest x3 150 us: sum_at_owner(): lax.all_to_all(tiles, axis, split_axis=0, concat_axis=0, tiled=True)]
    dot_general x31 -> x0, matrix products: 103 us -> none  [the longest x1 13.2 us: local(): jnp.einsum('sech,edh->secd', d_up, w_up, preferred_element_type=jnp.float32)]
    gather x10 -> x0, local copies, waits for them, and re-layouts: 85.2 us -> none  [the longest x1 17.6 us: local(): returned.reshape(expert_count * capacity, model_width)[slot_where]]
    slice x5 -> x1, local copies, waits for them, and re-layouts: 63.7 us -> 1.43 us  [gather_plan(): gains[1]]
    psum x3 -> x0, waiting for transfers between devices: 55.4 us -> none  [the longest x1 40.2 us: local(): lax.psum(back_part.astype(jnp.bfloat16), 'tensor').astype(jnp.float32)]
    all_to_all x3 -> x0, blocking collectives: 41.5 us -> none  [the longest x1 17.9 us: local(): lax.all_to_all(expert_out.reshape(expert_count, capacity, model_width), '...]
  transfers between devices with their start and end apart: 10 -> 0, of which waited for: 9 -> 0; matrix products, arithmetic and copies ran while one was open for 18% -> 0% of each run, Pallas kernels for 0% -> 0%
where the time goes in v2:
time: 304 us; the launch traced here: 303 us
  Pallas kernels  288 us (95%)
  local copies, waits for them, and re-layouts  11.9 us (4%)
    pallas_call x1, Pallas kernels, weight_grads(): pl.pallas_call(weights_kernel, grid_spec=pltpu.PrefetchScalarGridSpec(num...  91.8 us
    pallas_call x1, Pallas kernels, backward(): pl.pallas_call(functools.partial(backward_kernel, dp, tp), out_shape=[jax...  91.2 us
    pallas_call x1, Pallas kernels, plane_experts(): pl.pallas_call(functools.partial(plane_kernel, dp, tp), grid=(count // 2,...  68.9 us
    pallas_call x1, Pallas kernels, forward(): pl.pallas_call(functools.partial(forward_kernel, dp, tp), out_shape=[jax....  36.6 us
    unnamed x12, local copies, waits for them, and re-layouts  7 us

profile of v2, /device:TPU:0, one launch (start us, length us, event | category | flops | bytes accessed | tf_op | source)
XLA Modules:
  0.0 303.3 jit_solution(5872492804511225935)
XLA Ops:
  0.6 1.5 copy.25.routes_ref
  2.1 1.3 broadcast_in_dim.11.ga_ref
  3.4 1.3 broadcast_in_dim.12.gm_ref
  4.7 0.5 fusion.1
  5.3 0.4 maximum_bitcast_fusion.1
  5.6 0.8 pad_maximum_fusion.rope_ref
  6.4 0.0 copy-start.2
  6.4 36.6 %forward.1 = (bf16[512,1664]{1,0:T(8,128)(2,1)}, bf16[512,1536]{1,0:T(8,128)(2,1)}, bf16[3,64,1536]{2,1,0:T(8,128)(2,1)}, f32[64,1536]{1,0:T(8,128)}, bf16[256,1...) custom-call(bf16[256,1536]{1,0:T(8,128)(2,1)} %tok_ref.3, ...), custom_call_target="tpu_custom_call" | custom-call | tf_op jit(solution)/shard_map/forward/pallas_call | solution.py:601
  43.0 0.0 copy-done.2
  43.1 0.2 copy.26
  43.3 0.8 pad.4.wr_ref
  44.1 68.9 %plane_experts.1 = (bf16[2048,1664]{1,0:T(8,128)(2,1)}, bf16[2048,1536]{1,0:T(8,128)(2,1)}, bf16[2048,384]{1,0:T(8,128)(2,1)}, bf16[512,1536]{1,0:T(8,128)(2,1)}...) custom-call(bf16[512,1664]{1,0:T(8,128)(2,1)} %get-tuple-element.44., ...), custom_call_target="tpu_custom_call" | custom-call | tf_op jit(solution)/shard_map/plane_experts/pallas_call | solution.py:840
  113.0 91.2 %backward.1 = (bf16[256,1536]{1,0:T(8,128)(2,1)}, bf16[256,1536]{1,0:T(8,128)(2,1)}, bf16[2048,384]{1,0:T(8,128)(2,1)}, bf16[2048,384]{1,0:T(8,128)(2,1)}, bf16[2048,768]{1,0:T(8,128)(2,1)}, /*index=5*/f32[8,384]{1,0:T(8,128)}) custom-call(bf16[512,1536]{1,0:T(8,128)(2,1)} %get-tuple-element.48.back_ref, bf16[512,1536]{1,0:T(8,128)(2,1)} %get-tuple-element.49.moe_ref, ...), custom_call_target="tpu_custom_call" | custom-call | tf_op jit(solution)/shard_map/backward/pallas_call | solution.py:1093
  204.2 1.4 fusion.3
  205.7 0.6 pad_add_fusion.place_ref
  206.3 0.0 copy-start.1
  206.3 91.8 %weight_grads.1 = (f32[20,384,128]{2,1,0:T(8,128)}, f32[20,384,128]{2,1,0:T(8,128)}, f32[20,128,384]{2,1,0:T(8,128)}, f32[192,384]{1,0:T(8,128)}, f32[192,128]{1...) custom-call(s32[2]{0:T(128)} %pad_add_fusion.place_ref, ...), custom_call_target="tpu_custom_call" | custom-call | tf_op jit(solution)/shard_map/weight_grads/pallas_call | solution.py:1234
  298.0 0.0 copy-start
  298.0 1.9 copy.27
  300.0 1.6 copy.28
  301.6 0.0 copy-done.1
  301.6 0.9 copy.31
  302.4 0.0 copy-done
  302.4 0.9 copy.32
  (2 shorter events, 0.0 us)
Async XLA Ops:
  6.4 36.6 %copy-start.2 = (bf16[1536,40]{0,1:T(8,128)(2,1)S(1)}, bf16[1536,40]{0,1:T(8,128)(2,1)}, u32[]{:S(2)}) copy-start(bf16[1536,40]{0,1:T(8,128)(2,1)} %param.20) | copy-start | bytes 368644
  206.3 95.3 %copy-start.1 = (bf16[256,1536]{1,0:T(8,128)(2,1)S(1)}, bf16[256,1536]{1,0:T(8,128)(2,1)}, u32[]{:S(2)}) copy-start(bf16[256,1536]{1,0:T(8,128)(2,1)} %get-tuple-element.108) | copy-start | bytes 2359300
  298.0 4.4 %copy-start = (bf16[256,1536]{1,0:T(8,128)(2,1)S(1)}, bf16[256,1536]{1,0:T(8,128)(2,1)}, u32[]{:S(2)}) copy-start(bf16[256,1536]{1,0:T(8,128)(2,1)} %get-tuple-element.109) | copy-start | bytes 2359300

commit v3 on v2

--- a/solution.py
+++ b/solution.py
@@ -880,12 +880,23 @@
     att_ref,
     lse_ref,
     rope_ref,
+    xr_ref,
+    gr_ref,
+    wg_ref,
+    wu_ref,
+    wd_ref,
     out_ref,
     in_ref,
     att_all,
     da_cols,
     d_all,
     gains_ref,
+    ghid_ref,
+    dgp_ref,
+    dup_ref,
+    x_rest,
+    g_rest,
+    split,
     pair_b,
     pair_m,
     pair_d,
@@ -895,6 +906,7 @@
     rs_b,
     rs_m,
     rs_d,
+    dh1_buf,
     da_buf,
     dl_buf,
     d_buf,
@@ -906,15 +918,19 @@
     gain_z,
     gain_zs,
     gain_c,
+    out_buf,
+    in_buf,
     send_sem,
     recv_sem,
     keep_sem,
 ):
+    step, last = pl.program_id(0), pl.num_programs(0) - 1
     net = Peers(dp, tp, send_sem, recv_sem)
     z, c, t = net.z, net.c, net.t
     length, model = tok_ref.shape
     own = length // tp
     part = model // dp
+    width = wg_ref.shape[2]
     q_width, kv_width = wq_ref.shape[1], wk_ref.shape[1]
     group = q_width // kv_width
     others, sides = range(1, dp), range(1, tp)
@@ -924,214 +940,320 @@
     def columns(index):
         return pl.ds(pl.multiple_of(index * part, 128), part)
 
+    def link(src, dst, device):
+        return net.make(src, dst, net.number(1), device)
+
     def to_sides(ref, into):
         return [
-            net.to(ref.at[ds(lax.rem(t + k, tp), own)], into.at[k - 1], net.tensor(k))
-            for k in sides
+            link(ref.at[ds(lax.rem(t + k, tp), own)], into.at[k - 1], net.tensor(k)) for k in sides
         ]
 
     def share(ref):
-        return [net.to(ref.at[mine], ref.at[mine], net.tensor(k)) for k in sides]
+        return [link(ref.at[mine], ref.at[mine], net.tensor(k)) for k in sides]
 
     def on_to_partner(ref):
         rows = [ds(p * 2 + c, length) for p in others]
-        return [net.to(ref.at[r], ref.at[r], net.partner()) for r in rows]
-
-    net.greet()
-    got_b = [
-        net.to(back_ref.at[there], pair_b, net.partner()),
-        net.to(dgate_ref.at[there], pair_d, net.partner()),
+        return [link(ref.at[r], ref.at[r], net.partner()) for r in rows]
+
+    def over_planes(ref, into):
+        return [link(ref, into.at[ds((dp - k) * 2 + c, length)], net.plane(k)) for k in others]
+
+    def start(copies):
+        for copy in copies:
+            copy.start()
+
+    pair_bd = [
+        link(back_ref.at[there], pair_b, net.partner()),
+        link(dgate_ref.at[there], pair_d, net.partner()),
     ]
-    got_m = [net.to(moe_ref.at[there], pair_m, net.partner())]
-    att_z = [net.to(att_ref, att_all.at[ds((dp - k) * 2 + c, length)], net.plane(k)) for k in others]
-    att_own = net.to(att_ref, att_all.at[here], net.partner())
-    kept = [net.keep(att_ref, att_all.at[here], keep_sem.at[0])]
-    arrived(got_b)
-    sum_b[...] = (back_ref[here, :].astype(F32) + pair_b[...].astype(F32)).astype(BF16)
-    sum_d[...] = dgate_ref[here, :] + pair_d[...]
-    got_b = to_sides(sum_b, rs_b) + to_sides(sum_d, rs_d)
-    arrived(got_m)
-    sum_m[...] = (moe_ref[here, :].astype(F32) + pair_m[...].astype(F32)).astype(BF16)
-    arrived(got_b)
-    d_n2 = sum_b[mine, :].astype(F32)
-    dgate = sum_d[mine, :]
-    for k in sides:
-        d_n2 = d_n2 + rs_b[k - 1].astype(F32)
-        dgate = dgate + rs_d[k - 1]
-    gates = gates_ref[ds(c * tp + t, own), :]
-    d_logits = gates * (dgate - jnp.sum(gates * dgate, axis=1, keepdims=True))
-    dl_buf[mine, :] = d_logits.astype(BF16)
-    d_n2 = d_n2 + dot_nt(d_logits.astype(BF16), wr_ref[...])
-    h1 = h1_ref[...]
-    r2 = inverse_rms(h1)
-    weighted = d_n2 * gm_ref[...]
-    inner = jnp.mean(weighted * h1, axis=-1, keepdims=True)
-    gain_buf[...] = jnp.zeros_like(gain_buf)
-    gain_buf[1:2, :] = jnp.sum(d_n2 * h1 * r2, axis=0, keepdims=True)
-    d_h1 = cot_ref[mine, :].astype(F32) + (r2 * weighted - h1 * (r2 * r2 * r2) * inner)
-    da_buf[mine, :] = d_h1.astype(BF16)
-    got_da = share(da_buf) + share(dl_buf)
-    got_m = to_sides(sum_m, rs_m)
-    arrived(att_z)
+    pair_mo = [link(moe_ref.at[there], pair_m, net.partner())]
+    att_z = over_planes(att_ref, att_all)
     att_c = on_to_partner(att_all)
-    arrived(got_da)
-    d_buf[:, q_width + 2 * kv_width :] = dl_buf[...]
+    att_own = [link(att_ref, att_all.at[here], net.partner())]
+    side_bd = to_sides(sum_b, rs_b) + to_sides(sum_d, rs_d)
+    side_mo = to_sides(sum_m, rs_m)
+    share_da = share(da_buf) + share(dl_buf)
     da_z = [
-        net.to(
+        link(
             da_buf.at[:, columns(lax.rem(z + k, dp))],
             da_cols.at[ds((dp - k) * 2 + c, length)],
             net.plane(k),
         )
         for k in others
     ]
-    da_own = net.to(da_buf.at[:, columns(z)], da_cols.at[here], net.partner())
-    kept.append(net.keep(da_buf.at[:, columns(z)], da_cols.at[here], keep_sem.at[1]))
-    do_buf[...] = dot_nt(da_buf[...], wo_ref[...]).astype(BF16)
-
-    arrived(got_m)
-    total = h1 + sum_m[mine, :].astype(F32)
-    for k in sides:
-        total = total + rs_m[k - 1].astype(F32)
-    out_ref[mine, :] = total.astype(BF16)
-    got_out = share(out_ref)
-
-    seen = causal(length)
-    scale = HEAD_SIZE ** (-0.5)
-    d_key, d_val, d_query = [], [], []
-    for kv in range(kv_width // HEAD_SIZE):
-        at_k = q_width + kv * HEAD_SIZE
-        at_v = q_width + kv_width + kv * HEAD_SIZE
-        key = qkv_ref[:, at_k : at_k + HEAD_SIZE]
-        val = qkv_ref[:, at_v : at_v + HEAD_SIZE]
-        dk = jnp.zeros((length, HEAD_SIZE), F32)
-        dv = jnp.zeros((length, HEAD_SIZE), F32)
-        for h in range(kv * group, (kv + 1) * group):
-            at = slice(h * HEAD_SIZE, (h + 1) * HEAD_SIZE)
-            q = qkv_ref[:, at]
-            d_out = do_buf[:, at]
-            s = jnp.where(seen, dot_nt(q, key) * scale, -1e30)
-            prob = jnp.exp(s - lse_ref[:, h : h + 1])
-            delta = jnp.sum(d_out.astype(F32) * att_ref[:, at].astype(F32), axis=-1, keepdims=True)
-            d_s = (prob * (dot_nt(d_out, val) - delta)).astype(BF16)
-            d_query.append(dot(d_s, key) * scale)
-            dk = dk + dot_tn(d_s, q)
-            dv = dv + dot_tn(prob.astype(BF16), d_out)
-        d_key.append(dk * scale)
-        d_val.append(dv)
-    d_buf[:, :q_width] = rotate(jnp.concatenate(d_query, axis=1), rope_ref, -1.0).astype(BF16)
-    d_buf[:, q_width : q_width + kv_width] = rotate(
-        jnp.concatenate(d_key, axis=1), rope_ref, -1.0
-    ).astype(BF16)
-    d_buf[:, q_width + kv_width : q_width + 2 * kv_width] = jnp.concatenate(d_val, axis=1).astype(BF16)
-    d_z = [net.to(d_buf, d_all.at[ds((dp - k) * 2 + c, length)], net.plane(k)) for k in others]
-    d_own = net.to(d_buf, d_all.at[here], net.partner())
-    kept.append(net.keep(d_buf, d_all.at[here], keep_sem.at[2]))
-    part_n1 = dot_nt(d_buf[:, :q_width], wq_ref[...])
-    part_n1 = part_n1 + dot_nt(d_buf[:, q_width : q_width + kv_width], wk_ref[...])
-    part_n1 = part_n1 + dot_nt(
-        d_buf[:, q_width + kv_width : q_width + 2 * kv_width], wv_ref[...]
-    )
-    part_buf[...] = part_n1.astype(BF16)
-    got_3 = to_sides(part_buf, rs_3)
-    arrived(da_z)
     da_c = on_to_partner(da_cols)
-    arrived(got_3)
-    d_n1 = part_buf[mine, :].astype(F32)
-    for k in sides:
-        d_n1 = d_n1 + rs_3[k - 1].astype(F32)
-    resid = tok_ref[mine, :].astype(F32)
-    r1 = inverse_rms(resid)
-    weighted = d_n1 * ga_ref[...]
-    inner = jnp.mean(weighted * resid, axis=-1, keepdims=True)
-    gain_buf[0:1, :] = jnp.sum(d_n1 * resid * r1, axis=0, keepdims=True)
-    d_x = d_h1 + (r1 * weighted - resid * (r1 * r1 * r1) * inner)
-    in_ref[mine, :] = d_x.astype(BF16)
-    got_gain = [net.to(gain_buf, gain_t.at[k - 1], net.tensor(k)) for k in sides]
-    got_in = share(in_ref)
-    arrived(got_gain)
-    gain = gain_buf[...]
-    for k in sides:
-        gain = gain + gain_t[k - 1]
-    gain_zs[...] = gain
-    got_gain = [
-        net.to(gain_zs.at[:, columns(lax.rem(z + k, dp))], gain_z.at[k - 1], net.plane(k))
+    da_own = [link(da_buf.at[:, columns(z)], da_cols.at[here], net.partner())]
+    share_out = share(out_buf)
+    d_z = over_planes(d_buf, d_all)
+    d_c = on_to_partner(d_all)
+    d_own = [link(d_buf, d_all.at[here], net.partner())]
+    side_3 = to_sides(part_buf, rs_3)
+    share_in = share(in_buf)
+    side_gain = [link(gain_buf, gain_t.at[k - 1], net.tensor(k)) for k in sides]
+    plane_gain = [
+        link(gain_zs.at[:, columns(lax.rem(z + k, dp))], gain_z.at[k - 1], net.plane(k))
         for k in others
     ]
-    arrived(got_gain)
-    gain = gain_zs[:, columns(z)]
-    for k in others:
-        gain = gain + gain_z[k - 1]
-    gain_c[0] = gain
-    got_gain = net.to(gain_c.at[0], gain_c.at[1], net.partner())
-    arrived(d_z)
-    d_c = on_to_partner(d_all)
-    arrived([got_gain])
-    gains_ref[...] = gain + gain_c[1]
-    arrived(got_out + got_in + [att_own, da_own, d_own] + att_c + da_c + d_c)
-    for copy in kept:
-        copy.wait()
-    net.drain()
-
-
-def backward(dp, tp, *arrays):
-    back, _, _, _, _, tokens, _, _, _, _, wq, wk, wv = arrays[:13]
-    rows, model = back.shape
+    pair_gain = [link(gain_c.at[0], gain_c.at[1], net.partner())]
+    keep_att = pltpu.make_async_copy(att_ref, att_all.at[here], keep_sem.at[0])
+    keep_da = pltpu.make_async_copy(da_buf.at[:, columns(z)], da_cols.at[here], keep_sem.at[1])
+    keep_d = pltpu.make_async_copy(d_buf, d_all.at[here], keep_sem.at[2])
+    plane_rows = xr_ref.shape[0] // dp
+    rest = pl.ds(plane_rows, xr_ref.shape[0] - plane_rows)
+    load_x = pltpu.make_async_copy(xr_ref.at[rest], x_rest, keep_sem.at[3])
+    load_g = pltpu.make_async_copy(gr_ref.at[rest], g_rest, keep_sem.at[4])
+
+    @pl.when(step == 0)
+    def _():
+        load_x.start()
+        load_g.start()
+        net.greet()
+        start(pair_bd + pair_mo + att_z + att_own)
+        keep_att.start()
+        load_x.wait()
+        store_split(gates_of(x_rest, wr_ref, model), split)
+        load_g.wait()
+
+    @pl.when(step == 1)
+    def _():
+        arrived(pair_bd)
+        sum_b[...] = (back_ref[here, :].astype(F32) + pair_b[...].astype(F32)).astype(BF16)
+        sum_d[...] = dgate_ref[here, :] + pair_d[...]
+        start(side_bd)
+
+    @pl.when(step == 3)
+    def _():
+        arrived(side_bd)
+        d_n2 = sum_b[mine, :].astype(F32)
+        dgate = sum_d[mine, :]
+        for k in sides:
+            d_n2 = d_n2 + rs_b[k - 1].astype(F32)
+            dgate = dgate + rs_d[k - 1]
+        gates = gates_ref[ds(c * tp + t, own), :]
+        d_logits = gates * (dgate - jnp.sum(gates * dgate, axis=1, keepdims=True))
+        dl_buf[mine, :] = d_logits.astype(BF16)
+        d_n2 = d_n2 + dot_nt(d_logits.astype(BF16), wr_ref[...])
+        h1 = h1_ref[...]
+        r2 = inverse_rms(h1)
+        weighted = d_n2 * gm_ref[...]
+        inner = jnp.mean(weighted * h1, axis=-1, keepdims=True)
+        gain_buf[...] = jnp.zeros_like(gain_buf)
+        gain_buf[1:2, :] = jnp.sum(d_n2 * h1 * r2, axis=0, keepdims=True)
+        d_h1 = cot_ref[mine, :].astype(F32) + (r2 * weighted - h1 * (r2 * r2 * r2) * inner)
+        dh1_buf[...] = d_h1
+        da_buf[mine, :] = d_h1.astype(BF16)
+        start(share_da)
+        arrived(pair_mo)
+        sum_m[...] = (moe_ref[here, :].astype(F32) + pair_m[...].astype(F32)).astype(BF16)
+        start(side_mo)
+        arrived(att_z)
+        start(att_c)
+
+    @pl.when(step == 5)
+    def _():
+        arrived(share_da)
+        start(da_z + da_own)
+        keep_da.start()
+        d_buf[:, q_width + 2 * kv_width :] = dl_buf[...]
+        do_buf[...] = dot_nt(da_buf[...], wo_ref[...]).astype(BF16)
+        arrived(side_mo)
+        total = h1_ref[...] + sum_m[mine, :].astype(F32)
+        for k in sides:
+            total = total + rs_m[k - 1].astype(F32)
+        out_buf[mine, :] = total.astype(BF16)
+        start(share_out)
+        seen = causal(length)
+        scale = HEAD_SIZE ** (-0.5)
+        d_key, d_val, d_query = [], [], []
+        for kv in range(kv_width // HEAD_SIZE):
+            at_k = q_width + kv * HEAD_SIZE
+            at_v = q_width + kv_width + kv * HEAD_SIZE
+            key = qkv_ref[:, at_k : at_k + HEAD_SIZE]
+            val = qkv_ref[:, at_v : at_v + HEAD_SIZE]
+            dk = jnp.zeros((length, HEAD_SIZE), F32)
+            dv = jnp.zeros((length, HEAD_SIZE), F32)
+            for h in range(kv * group, (kv + 1) * group):
+                at = slice(h * HEAD_SIZE, (h + 1) * HEAD_SIZE)
+                q = qkv_ref[:, at]
+                d_out = do_buf[:, at]
+                s = jnp.where(seen, dot_nt(q, key) * scale, -1e30)
+                prob = jnp.exp(s - lse_ref[:, h : h + 1])
+                delta = jnp.sum(
+                    d_out.astype(F32) * att_ref[:, at].astype(F32), axis=-1, keepdims=True
+                )
+                d_s = (prob * (dot_nt(d_out, val) - delta)).astype(BF16)
+                d_query.append(dot(d_s, key) * scale)
+                dk = dk + dot_tn(d_s, q)
+                dv = dv + dot_tn(prob.astype(BF16), d_out)
+            d_key.append(dk * scale)
+            d_val.append(dv)
+        d_buf[:, :q_width] = rotate(jnp.concatenate(d_query, axis=1), rope_ref, -1.0).astype(BF16)
+        d_buf[:, q_width : q_width + kv_width] = rotate(
+            jnp.concatenate(d_key, axis=1), rope_ref, -1.0
+        ).astype(BF16)
+        d_buf[:, q_width + kv_width : q_width + 2 * kv_width] = jnp.concatenate(
+            d_val, axis=1
+        ).astype(BF16)
+        part_n1 = dot_nt(d_buf[:, :q_width], wq_ref[...])
+        part_n1 = part_n1 + dot_nt(d_buf[:, q_width : q_width + kv_width], wk_ref[...])
+        part_n1 = part_n1 + dot_nt(
+            d_buf[:, q_width + kv_width : q_width + 2 * kv_width], wv_ref[...]
+        )
+        part_buf[...] = part_n1.astype(BF16)
+        start(side_3 + d_z + d_own)
+        keep_d.start()
+
+    @pl.when(step == 7)
+    def _():
+        arrived(side_3)
+        d_n1 = part_buf[mine, :].astype(F32)
+        for k in sides:
+            d_n1 = d_n1 + rs_3[k - 1].astype(F32)
+        resid = tok_ref[mine, :].astype(F32)
+        r1 = inverse_rms(resid)
+        weighted = d_n1 * ga_ref[...]
+        inner = jnp.mean(weighted * resid, axis=-1, keepdims=True)
+        gain_buf[0:1, :] = jnp.sum(d_n1 * resid * r1, axis=0, keepdims=True)
+        d_x = dh1_buf[...] + (r1 * weighted - resid * (r1 * r1 * r1) * inner)
+        in_buf[mine, :] = d_x.astype(BF16)
+        start(side_gain + share_in)
+        arrived(da_z)
+        start(da_c)
+
+    @pl.when(step == 8)
+    def _():
+        arrived(side_gain)
+        gain = gain_buf[...]
+        for k in sides:
+            gain = gain + gain_t[k - 1]
+        gain_zs[...] = gain
+        start(plane_gain)
+
+    @pl.when(step == 9)
+    def _():
+        arrived(plane_gain)
+        gain = gain_zs[:, columns(z)]
+        for k in others:
+            gain = gain + gain_z[k - 1]
+        gain_c[0] = gain
+        start(pair_gain)
+
+    first = c * (2 * pl.num_programs(0)) + 2 * step
+    wd_pair = wd_ref[...].reshape(2 * width, model)
+    gate_pair = pair_of_gates(split[...], first, width)
+    dh_pair = dot_nt(g_rest[...], wd_pair)
+    for k in range(2):
+        lanes = slice(k * width, (k + 1) * width)
+        both = dot(x_rest[:, :model], jnp.concatenate([wg_ref[k], wu_ref[k]], axis=1))
+        _, ghid, dgp, dup = swiglu(both, dh_pair[:, lanes], gate_pair[:, lanes])
+        ghid_ref[:, lanes] = ghid
+        dgp_ref[:, lanes] = dgp
+        dup_ref[:, lanes] = dup
+
+    @pl.when(step == last)
+    def _():
+        arrived(d_z)
+        start(d_c)
+        arrived(pair_gain)
+        gains_ref[...] = gain_c[0] + gain_c[1]
+        arrived(share_out + share_in + att_own + da_own + d_own + att_c + da_c + d_c)
+        out_ref[...] = out_buf[...]
+        in_ref[...] = in_buf[...]
+        for copy in (keep_att, keep_da, keep_d):
+            copy.wait()
+        sent = pair_bd + pair_mo + att_z + att_c + att_own + side_bd + side_mo + share_da
+        sent = sent + da_z + da_c + da_own + share_out + d_z + d_c + d_own + side_3 + share_in
+        for copy in sent + side_gain + plane_gain + pair_gain:
+            copy.wait_send()
+
+
+def whole_spec(a):
+    shape = a.shape
+    return pl.BlockSpec(shape, lambda *_: (0,) * len(shape), pipeline_mode=pl.Buffered(1))
+
+
+def backward(dp, tp, arrays, streamed, weights):
+    tokens = arrays[5]
+    wq, wk, wv = arrays[10:13]
+    all_rows, model = streamed[1].shape
+    rest_rows = all_rows - all_rows // dp
+    count, _, width = weights[0].shape
     length = tokens.shape[0]
     own, part = length // tp, model // dp
     q_width = wq.shape[1]
     wide = q_width + wk.shape[1] + wv.shape[1] + EXTRA
     others, sides = dp - 1, tp - 1
-    copies = 3 + 3 * (2 * others + 1) + 2 * sides + 2 * sides + 4 * sides + sides + others + 1
+    copies = 3 + 3 * (2 * others + 1) + 9 * sides + sides + others + 1
+    by_pair = lambda shape: pl.BlockSpec((2,) + shape, lambda i: (i, 0, 0))
+    saved = pl.BlockSpec((rest_rows, 2 * width), lambda i: (0, i))
     shapes = [
         ((length, model), BF16),
         ((length, model), BF16),
-        ((rows * dp, q_width), BF16),
-        ((rows * dp, part), BF16),
-        ((rows * dp, wide), BF16),
+        ((all_rows, q_width), BF16),
+        ((all_rows, part), BF16),
+        ((all_rows, wide), BF16),
         ((8, part), F32),
+        ((rest_rows, count * width), BF16),
+        ((rest_rows, count * width), BF16),
+        ((rest_rows, count * width), BF16),
+    ]
+    shapes = [jax.ShapeDtypeStruct(*s) for s in shapes]
+    full, block, slots = (length, model), (own, model), (sides, own, model)
+    scratch = [
+        ((rest_rows, streamed[0].shape[1]), BF16),
+        ((rest_rows, model), BF16),
+        ((rest_rows, 2 * EXTRA), BF16),
+        (full, BF16),
+        (full, BF16),
+        ((length, EXTRA), F32),
+        (full, BF16),
+        (full, BF16),
+        ((length, EXTRA), F32),
+        (slots, BF16),
+        (slots, BF16),
+        ((sides, own, EXTRA), F32),
+        (block, F32),
+        (full, BF16),
+        ((length, EXTRA), BF16),
+        ((length, wide), BF16),
+        ((length, q_width), BF16),
+        (full, BF16),
+        (slots, BF16),
+        ((8, model), F32),
+        ((sides, 8, model), F32),
+        ((others, 8, part), F32),
+        ((8, model), F32),
+        ((2, 8, part), F32),
+        (full, BF16),
+        (full, BF16),
     ]
     return pl.pallas_call(
         functools.partial(backward_kernel, dp, tp),
-        out_shape=[jax.ShapeDtypeStruct(*s) for s in shapes],
-        in_specs=[VMEM] * len(arrays),
-        out_specs=[VMEM, VMEM, ANY, ANY, ANY, VMEM],
-        scratch_shapes=[
-            pltpu.VMEM((length, model), BF16),
-            pltpu.VMEM((length, model), BF16),
-            pltpu.VMEM((length, EXTRA), F32),
-            pltpu.VMEM((length, model), BF16),
-            pltpu.VMEM((length, model), BF16),
-            pltpu.VMEM((length, EXTRA), F32),
-            pltpu.VMEM((sides, own, model), BF16),
-            pltpu.VMEM((sides, own, model), BF16),
-            pltpu.VMEM((sides, own, EXTRA), F32),
-            pltpu.VMEM((length, model), BF16),
-            pltpu.VMEM((length, EXTRA), BF16),
-            pltpu.VMEM((length, wide), BF16),
-            pltpu.VMEM((length, q_width), BF16),
-            pltpu.VMEM((length, model), BF16),
-            pltpu.VMEM((sides, own, model), BF16),
-            pltpu.VMEM((8, model), F32),
-            pltpu.VMEM((sides, 8, model), F32),
-            pltpu.VMEM((others, 8, part), F32),
-            pltpu.VMEM((8, model), F32),
-            pltpu.VMEM((2, 8, part), F32),
+        grid=(count // 2,),
+        out_shape=shapes,
+        in_specs=[whole_spec(a) for a in arrays]
+        + [ANY, ANY]
+        + [by_pair((model, width)), by_pair((model, width)), by_pair((width, model))],
+        out_specs=[whole_spec(shapes[0]), whole_spec(shapes[1]), ANY, ANY, ANY]
+        + [whole_spec(shapes[5])]
+        + [saved] * 3,
+        scratch_shapes=[pltpu.VMEM(*s) for s in scratch]
+        + [
             pltpu.SemaphoreType.DMA((copies,)),
             pltpu.SemaphoreType.DMA((copies,)),
-            pltpu.SemaphoreType.DMA((3,)),
+            pltpu.SemaphoreType.DMA((5,)),
         ],
         compiler_params=pltpu.CompilerParams(
             collective_id=2, has_side_effects=True, vmem_limit_bytes=VMEM_LIMIT
         ),
         name="backward",
-    )(*arrays)
+    )(*arrays, *streamed, *weights)
 
 
 def weights_kernel(
     place_ref,
     x_ref,
     g_ref,
-    wr_ref,
     att_ref,
     da_ref,
     n1_ref,
@@ -1139,9 +1261,9 @@
     ghid_ref,
     dgp_ref,
     dup_ref,
-    wg_ref,
-    wu_ref,
-    wd_ref,
+    ghid_rest,
+    dgp_rest,
+    dup_rest,
     gate_grad_ref,
     up_grad_ref,
     down_grad_ref,
@@ -1150,57 +1272,38 @@
     value_ref,
     out_grad_ref,
     router_ref,
-    split,
     xt_buf,
     gt_buf,
-    hid_buf,
-    dgate_buf,
-    dup_buf,
     side_buf,
 ):
     step = pl.program_id(0)
-    z, c = place_ref[0], place_ref[1]
-    rows, model = g_ref.shape
-    width = wg_ref.shape[2]
-    part = xt_buf.shape[0]
+    c = place_ref[1]
+    width = gate_grad_ref.shape[2]
     plane_rows = ghid_ref.shape[0]
-    rest = slice(plane_rows, rows)
 
     @pl.when(step == 0)
     def _():
-        store_split(gates_of(x_ref, wr_ref, model), split)
-        cols = pl.ds(pl.multiple_of(z * part, 128), part)
-        xt_buf[...] = x_ref[:, cols].T
-        gt_buf[...] = g_ref[:, cols].T
+        xt_buf[...] = x_ref[...].T
+        gt_buf[...] = g_ref[...].T
         q_width, kv_width = query_ref.shape[1], key_ref.shape[1]
         half = query_ref.shape[0]
         at = pl.ds(pl.multiple_of(c * half, 8), half)
-        side_buf[:, : d_ref.shape[1] - EXTRA] = dot_tn(n1_ref[...], d_ref[:, : d_ref.shape[1] - EXTRA])
-        side_buf[:, d_ref.shape[1] - EXTRA :] = dot(xt_buf[...], d_ref[:, d_ref.shape[1] - EXTRA :])
+        tail = d_ref.shape[1] - EXTRA
+        side_buf[:, :tail] = dot_tn(n1_ref[...], d_ref[:, :tail])
+        side_buf[:, tail:] = dot(xt_buf[...], d_ref[:, tail:])
         query_ref[...] = side_buf[at, :q_width]
         key_ref[...] = side_buf[at, q_width : q_width + kv_width]
         value_ref[...] = side_buf[at, q_width + kv_width : q_width + 2 * kv_width]
-        router_ref[...] = side_buf[at, d_ref.shape[1] - EXTRA :][:, : router_ref.shape[1]]
+        router_ref[...] = side_buf[at, tail:][:, : router_ref.shape[1]]
         out_all = dot_tn(att_ref[...], da_ref[...])
         out_grad_ref[...] = jnp.where(c == 0, out_all[:, :half], out_all[:, half:])
 
-    first = c * (2 * pl.num_programs(0)) + 2 * step
-    wd_pair = wd_ref[...].reshape(2 * width, model)
-    gate_pair = pair_of_gates(split[rest, :], first, width)
-    dh_pair = dot_nt(g_ref[rest, :], wd_pair)
-    hid_buf[:plane_rows, :] = ghid_ref[...]
-    dgate_buf[:plane_rows, :] = dgp_ref[...]
-    dup_buf[:plane_rows, :] = dup_ref[...]
-    for k in range(2):
-        lanes = slice(k * width, (k + 1) * width)
-        both = dot(x_ref[rest, :model], jnp.concatenate([wg_ref[k], wu_ref[k]], axis=1))
-        _, ghid, dgp, dup = swiglu(both, dh_pair[:, lanes], gate_pair[:, lanes])
-        hid_buf[rest, lanes] = ghid
-        dgate_buf[rest, lanes] = dgp
-        dup_buf[rest, lanes] = dup
-    gate_both = dot(xt_buf[...], dgate_buf[...])
-    up_both = dot(xt_buf[...], dup_buf[...])
-    down_both = dot(gt_buf[...], hid_buf[...]).T
+    def contract(left, own, rest):
+        return dot(left[:, :plane_rows], own[...]) + dot(left[:, plane_rows:], rest[...])
+
+    gate_both = contract(xt_buf, dgp_ref, dgp_rest)
+    up_both = contract(xt_buf, dup_ref, dup_rest)
+    down_both = contract(gt_buf, ghid_ref, ghid_rest).T
     for k in range(2):
         lanes = slice(k * width, (k + 1) * width)
         gate_grad_ref[k] = gate_both[:, lanes]
@@ -1208,18 +1311,15 @@
         down_grad_ref[k] = down_both[lanes, :]
 
 
-def weight_grads(place, x, g, wr, att, da, n1, d, ghid, dgp, dup, w_gate, w_up, w_down, kv_width, experts):
-    rows, model = g.shape
-    count, _, width = w_gate.shape
+def weight_grads(place, x, g, sides, own, rest, count, kv_width, experts):
+    rows = x.shape[0]
+    att, _, n1, d = sides
+    width = own[0].shape[1] // count
     part = n1.shape[1]
     q_width, half = att.shape[1], part // 2
-
-    def whole(a):
-        shape = a.shape
-        return pl.BlockSpec(shape, lambda i, p: (0,) * len(shape), pipeline_mode=pl.Buffered(1))
-
     by_pair = lambda shape: pl.BlockSpec((2,) + shape, lambda i, p: (i, 0, 0))
-    saved = pl.BlockSpec((ghid.shape[0], 2 * width), lambda i, p: (0, i))
+    saved = lambda a: pl.BlockSpec((a.shape[0], 2 * width), lambda i, p: (0, i))
+    columns = pl.BlockSpec((rows, part), lambda i, p: (0, p[0]), pipeline_mode=pl.Buffered(1))
     shapes = [
         (count, part, width),
         (count, part, width),
@@ -1236,25 +1336,22 @@
         grid_spec=pltpu.PrefetchScalarGridSpec(
             num_scalar_prefetch=1,
             grid=(count // 2,),
-            in_specs=[whole(a) for a in (x, g, wr, att, da, n1, d)]
-            + [saved] * 3
-            + [by_pair((model, width)), by_pair((model, width)), by_pair((width, model))],
+            in_specs=[columns, columns]
+            + [whole_spec(a) for a in sides]
+            + [saved(a) for a in own]
+            + [saved(a) for a in rest],
             out_specs=[by_pair((part, width)), by_pair((part, width)), by_pair((width, part))]
-            + [whole(s) for s in shapes[3:]],
+            + [whole_spec(s) for s in shapes[3:]],
             scratch_shapes=[
-                pltpu.VMEM((rows, 2 * EXTRA), BF16),
                 pltpu.VMEM((part, rows), BF16),
                 pltpu.VMEM((part, rows), BF16),
-                pltpu.VMEM((rows, 2 * width), BF16),
-                pltpu.VMEM((rows, 2 * width), BF16),
-                pltpu.VMEM((rows, 2 * width), BF16),
                 pltpu.VMEM((part, d.shape[1]), F32),
             ],
         ),
         out_shape=shapes,
         compiler_params=pltpu.CompilerParams(vmem_limit_bytes=VMEM_LIMIT),
         name="weight_grads",
-    )(place, x, g, wr, att, da, n1, d, ghid, dgp, dup, w_gate, w_up, w_down)
+    )(place, x, g, *sides, *own, *rest)
 
 
 def rope_rows(length):
@@ -1293,8 +1390,12 @@
     x_all, g_all, n1_cols, moe, back, dgate, gates, ghid, dgp, dup = plane_experts(
         dp, tp, x, g, gz, n1, wr, w_gate, w_up, w_down
     )
-    output, input_grad, att_all, da_cols, d_all, gains = backward(
-        dp, tp, back, moe, dgate, gates, h1, tokens, cotangent, ga, gm, wr, *heads, qkv, att, lse, rope
+    output, input_grad, att_all, da_cols, d_all, gains, *rest = backward(
+        dp,
+        tp,
+        (back, moe, dgate, gates, h1, tokens, cotangent, ga, gm, wr, *heads, qkv, att, lse, rope),
+        (x_all, g_all),
+        (w_gate, w_up, w_down),
     )
     z, core = lax.axis_index("dp"), lax.axis_index("expert")
     place = jnp.stack([z, core]).astype(jnp.int32)
@@ -1302,17 +1403,10 @@
         place,
         x_all,
         g_all,
-        wr,
-        att_all,
-        da_cols,
-        n1_cols,
-        d_all,
-        ghid,
-        dgp,
-        dup,
-        w_gate,
-        w_up,
-        w_down,
+        (att_all, da_cols, n1_cols, d_all),
+        (ghid, dgp, dup),
+        rest,
+        w_gate.shape[0],
         key_projection.shape[1],
         experts,
     )

time: 304 us -> 251 us (0.83)
  Pallas kernels: 288 us -> 235 us
    pallas_call x1, Pallas kernels: 91.8 us -> 28.4 us  [weight_grads(): pl.pallas_call(weights_kernel, grid_spec=pltpu.PrefetchScalarGridSpec(num...]
    pallas_call x1, Pallas kernels: 91.2 us -> 101 us  [backward(): pl.pallas_call(functools.partial(backward_kernel, dp, tp), grid=(count //...]
where the time goes in v3:
time: 251 us; the launch traced here: 250 us
  Pallas kernels  235 us (94%)
  local copies, waits for them, and re-layouts  11.8 us (5%)
    pallas_call x1, Pallas kernels, backward(): pl.pallas_call(functools.partial(backward_kernel, dp, tp), grid=(count //...  101 us
    pallas_call x1, Pallas kernels, plane_experts(): pl.pallas_call(functools.partial(plane_kernel, dp, tp), grid=(count // 2,...  68.9 us
    pallas_call x1, Pallas kernels, forward(): pl.pallas_call(functools.partial(forward_kernel, dp, tp), out_shape=[jax....  36.6 us
    pallas_call x1, Pallas kernels, weight_grads(): pl.pallas_call(weights_kernel, grid_spec=pltpu.PrefetchScalarGridSpec(num...  28.4 us
    unnamed x12, local copies, waits for them, and re-layouts  6.93 us

profile of v3, /device:TPU:0, one launch (start us, length us, event | category | flops | bytes accessed | tf_op | source)
XLA Modules:
  0.0 250.1 jit_solution(1652899892549093350)
XLA Ops:
  0.6 1.5 copy.25.routes_ref
  2.1 1.3 broadcast_in_dim.11.ga_ref
  3.4 1.3 broadcast_in_dim.12.gm_ref
  4.7 0.5 fusion.1
  5.3 0.4 maximum_bitcast_fusion.1
  5.6 0.0 copy-start.2
  5.6 0.8 pad_maximum_fusion.rope_ref
  6.4 36.6 %forward.1 = (bf16[512,1664]{1,0:T(8,128)(2,1)}, bf16[512,1536]{1,0:T(8,128)(2,1)}, bf16[3,64,1536]{2,1,0:T(8,128)(2,1)}, f32[64,1536]{1,0:T(8,128)}, bf16[256,1...) custom-call(bf16[256,1536]{1,0:T(8,128)(2,1)} %tok_ref.3, ...), custom_call_target="tpu_custom_call" | custom-call | tf_op jit(solution)/shard_map/forward/pallas_call | solution.py:601
  43.0 0.0 copy-done.2
  43.0 0.2 copy.26
  43.3 0.8 pad.4.wr_ref
  44.1 68.9 %plane_experts.1 = (bf16[2048,1664]{1,0:T(8,128)(2,1)}, bf16[2048,1536]{1,0:T(8,128)(2,1)}, bf16[2048,384]{1,0:T(8,128)(2,1)}, bf16[512,1536]{1,0:T(8,128)(2,1)}...) custom-call(bf16[512,1664]{1,0:T(8,128)(2,1)} %get-tuple-element.47., ...), custom_call_target="tpu_custom_call" | custom-call | tf_op jit(solution)/shard_map/plane_experts/pallas_call | solution.py:840
  113.0 101.5 %backward.1 = (bf16[256,1536]{1,0:T(8,128)(2,1)}, bf16[256,1536]{1,0:T(8,128)(2,1)}, bf16[2048,384]{1,0:T(8,128)(2,1)}, bf16[2048,384]{1,0:T(8,128)(2,1)}, bf16[...) custom-call(bf16[512,1536]{1,0:T(8,128)(2,1)} %get-tuple-element.51., ...), custom_call_target="tpu_custom_call" | custom-call | tf_op jit(solution)/shard_map/backward/pallas_call | solution.py:1230
  214.5 1.4 fusion.3
  215.9 0.6 pad_add_fusion.place_ref
  216.5 0.0 copy-start.1
  216.5 0.0 copy-start
  216.5 28.4 %weight_grads.1 = (f32[20,384,128]{2,1,0:T(8,128)}, f32[20,384,128]{2,1,0:T(8,128)}, f32[20,128,384]{2,1,0:T(8,128)}, f32[192,384]{1,0:T(8,128)}, f32[192,128]{1...) custom-call(s32[2]{0:T(128)} %pad_add_fusion.place_ref, ...), custom_call_target="tpu_custom_call" | custom-call | tf_op jit(solution)/shard_map/weight_grads/pallas_call | solution.py:1334
  244.9 1.9 copy.27
  246.8 1.6 copy.28
  248.3 0.0 copy-done.1
  248.3 0.9 copy.31
  249.2 0.0 copy-done
  249.2 0.9 copy.32
  (2 shorter events, 0.0 us)
Async XLA Ops:
  5.6 37.4 %copy-start.2 = (bf16[1536,40]{0,1:T(8,128)(2,1)S(1)}, bf16[1536,40]{0,1:T(8,128)(2,1)}, u32[]{:S(2)}) copy-start(bf16[1536,40]{0,1:T(8,128)(2,1)} %param.20) | copy-start | bytes 368644
  216.5 31.9 %copy-start.1 = (bf16[256,1536]{1,0:T(8,128)(2,1)S(1)}, bf16[256,1536]{1,0:T(8,128)(2,1)}, u32[]{:S(2)}) copy-start(bf16[256,1536]{1,0:T(8,128)(2,1)} %get-tuple-element.114) | copy-start | bytes 2359300
  216.5 32.8 %copy-start = (bf16[256,1536]{1,0:T(8,128)(2,1)S(1)}, bf16[256,1536]{1,0:T(8,128)(2,1)}, u32[]{:S(2)}) copy-start(bf16[256,1536]{1,0:T(8,128)(2,1)} %get-tuple-element.115) | copy-start | bytes 2359300

commit v4 on v3

--- a/solution.py
+++ b/solution.py
@@ -3,6 +3,7 @@
 
 import jax
 import jax.numpy as jnp
+import numpy as np
 from jax import lax
 from jax.experimental import pallas as pl
 from jax.experimental.pallas import tpu as pltpu
@@ -421,6 +422,11 @@
 
     def tensor(self, k):
         return (self.z, self.c, lax.rem(self.t + k, self.tp))
+
+    def near(self, axis):
+        row, col = self.t // 2, self.t % 2
+        index = row * 2 + (1 - col) if axis == 0 else (1 - row) * 2 + col
+        return (self.z, self.c, index)
 
     def plane(self, k):
         return (lax.rem(self.z + k, self.dp), self.c, self.t)
@@ -532,7 +538,7 @@
     g_ref[seq_rows, :] = cot_ref[...]
 
     resid = tok_ref[...].astype(F32)
-    n1 = (resid * inverse_rms(resid) * ga_ref[...]).astype(BF16)
+    n1 = (resid * inverse_rms(resid) * ga_ref[...].reshape(1, -1)).astype(BF16)
     n1_ref[...] = n1
     qkv_ref[:, :q_width] = rotate(dot(n1, wq_ref[...]), rope_ref, 1.0).astype(BF16)
     qkv_ref[:, q_width : q_width + kv_width] = rotate(dot(n1, wk_ref[...]), rope_ref, 1.0).astype(BF16)
@@ -572,7 +578,7 @@
     for k in range(1, tp):
         total = total + rs_buf[k - 1].astype(F32)
     h1_ref[...] = total
-    n2 = (total * inverse_rms(total) * gm_ref[...]).astype(BF16)
+    n2 = (total * inverse_rms(total) * gm_ref[...].reshape(1, -1)).astype(BF16)
     mine = ds(c * tp + t, own)
     x_ref[mine, :model] = n2
     x_ref[mine, model:] = jnp.where(chosen, 1.0, 0.0).astype(BF16)
@@ -654,14 +660,12 @@
     x_ref,
     g_ref,
     gz_ref,
-    n1_ref,
     wr_ref,
     wg_ref,
     wu_ref,
     wd_ref,
     xr_ref,
     gr_ref,
-    n1c_ref,
     moe_ref,
     back_ref,
     dgate_ref,
@@ -683,77 +687,65 @@
     length = rows // 2
     own = length // tp
     width = wg_ref.shape[2]
-    part = model // dp
     others = range(1, dp)
-    sides = range(1, tp)
 
     def block(plane, core, tensor):
         return ds((plane * 2 + core) * tp + tensor, own)
 
-    def columns(index):
-        return pl.ds(pl.multiple_of(index * part, 128), part)
+    def link(src, dst, device):
+        return net.make(src, dst, net.number(1), device)
+
+    def start(copies):
+        for copy in copies:
+            copy.start()
 
     mine = ds(c * tp + t, own)
-    x_z = [
-        net.make(x_ref.at[mine], xr_ref.at[block(dp - k, c, t)], net.number(1), net.plane(k))
-        for k in others
-    ]
-    n1_z = [
-        net.make(
-            n1_ref.at[:, columns(lax.rem(z + k, dp))],
-            n1c_ref.at[ds((dp - k) * 2 + c, length)],
-            net.number(1),
-            net.plane(k),
-        )
-        for k in others
-    ]
-    n1_own = net.make(
-        n1_ref.at[:, columns(z)], n1c_ref.at[ds(c, length)], net.number(1), net.partner()
-    )
-    g_t = [
-        net.make(gz_ref.at[p - 1], gr_ref.at[block(p, c, t)], net.number(1), net.tensor(k))
-        for p in others
-        for k in sides
-    ]
-    x_t = [
-        net.make(
-            xr_ref.at[block(p, c, t)], xr_ref.at[block(p, c, t)], net.number(1), net.tensor(k)
-        )
-        for p in others
-        for k in sides
-    ]
-
-    def over(ref):
-        return [
-            net.make(
-                ref.at[ds(p * 2 + c, length)],
-                ref.at[ds(p * 2 + c, length)],
-                net.number(1),
-                net.partner(),
-            )
+    near = [net.near(axis) for axis in range(2)]
+    far = tp - 1 - t
+    half = own // 2
+
+    def piece(plane, tensor, part_of):
+        at = (((plane * 2 + c) * tp + tensor) * 2 + part_of) * half
+        return pl.ds(pl.multiple_of(at, half), half)
+
+    def spread(ref, sources):
+        direct = [
+            link(sources[p - 1], ref.at[block(p, c, t)], near[axis])
             for p in others
+            for axis in range(2)
         ]
-
-    g_c, x_c, n1_c = over(gr_ref), over(xr_ref), over(n1c_ref)
+        relay = []
+        for p in others:
+            for axis in range(2):
+                rows = piece(p, near[axis][2], axis)
+                relay.append(link(ref.at[rows], ref.at[rows], near[1 - axis]))
+        to_core = [link(sources[p - 1], ref.at[block(p, c, t)], net.partner()) for p in others]
+        near_core, far_core = [], []
+        for p in others:
+            for axis in range(2):
+                rows = block(p, c, near[axis][2])
+                near_core.append(link(ref.at[rows], ref.at[rows], net.partner()))
+            rows = block(p, c, far)
+            far_core.append(link(ref.at[rows], ref.at[rows], net.partner()))
+        return direct, relay, to_core, near_core, far_core
+
+    x_z = [link(x_ref.at[mine], xr_ref.at[block(dp - k, c, t)], net.plane(k)) for k in others]
+    g_direct, g_relay, g_core, g_near, g_far = spread(gr_ref, [gz_ref.at[p - 1] for p in others])
+    x_direct, x_relay, x_core, x_near, x_far = spread(
+        xr_ref, [xr_ref.at[block(p, c, t)] for p in others]
+    )
     kept = [
         pltpu.make_async_copy(x_ref, xr_ref.at[pl.ds(0, rows)], keep_sem.at[0]),
         pltpu.make_async_copy(g_ref, gr_ref.at[pl.ds(0, rows)], keep_sem.at[1]),
-        pltpu.make_async_copy(
-            n1_ref.at[:, columns(z)], n1c_ref.at[ds(c, length)], keep_sem.at[2]
-        ),
     ] + [
-        pltpu.make_async_copy(gz_ref.at[p - 1], gr_ref.at[block(p, c, t)], keep_sem.at[2 + p])
+        pltpu.make_async_copy(gz_ref.at[p - 1], gr_ref.at[block(p, c, t)], keep_sem.at[1 + p])
         for p in others
     ]
 
-    def start(copies):
-        for copy in copies:
-            copy.start()
-
     @pl.when(step == 0)
     def _():
         net.greet()
-        start(x_z + g_t + n1_z + [n1_own])
+        start(x_z + g_direct + g_core)
         start(kept)
         moe_acc[...] = jnp.zeros_like(moe_acc)
         back_acc[...] = jnp.zeros_like(back_acc)
@@ -762,22 +754,25 @@
         gates_ref[...] = gates
         store_split(gates, split)
 
-    @pl.when(step == 4)
+    @pl.when(step == 3)
+    def _():
+        arrived(g_direct)
+        start(g_relay + g_near)
+
+    @pl.when(step == 5)
     def _():
         arrived(x_z)
-        start(x_t)
+        start(x_direct + x_core)
 
     @pl.when(step == 6)
     def _():
-        arrived(g_t)
-        for copy in kept:
-            copy.wait()
-        start(g_c)
+        arrived(g_relay)
+        start(g_far)
 
     @pl.when(step == 8)
     def _():
-        arrived(n1_z)
-        start(n1_c)
+        arrived(x_direct)
+        start(x_relay + x_near)
 
     first = c * (2 * pl.num_programs(0)) + 2 * step
     gate_pair = pair_of_gates(split[...], first, width)
@@ -802,21 +797,24 @@
     def _():
         moe_ref[...] = moe_acc[...].astype(BF16)
         back_ref[...] = back_acc[...].astype(BF16)
-        arrived(x_t)
-        start(x_c)
-        arrived(g_c + n1_c + [n1_own])
-        arrived(x_c)
-        for copy in x_z + g_t + n1_z + [n1_own] + x_t + g_c + n1_c + x_c:
+        for copy in kept:
+            copy.wait()
+        arrived(g_core + g_near + g_far + x_core + x_relay)
+        start(x_far)
+        arrived(x_near + x_far)
+        for copy in x_z + g_direct + g_relay + g_core + g_near + g_far:
             copy.wait_send()
-
-
-def plane_experts(dp, tp, x, g, gz, n1, wr, w_gate, w_up, w_down):
+        for copy in x_direct + x_relay + x_core + x_near + x_far:
+            copy.wait_send()
+
+
+def plane_experts(dp, tp, x, g, gz, wr, w_gate, w_up, w_down):
     rows, model = g.shape
     length = rows // 2
     count, _, width = w_gate.shape
     all_rows = rows * dp
-    others, sides = dp - 1, tp - 1
-    copies = 2 * others + 1 + 2 * others * sides + 3 * others
+    others = dp - 1
+    copies = others + 2 * 8 * others
 
     def whole(a):
         shape = a.shape
@@ -827,7 +825,6 @@
     shapes = [
         ((all_rows, x.shape[1]), BF16),
         ((all_rows, model), BF16),
-        ((all_rows, model // dp), BF16),
         ((rows, model), BF16),
         ((rows, model), BF16),
         ((rows, EXTRA), F32),
@@ -841,22 +838,22 @@
         functools.partial(plane_kernel, dp, tp),
         grid=(count // 2,),
         out_shape=shapes,
-        in_specs=[whole(x), whole(g), whole(gz), whole(n1), whole(wr)]
+        in_specs=[whole(x), whole(g), whole(gz), whole(wr)]
         + [by_pair((model, width)), by_pair((model, width)), by_pair((width, model))],
-        out_specs=[ANY, ANY, ANY] + [whole(s) for s in shapes[3:7]] + [saved] * 3,
+        out_specs=[ANY, ANY] + [whole(s) for s in shapes[2:6]] + [saved] * 3,
         scratch_shapes=[
             pltpu.VMEM((rows, 2 * EXTRA), BF16),
             pltpu.VMEM((rows, model), F32),
             pltpu.VMEM((rows, model), F32),
             pltpu.SemaphoreType.DMA((copies,)),
             pltpu.SemaphoreType.DMA((copies,)),
-            pltpu.SemaphoreType.DMA((3 + others,)),
+            pltpu.SemaphoreType.DMA((2 + others,)),
         ],
         compiler_params=pltpu.CompilerParams(
             collective_id=1, has_side_effects=True, vmem_limit_bytes=VMEM_LIMIT
         ),
         name="plane_experts",
-    )(x, g, gz, n1, wr, w_gate, w_up, w_down)
+    )(x, g, gz, wr, w_gate, w_up, w_down)
 
 
 def backward_kernel(
@@ -879,6 +876,7 @@
     qkv_ref,
     att_ref,
     lse_ref,
+    n1_ref,
     rope_ref,
     xr_ref,
     gr_ref,
@@ -887,9 +885,9 @@
     wd_ref,
     out_ref,
     in_ref,
-    att_all,
-    da_cols,
-    d_all,
+    dl_all,
+    qkv_grad_ref,
+    o_grad_ref,
     gains_ref,
     ghid_ref,
     dgp_ref,
@@ -920,6 +918,14 @@
     gain_c,
     out_buf,
     in_buf,
+    q_part,
+    q_pair,
+    q_sum,
+    q_in,
+    o_part,
+    o_pair,
+    o_sum,
+    o_in,
     send_sem,
     recv_sem,
     keep_sem,
@@ -967,26 +973,17 @@
         link(dgate_ref.at[there], pair_d, net.partner()),
     ]
     pair_mo = [link(moe_ref.at[there], pair_m, net.partner())]
-    att_z = over_planes(att_ref, att_all)
-    att_c = on_to_partner(att_all)
-    att_own = [link(att_ref, att_all.at[here], net.partner())]
     side_bd = to_sides(sum_b, rs_b) + to_sides(sum_d, rs_d)
     side_mo = to_sides(sum_m, rs_m)
     share_da = share(da_buf) + share(dl_buf)
-    da_z = [
-        link(
-            da_buf.at[:, columns(lax.rem(z + k, dp))],
-            da_cols.at[ds((dp - k) * 2 + c, length)],
-            net.plane(k),
-        )
-        for k in others
-    ]
-    da_c = on_to_partner(da_cols)
-    da_own = [link(da_buf.at[:, columns(z)], da_cols.at[here], net.partner())]
+    dl_z = over_planes(dl_buf, dl_all)
+    dl_own = [link(dl_buf, dl_all.at[here], net.partner())]
+    dl_c = on_to_partner(dl_all)
+    q_core = [link(q_part.at[:, 1 - c], q_pair, net.partner())]
+    q_z = [link(q_sum.at[lax.rem(z + k, dp)], q_in.at[k - 1], net.plane(k)) for k in others]
+    o_core = [link(o_part.at[:, 1 - c], o_pair, net.partner())]
+    o_z = [link(o_sum.at[lax.rem(z + k, dp)], o_in.at[k - 1], net.plane(k)) for k in others]
     share_out = share(out_buf)
-    d_z = over_planes(d_buf, d_all)
-    d_c = on_to_partner(d_all)
-    d_own = [link(d_buf, d_all.at[here], net.partner())]
     side_3 = to_sides(part_buf, rs_3)
     share_in = share(in_buf)
     side_gain = [link(gain_buf, gain_t.at[k - 1], net.tensor(k)) for k in sides]
@@ -995,21 +992,18 @@
         for k in others
     ]
     pair_gain = [link(gain_c.at[0], gain_c.at[1], net.partner())]
-    keep_att = pltpu.make_async_copy(att_ref, att_all.at[here], keep_sem.at[0])
-    keep_da = pltpu.make_async_copy(da_buf.at[:, columns(z)], da_cols.at[here], keep_sem.at[1])
-    keep_d = pltpu.make_async_copy(d_buf, d_all.at[here], keep_sem.at[2])
+    keep_dl = pltpu.make_async_copy(dl_buf, dl_all.at[here], keep_sem.at[0])
     plane_rows = xr_ref.shape[0] // dp
     rest = pl.ds(plane_rows, xr_ref.shape[0] - plane_rows)
-    load_x = pltpu.make_async_copy(xr_ref.at[rest], x_rest, keep_sem.at[3])
-    load_g = pltpu.make_async_copy(gr_ref.at[rest], g_rest, keep_sem.at[4])
+    load_x = pltpu.make_async_copy(xr_ref.at[rest], x_rest, keep_sem.at[1])
+    load_g = pltpu.make_async_copy(gr_ref.at[rest], g_rest, keep_sem.at[2])
 
     @pl.when(step == 0)
     def _():
         load_x.start()
         load_g.start()
         net.greet()
-        start(pair_bd + pair_mo + att_z + att_own)
-        keep_att.start()
+        start(pair_bd)
         load_x.wait()
         store_split(gates_of(x_rest, wr_ref, model), split)
         load_g.wait()
@@ -1019,7 +1013,16 @@
         arrived(pair_bd)
         sum_b[...] = (back_ref[here, :].astype(F32) + pair_b[...].astype(F32)).astype(BF16)
         sum_d[...] = dgate_ref[here, :] + pair_d[...]
-        start(side_bd)
+        start(side_bd + pair_mo)
+
+    def over_pair(part, pair, total):
+        total[...] = (part[:, c].astype(F32) + pair[...].astype(F32)).astype(BF16)
+
+    def over_z(total, came, out):
+        value = total[z].astype(F32)
+        for k in others:
+            value = value + came[k - 1].astype(F32)
+        out[...] = value
 
     @pl.when(step == 3)
     def _():
@@ -1035,7 +1038,7 @@
         d_n2 = d_n2 + dot_nt(d_logits.astype(BF16), wr_ref[...])
         h1 = h1_ref[...]
         r2 = inverse_rms(h1)
-        weighted = d_n2 * gm_ref[...]
+        weighted = d_n2 * gm_ref[...].reshape(1, -1)
         inner = jnp.mean(weighted * h1, axis=-1, keepdims=True)
         gain_buf[...] = jnp.zeros_like(gain_buf)
         gain_buf[1:2, :] = jnp.sum(d_n2 * h1 * r2, axis=0, keepdims=True)
@@ -1045,27 +1048,23 @@
         start(share_da)
         arrived(pair_mo)
         sum_m[...] = (moe_ref[here, :].astype(F32) + pair_m[...].astype(F32)).astype(BF16)
-        start(side_mo)
-        arrived(att_z)
-        start(att_c)
 
     @pl.when(step == 5)
     def _():
         arrived(share_da)
-        start(da_z + da_own)
-        keep_da.start()
-        d_buf[:, q_width + 2 * kv_width :] = dl_buf[...]
+        start(side_mo + dl_z + dl_own)
+        keep_dl.start()
         do_buf[...] = dot_nt(da_buf[...], wo_ref[...]).astype(BF16)
-        arrived(side_mo)
-        total = h1_ref[...] + sum_m[mine, :].astype(F32)
-        for k in sides:
-            total = total + rs_m[k - 1].astype(F32)
-        out_buf[mine, :] = total.astype(BF16)
-        start(share_out)
+        o_part[...] = dot_tn(da_buf[...], att_ref[...]).astype(BF16).reshape(o_part.shape)
+        start(o_core)
         seen = causal(length)
         scale = HEAD_SIZE ** (-0.5)
         d_key, d_val, d_query = [], [], []
         for kv in range(kv_width // HEAD_SIZE):
+            if kv == 1:
+                arrived(o_core)
+                over_pair(o_part, o_pair, o_sum)
+                start(o_z)
             at_k = q_width + kv * HEAD_SIZE
             at_v = q_width + kv_width + kv * HEAD_SIZE
             key = qkv_ref[:, at_k : at_k + HEAD_SIZE]
@@ -1091,17 +1090,27 @@
         d_buf[:, q_width : q_width + kv_width] = rotate(
             jnp.concatenate(d_key, axis=1), rope_ref, -1.0
         ).astype(BF16)
-        d_buf[:, q_width + kv_width : q_width + 2 * kv_width] = jnp.concatenate(
-            d_val, axis=1
-        ).astype(BF16)
+        d_buf[:, q_width + kv_width :] = jnp.concatenate(d_val, axis=1).astype(BF16)
         part_n1 = dot_nt(d_buf[:, :q_width], wq_ref[...])
         part_n1 = part_n1 + dot_nt(d_buf[:, q_width : q_width + kv_width], wk_ref[...])
-        part_n1 = part_n1 + dot_nt(
-            d_buf[:, q_width + kv_width : q_width + 2 * kv_width], wv_ref[...]
-        )
+        part_n1 = part_n1 + dot_nt(d_buf[:, q_width + kv_width :], wv_ref[...])
         part_buf[...] = part_n1.astype(BF16)
-        start(side_3 + d_z + d_own)
-        keep_d.start()
+        start(side_3)
+        q_part[...] = dot_tn(n1_ref[...], d_buf[...]).astype(BF16).reshape(q_part.shape)
+        start(q_core)
+
+    @pl.when(step == 6)
+    def _():
+        arrived(q_core)
+        over_pair(q_part, q_pair, q_sum)
+        start(q_z)
+        arrived(side_mo)
+        total = h1_ref[...] + sum_m[mine, :].astype(F32)
+        for k in sides:
+            total = total + rs_m[k - 1].astype(F32)
+        out_buf[mine, :] = total.astype(BF16)
+        arrived(dl_z)
+        start(dl_c)
 
     @pl.when(step == 7)
     def _():
@@ -1111,14 +1120,12 @@
             d_n1 = d_n1 + rs_3[k - 1].astype(F32)
         resid = tok_ref[mine, :].astype(F32)
         r1 = inverse_rms(resid)
-        weighted = d_n1 * ga_ref[...]
+        weighted = d_n1 * ga_ref[...].reshape(1, -1)
         inner = jnp.mean(weighted * resid, axis=-1, keepdims=True)
         gain_buf[0:1, :] = jnp.sum(d_n1 * resid * r1, axis=0, keepdims=True)
         d_x = dh1_buf[...] + (r1 * weighted - resid * (r1 * r1 * r1) * inner)
         in_buf[mine, :] = d_x.astype(BF16)
         start(side_gain + share_in)
-        arrived(da_z)
-        start(da_c)
 
     @pl.when(step == 8)
     def _():
@@ -1127,7 +1134,7 @@
         for k in sides:
             gain = gain + gain_t[k - 1]
         gain_zs[...] = gain
-        start(plane_gain)
+        start(plane_gain + share_out)
 
     @pl.when(step == 9)
     def _():
@@ -1152,17 +1159,19 @@
 
     @pl.when(step == last)
     def _():
-        arrived(d_z)
-        start(d_c)
         arrived(pair_gain)
         gains_ref[...] = gain_c[0] + gain_c[1]
-        arrived(share_out + share_in + att_own + da_own + d_own + att_c + da_c + d_c)
+        arrived(o_z)
+        over_z(o_sum, o_in, o_grad_ref)
+        arrived(share_out + share_in)
         out_ref[...] = out_buf[...]
         in_ref[...] = in_buf[...]
-        for copy in (keep_att, keep_da, keep_d):
-            copy.wait()
-        sent = pair_bd + pair_mo + att_z + att_c + att_own + side_bd + side_mo + share_da
-        sent = sent + da_z + da_c + da_own + share_out + d_z + d_c + d_own + side_3 + share_in
+        arrived(q_z)
+        over_z(q_sum, q_in, qkv_grad_ref)
+        arrived(dl_own + dl_c)
+        keep_dl.wait()
+        sent = pair_bd + pair_mo + side_bd + side_mo + share_da + share_out + share_in + side_3
+        sent = sent + dl_z + dl_own + dl_c + q_core + q_z + o_core + o_z
         for copy in sent + side_gain + plane_gain + pair_gain:
             copy.wait_send()
 
@@ -1181,17 +1190,17 @@
     length = tokens.shape[0]
     own, part = length // tp, model // dp
     q_width = wq.shape[1]
-    wide = q_width + wk.shape[1] + wv.shape[1] + EXTRA
+    wide = q_width + wk.shape[1] + wv.shape[1]
     others, sides = dp - 1, tp - 1
-    copies = 3 + 3 * (2 * others + 1) + 9 * sides + sides + others + 1
+    copies = 3 + 9 * sides + (2 * others + 1) + 2 * (1 + others) + sides + others + 1
     by_pair = lambda shape: pl.BlockSpec((2,) + shape, lambda i: (i, 0, 0))
     saved = pl.BlockSpec((rest_rows, 2 * width), lambda i: (0, i))
     shapes = [
         ((length, model), BF16),
         ((length, model), BF16),
-        ((all_rows, q_width), BF16),
-        ((all_rows, part), BF16),
-        ((all_rows, wide), BF16),
+        ((all_rows, EXTRA), BF16),
+        ((part // 2, wide), F32),
+        ((part // 2, q_width), F32),
         ((8, part), F32),
         ((rest_rows, count * width), BF16),
         ((rest_rows, count * width), BF16),
@@ -1226,6 +1235,14 @@
         ((2, 8, part), F32),
         (full, BF16),
         (full, BF16),
+        ((dp, 2, part // 2, wide), BF16),
+        ((dp, part // 2, wide), BF16),
+        ((dp, part // 2, wide), BF16),
+        ((others, part // 2, wide), BF16),
+        ((dp, 2, part // 2, q_width), BF16),
+        ((dp, part // 2, q_width), BF16),
+        ((dp, part // 2, q_width), BF16),
+        ((others, part // 2, q_width), BF16),
     ]
     return pl.pallas_call(
         functools.partial(backward_kernel, dp, tp),
@@ -1234,14 +1251,14 @@
         in_specs=[whole_spec(a) for a in arrays]
         + [ANY, ANY]
         + [by_pair((model, width)), by_pair((model, width)), by_pair((width, model))],
-        out_specs=[whole_spec(shapes[0]), whole_spec(shapes[1]), ANY, ANY, ANY]
-        + [whole_spec(shapes[5])]
+        out_specs=[whole_spec(shapes[0]), whole_spec(shapes[1]), ANY]
+        + [whole_spec(s) for s in shapes[3:6]]
         + [saved] * 3,
         scratch_shapes=[pltpu.VMEM(*s) for s in scratch]
         + [
             pltpu.SemaphoreType.DMA((copies,)),
             pltpu.SemaphoreType.DMA((copies,)),
-            pltpu.SemaphoreType.DMA((5,)),
+            pltpu.SemaphoreType.DMA((3,)),
         ],
         compiler_params=pltpu.CompilerParams(
             collective_id=2, has_side_effects=True, vmem_limit_bytes=VMEM_LIMIT
@@ -1254,10 +1271,12 @@
     place_ref,
     x_ref,
     g_ref,
-    att_ref,
-    da_ref,
-    n1_ref,
-    d_ref,
+    dl_ref,
+    qkv_grad_ref,
+    o_grad_ref,
+    gains_ref,
+    out_in_ref,
+    in_in_ref,
     ghid_ref,
     dgp_ref,
     dup_ref,
@@ -1272,9 +1291,12 @@
     value_ref,
     out_grad_ref,
     router_ref,
+    ga_grad_ref,
+    gm_grad_ref,
+    out_ref,
+    in_ref,
     xt_buf,
     gt_buf,
-    side_buf,
 ):
     step = pl.program_id(0)
     c = place_ref[1]
@@ -1287,16 +1309,17 @@
         gt_buf[...] = g_ref[...].T
         q_width, kv_width = query_ref.shape[1], key_ref.shape[1]
         half = query_ref.shape[0]
-        at = pl.ds(pl.multiple_of(c * half, 8), half)
-        tail = d_ref.shape[1] - EXTRA
-        side_buf[:, :tail] = dot_tn(n1_ref[...], d_ref[:, :tail])
-        side_buf[:, tail:] = dot(xt_buf[...], d_ref[:, tail:])
-        query_ref[...] = side_buf[at, :q_width]
-        key_ref[...] = side_buf[at, q_width : q_width + kv_width]
-        value_ref[...] = side_buf[at, q_width + kv_width : q_width + 2 * kv_width]
-        router_ref[...] = side_buf[at, tail:][:, : router_ref.shape[1]]
-        out_all = dot_tn(att_ref[...], da_ref[...])
-        out_grad_ref[...] = jnp.where(c == 0, out_all[:, :half], out_all[:, half:])
+        query_ref[...] = qkv_grad_ref[:, :q_width]
+        key_ref[...] = qkv_grad_ref[:, q_width : q_width + kv_width]
+        value_ref[...] = qkv_grad_ref[:, q_width + kv_width :]
+        out_grad_ref[...] = o_grad_ref[...]
+        out_ref[...] = out_in_ref[...]
+        in_ref[...] = in_in_ref[...]
+        router = dot(xt_buf[...], dl_ref[...]).T[: router_ref.shape[0]]
+        router_ref[...] = jnp.where(c == 0, router[:, :half], router[:, half:])
+        gains = jnp.where(c == 0, gains_ref[:, :half], gains_ref[:, half:])
+        ga_grad_ref[...] = gains[0:1, :]
+        gm_grad_ref[...] = gains[1:2, :]
 
     def contract(left, own, rest):
         return dot(left[:, :plane_rows], own[...]) + dot(left[:, plane_rows:], rest[...])
@@ -1313,10 +1336,10 @@
 
 def weight_grads(place, x, g, sides, own, rest, count, kv_width, experts):
     rows = x.shape[0]
-    att, _, n1, d = sides
+    _, qkv_grad, o_grad, gains, output, _ = sides
     width = own[0].shape[1] // count
-    part = n1.shape[1]
-    q_width, half = att.shape[1], part // 2
+    part = gains.shape[1]
+    q_width, half = o_grad.shape[1], part // 2
     by_pair = lambda shape: pl.BlockSpec((2,) + shape, lambda i, p: (i, 0, 0))
     saved = lambda a: pl.BlockSpec((a.shape[0], 2 * width), lambda i, p: (0, i))
     columns = pl.BlockSpec((rows, part), lambda i, p: (0, p[0]), pipeline_mode=pl.Buffered(1))
@@ -1327,10 +1350,13 @@
         (half, q_width),
         (half, kv_width),
         (half, kv_width),
-        (q_width, half),
-        (half, experts),
+        (half, q_width),
+        (experts, half),
+        (1, half),
+        (1, half),
     ]
     shapes = [jax.ShapeDtypeStruct(s, F32) for s in shapes]
+    shapes += [jax.ShapeDtypeStruct(output.shape, BF16)] * 2
     return pl.pallas_call(
         weights_kernel,
         grid_spec=pltpu.PrefetchScalarGridSpec(
@@ -1342,11 +1368,7 @@
             + [saved(a) for a in rest],
             out_specs=[by_pair((part, width)), by_pair((part, width)), by_pair((width, part))]
             + [whole_spec(s) for s in shapes[3:]],
-            scratch_shapes=[
-                pltpu.VMEM((part, rows), BF16),
-                pltpu.VMEM((part, rows), BF16),
-                pltpu.VMEM((part, d.shape[1]), F32),
-            ],
+            scratch_shapes=[pltpu.VMEM((part, rows), BF16), pltpu.VMEM((part, rows), BF16)],
         ),
         out_shape=shapes,
         compiler_params=pltpu.CompilerParams(vmem_limit_bytes=VMEM_LIMIT),
@@ -1355,11 +1377,12 @@
 
 
 def rope_rows(length):
-    positions = jnp.arange(length, dtype=F32)
-    cos, sin = rope_tables(positions, HEAD_SIZE)
-    none = jnp.zeros_like(sin)
-    double = lambda first, second: jnp.concatenate([first, second, first, second], axis=1)
-    return jnp.stack([double(cos, cos), double(-sin, none), double(none, sin)])
+    half = HEAD_SIZE // 2
+    frequency = ROPE_BASE ** (np.arange(half) * (-2.0 / HEAD_SIZE))
+    angles = np.arange(length)[:, None] * frequency[None, :]
+    cos, sin, none = np.cos(angles), np.sin(angles), np.zeros((length, half))
+    double = lambda first, second: np.concatenate([first, second, first, second], axis=1)
+    return np.stack([double(cos, cos), double(-sin, none), double(none, sin)]).astype(np.float32)
 
 
 def gather_plan(
@@ -1379,48 +1402,55 @@
 ):
     dp, tp = lax.axis_size("dp"), lax.axis_size("tensor")
     experts = w_router.shape[1]
-    half = tokens.shape[1] // dp // 2
-    rope = rope_rows(tokens.shape[0])
-    ga, gm = gain_attn[None, :], gain_moe[None, :]
+    rope = jnp.asarray(rope_rows(tokens.shape[0]))
+    ga, gm = gain_attn, gain_moe
     wr = jnp.pad(w_router, ((0, 0), (0, EXTRA - experts)))
     heads = (w_query, key_projection, value_projection, w_out)
     x, g, gz, h1, n1, qkv, att, lse = forward(
         dp, tp, tokens, cotangent, routes, ga, gm, *heads, rope
     )
-    x_all, g_all, n1_cols, moe, back, dgate, gates, ghid, dgp, dup = plane_experts(
-        dp, tp, x, g, gz, n1, wr, w_gate, w_up, w_down
-    )
-    output, input_grad, att_all, da_cols, d_all, gains, *rest = backward(
-        dp,
-        tp,
-        (back, moe, dgate, gates, h1, tokens, cotangent, ga, gm, wr, *heads, qkv, att, lse, rope),
-        (x_all, g_all),
-        (w_gate, w_up, w_down),
-    )
-    z, core = lax.axis_index("dp"), lax.axis_index("expert")
-    place = jnp.stack([z, core]).astype(jnp.int32)
-    gate_grad, up_grad, down_grad, query_grad, key_grad, value_grad, out_grad, router_grad = weight_grads(
+    x_all, g_all, moe, back, dgate, gates, ghid, dgp, dup = plane_experts(
+        dp, tp, x, g, gz, wr, w_gate, w_up, w_down
+    )
+    local = (back, moe, dgate, gates, h1, tokens, cotangent, ga, gm, wr, *heads)
+    output, input_grad, d_logits, qkv_grad, o_grad, gains, *rest = backward(
+        dp, tp, (*local, qkv, att, lse, n1, rope), (x_all, g_all), (w_gate, w_up, w_down)
+    )
+    place = jnp.stack([lax.axis_index("dp"), lax.axis_index("expert")]).astype(jnp.int32)
+    (
+        gate_grad,
+        up_grad,
+        down_grad,
+        query_grad,
+        key_grad,
+        value_grad,
+        out_grad,
+        router_grad,
+        gain_attn_grad,
+        gain_moe_grad,
+        output,
+        input_grad,
+    ) = weight_grads(
         place,
         x_all,
         g_all,
-        (att_all, da_cols, n1_cols, d_all),
+        (d_logits, qkv_grad, o_grad, gains, output, input_grad),
         (ghid, dgp, dup),
         rest,
         w_gate.shape[0],
         key_projection.shape[1],
         experts,
     )
-    gains = lax.dynamic_slice_in_dim(gains, core * half, half, axis=1)
     return (
         output,
         input_grad,
-        gains[0],
+        gain_attn_grad[0],
         query_grad,
         key_grad,
         value_grad,
-        out_grad,
-        gains[1],
-        router_grad,
+        out_grad.T,
+        gain_moe_grad[0],
+        router_grad.T,
         gate_grad,
         up_grad,
         down_grad,
@@ -1445,7 +1475,7 @@
     )
     sequences = mesh.shape["dp"] * mesh.shape["expert"]
     few = sequences * SEQUENCE_LENGTH <= GATHER_ROWS
-    few = few and mesh.shape["tensor"] > 1 and mesh.shape["expert"] == 2
+    few = few and mesh.shape["tensor"] == 4 and mesh.shape["expert"] == 2
     return jax.shard_map(
         gather_plan if few else reduce_plan,
         mesh=mesh,

time: 251 us -> 212 us (0.84)
  Pallas kernels: 235 us -> 207 us
  local copies, waits for them, and re-layouts: 11.8 us -> 3.43 us
    pallas_call x1, Pallas kernels: 101 us -> 87.9 us  [backward(): pl.pallas_call(functools.partial(backward_kernel, dp, tp), grid=(count //...]
    pallas_call x1, Pallas kernels: 68.9 us -> 56.9 us  [plane_experts(): pl.pallas_call(functools.partial(plane_kernel, dp, tp), grid=(count // 2,...]
    unnamed x12 -> x2, local copies, waits for them, and re-layouts: 6.93 us -> 2.61 us
    pallas_call x1, Pallas kernels: 28.4 us -> 25.7 us  [weight_grads(): pl.pallas_call(weights_kernel, grid_spec=pltpu.PrefetchScalarGridSpec(num...]
    broadcast_in_dim x3 -> x0, local copies, waits for them, and re-layouts: 2.6 us -> none  [the longest x2 2.59 us: gather_plan(): ga, gm = (gain_attn[None, :], gain_moe[None, :])]
where the time goes in v4:
time: 212 us
  Pallas kernels  207 us (98%)
  local copies, waits for them, and re-layouts  3.43 us (2%)
    pallas_call x1, Pallas kernels, backward(): pl.pallas_call(functools.partial(backward_kernel, dp, tp), grid=(count //...  87.9 us
    pallas_call x1, Pallas kernels, plane_experts(): pl.pallas_call(functools.partial(plane_kernel, dp, tp), grid=(count // 2,...  56.9 us
    pallas_call x1, Pallas kernels, forward(): pl.pallas_call(functools.partial(forward_kernel, dp, tp), out_shape=[jax....  36.6 us
    pallas_call x1, Pallas kernels, weight_grads(): pl.pallas_call(weights_kernel, grid_spec=pltpu.PrefetchScalarGridSpec(num...  25.7 us

profile of v4, /device:TPU:0, one launch (start us, length us, event | category | flops | bytes accessed | tf_op | source)
XLA Modules:
  0.0 211.9 jit_solution(14459522972291343866)
XLA Ops:
  0.6 0.6 pad_add_fusion.place_ref
  1.3 1.5 copy.26.routes_ref
  2.7 1.1 copy.27
  3.9 0.8 pad.4.wr_ref
  4.7 36.6 %forward.1 = (bf16[512,1664]{1,0:T(8,128)(2,1)}, bf16[512,1536]{1,0:T(8,128)(2,1)}, bf16[3,64,1536]{2,1,0:T(8,128)(2,1)}, f32[64,1536]{1,0:T(8,128)}, bf16[256,1...) custom-call(bf16[256,1536]{1,0:T(8,128)(2,1)} %tok_ref.3, ...), custom_call_target="tpu_custom_call" | custom-call | tf_op jit(solution)/shard_map/forward/pallas_call | solution.py:607
  41.3 56.9 %plane_experts.1 = (bf16[2048,1664]{1,0:T(8,128)(2,1)}, bf16[2048,1536]{1,0:T(8,128)(2,1)}, bf16[512,1536]{1,0:T(8,128)(2,1)}, bf16[512,1536]{1,0:T(8,128)(2,1)}...) custom-call(bf16[512,1664]{1,0:T(8,128)(2,1)} %get-tuple-element.50., ...), custom_call_target="tpu_custom_call" | custom-call | tf_op jit(solution)/shard_map/plane_experts/pallas_call | solution.py:837
  98.2 87.9 %backward.1 = (bf16[256,1536]{1,0:T(8,128)(2,1)}, bf16[256,1536]{1,0:T(8,128)(2,1)}, bf16[2048,128]{1,0:T(8,128)(2,1)}, f32[192,640]{1,0:T(8,128)}, f32[192,384]...) custom-call(bf16[512,1536]{1,0:T(8,128)(2,1)} %get-tuple-element.55., ...), custom_call_target="tpu_custom_call" | custom-call | tf_op jit(solution)/shard_map/backward/pallas_call | solution.py:1247
  186.1 25.7 %weight_grads.1 = (f32[20,384,128]{2,1,0:T(8,128)}, f32[20,384,128]{2,1,0:T(8,128)}, f32[20,128,384]{2,1,0:T(8,128)}, f32[192,384]{1,0:T(8,128)}, f32[192,128]{1...) custom-call(s32[2]{0:T(128)} %pad_add_fusion.place_ref, ...), custom_call_target="tpu_custom_call" | custom-call | tf_op jit(solution)/shard_map/weight_grads/pallas_call | solution.py:1360

commit v5 on v4

--- a/solution.py
+++ b/solution.py
@@ -498,130 +498,6 @@
     return col <= row
 
 
-def forward_kernel(
-    dp,
-    tp,
-    tok_ref,
-    cot_ref,
-    routes_ref,
-    ga_ref,
-    gm_ref,
-    wq_ref,
-    wk_ref,
-    wv_ref,
-    wo_ref,
-    rope_ref,
-    x_ref,
-    g_ref,
-    gz_ref,
-    h1_ref,
-    n1_ref,
-    qkv_ref,
-    att_ref,
-    lse_ref,
-    part_buf,
-    rs_buf,
-    send_sem,
-    recv_sem,
-):
-    net = Peers(dp, tp, send_sem, recv_sem)
-    z, c, t = net.z, net.c, net.t
-    length, model = tok_ref.shape
-    own = length // tp
-    q_width, kv_width = wq_ref.shape[1], wk_ref.shape[1]
-    group = q_width // kv_width
-    net.greet()
-    seq_rows = ds(c, length)
-    got_g = [net.to(cot_ref, g_ref.at[seq_rows], net.partner())]
-    for k in range(1, dp):
-        got_g.append(net.to(cot_ref.at[ds(t, own)], gz_ref.at[dp - 1 - k], net.plane(k)))
-    g_ref[seq_rows, :] = cot_ref[...]
-
-    resid = tok_ref[...].astype(F32)
-    n1 = (resid * inverse_rms(resid) * ga_ref[...].reshape(1, -1)).astype(BF16)
-    n1_ref[...] = n1
-    qkv_ref[:, :q_width] = rotate(dot(n1, wq_ref[...]), rope_ref, 1.0).astype(BF16)
-    qkv_ref[:, q_width : q_width + kv_width] = rotate(dot(n1, wk_ref[...]), rope_ref, 1.0).astype(BF16)
-    qkv_ref[:, q_width + kv_width :] = dot(n1, wv_ref[...]).astype(BF16)
-
-    seen = causal(length)
-    lane = lax.broadcasted_iota(jnp.int32, lse_ref.shape, 1)
-    lse_all = jnp.zeros(lse_ref.shape, F32)
-    scale = HEAD_SIZE ** (-0.5)
-    for h in range(q_width // HEAD_SIZE):
-        kv = h // group
-        at_k = q_width + kv * HEAD_SIZE
-        at_v = q_width + kv_width + kv * HEAD_SIZE
-        q = qkv_ref[:, h * HEAD_SIZE : (h + 1) * HEAD_SIZE]
-        key = qkv_ref[:, at_k : at_k + HEAD_SIZE]
-        val = qkv_ref[:, at_v : at_v + HEAD_SIZE]
-        s = jnp.where(seen, dot_nt(q, key) * scale, -1e30)
-        top = jnp.max(s, axis=-1, keepdims=True)
-        lse = top + jnp.log(jnp.sum(jnp.exp(s - top), axis=-1, keepdims=True))
-        prob = jnp.exp(s - lse).astype(BF16)
-        att_ref[:, h * HEAD_SIZE : (h + 1) * HEAD_SIZE] = dot(prob, val).astype(BF16)
-        lse_all = jnp.where(lane == h, lse, lse_all)
-    lse_ref[...] = lse_all
-    part_buf[...] = dot(att_ref[...], wo_ref[...]).astype(BF16)
-
-    got = []
-    for k in range(1, tp):
-        block = part_buf.at[ds(lax.rem(t + k, tp), own)]
-        got.append(net.to(block, rs_buf.at[k - 1], net.tensor(k)))
-    total = tok_ref[ds(t, own), :].astype(F32) + part_buf[ds(t, own), :].astype(F32)
-    picked = routes_ref[ds(t, own), :]
-    ids = lax.broadcasted_iota(jnp.int32, (own, EXTRA), 1)
-    chosen = picked[:, 0:1] == ids
-    for j in range(1, picked.shape[1]):
-        chosen = chosen | (picked[:, j : j + 1] == ids)
-    arrived(got)
-    for k in range(1, tp):
-        total = total + rs_buf[k - 1].astype(F32)
-    h1_ref[...] = total
-    n2 = (total * inverse_rms(total) * gm_ref[...].reshape(1, -1)).astype(BF16)
-    mine = ds(c * tp + t, own)
-    x_ref[mine, :model] = n2
-    x_ref[mine, model:] = jnp.where(chosen, 1.0, 0.0).astype(BF16)
-    got = [net.to(x_ref.at[mine], x_ref.at[mine], net.tensor(k)) for k in range(1, tp)]
-    arrived(got)
-    got = [net.to(x_ref.at[seq_rows], x_ref.at[seq_rows], net.partner())]
-    arrived(got_g + got)
-    net.drain()
-
-
-def forward(dp, tp, tokens, cotangent, routes, ga, gm, wq, wk, wv, wo, rope):
-    length, model = tokens.shape
-    own, wide = length // tp, model + EXTRA
-    widths = wq.shape[1] + wk.shape[1] + wv.shape[1]
-    copies = 2 + (dp - 1) + 2 * (tp - 1)
-    shapes = [
-        ((2 * length, wide), BF16),
-        ((2 * length, model), BF16),
-        ((dp - 1, own, model), BF16),
-        ((own, model), F32),
-        ((length, model), BF16),
-        ((length, widths), BF16),
-        ((length, wq.shape[1]), BF16),
-        ((length, 128), F32),
-    ]
-    return pl.pallas_call(
-        functools.partial(forward_kernel, dp, tp),
-        out_shape=[jax.ShapeDtypeStruct(*s) for s in shapes],
-        in_specs=[VMEM] * 10,
-        out_specs=[VMEM] * len(shapes),
-        scratch_shapes=[
-            pltpu.VMEM((length, model), BF16),
-            pltpu.VMEM((tp - 1, own, model), BF16),
-            pltpu.SemaphoreType.DMA((copies,)),
-            pltpu.SemaphoreType.DMA((copies,)),
-        ],
-        compiler_params=pltpu.CompilerParams(
-            collective_id=0, has_side_effects=True, vmem_limit_bytes=VMEM_LIMIT
-        ),
-        name="forward",
-    )(tokens, cotangent, routes, ga, gm, wq, wk, wv, wo, rope)
-
-
 def gates_of(x_ref, wr_ref, model):
     logits = dot(x_ref[:, :model], wr_ref[...])
     chosen = x_ref[:, model:].astype(F32) > 0.5
@@ -654,13 +530,20 @@
     return hid, (hid * gate).astype(BF16), d_gate.astype(BF16), (d_hid * act).astype(BF16)
 
 
-def plane_kernel(
+def front_kernel(
     dp,
     tp,
-    x_ref,
-    g_ref,
-    gz_ref,
+    tok_ref,
+    cot_ref,
+    routes_ref,
+    ga_ref,
+    gm_ref,
     wr_ref,
+    wq_ref,
+    wk_ref,
+    wv_ref,
+    wo_ref,
+    rope_ref,
     wg_ref,
     wu_ref,
     wd_ref,
@@ -670,9 +553,22 @@
     back_ref,
     dgate_ref,
     gates_ref,
+    h1_ref,
+    qkv_ref,
+    att_ref,
+    prob_ref,
+    prob_t_ref,
+    n1t_ref,
     ghid_ref,
     dgp_ref,
     dup_ref,
+    x_buf,
+    g_buf,
+    gz_buf,
+    n1_buf,
+    part_buf,
+    rs_buf,
+    dh_buf,
     split,
     moe_acc,
     back_acc,
@@ -681,13 +577,16 @@
     keep_sem,
 ):
     step, last = pl.program_id(0), pl.num_programs(0) - 1
+    pairs = pl.num_programs(0) // 2
     net = Peers(dp, tp, send_sem, recv_sem)
     z, c, t = net.z, net.c, net.t
-    rows, model = g_ref.shape
-    length = rows // 2
+    length, model = tok_ref.shape
+    rows = 2 * length
     own = length // tp
     width = wg_ref.shape[2]
-    others = range(1, dp)
+    q_width, kv_width = wq_ref.shape[1], wk_ref.shape[1]
+    group = q_width // kv_width
+    others, sides = range(1, dp), range(1, tp)
 
     def block(plane, core, tensor):
         return ds((plane * 2 + core) * tp + tensor, own)
@@ -700,6 +599,7 @@
             copy.start()
 
     mine = ds(c * tp + t, own)
+    seq_rows = ds(c, length)
     near = [net.near(axis) for axis in range(2)]
     far = tp - 1 - t
     half = own // 2
@@ -708,176 +608,270 @@
         at = (((plane * 2 + c) * tp + tensor) * 2 + part_of) * half
         return pl.ds(pl.multiple_of(at, half), half)
 
-    def spread(ref, sources):
+    def spread(ref, sources, relayed):
         direct = [
             link(sources[p - 1], ref.at[block(p, c, t)], near[axis])
             for p in others
             for axis in range(2)
         ]
         relay = []
-        for p in others:
+        for p in others if relayed else ():
             for axis in range(2):
-                rows = piece(p, near[axis][2], axis)
-                relay.append(link(ref.at[rows], ref.at[rows], near[1 - axis]))
+                at = piece(p, near[axis][2], axis)
+                relay.append(link(ref.at[at], ref.at[at], near[1 - axis]))
         to_core = [link(sources[p - 1], ref.at[block(p, c, t)], net.partner()) for p in others]
         near_core, far_core = [], []
         for p in others:
             for axis in range(2):
-                rows = block(p, c, near[axis][2])
-                near_core.append(link(ref.at[rows], ref.at[rows], net.partner()))
-            rows = block(p, c, far)
-            far_core.append(link(ref.at[rows], ref.at[rows], net.partner()))
+                at = block(p, c, near[axis][2])
+                near_core.append(link(ref.at[at], ref.at[at], net.partner()))
+            at = block(p, c, far)
+            far_core.append(link(ref.at[at], ref.at[at], net.partner()))
         return direct, relay, to_core, near_core, far_core
 
-    x_z = [link(x_ref.at[mine], xr_ref.at[block(dp - k, c, t)], net.plane(k)) for k in others]
-    g_direct, g_relay, g_core, g_near, g_far = spread(gr_ref, [gz_ref.at[p - 1] for p in others])
-    x_direct, x_relay, x_core, x_near, x_far = spread(
-        xr_ref, [xr_ref.at[block(p, c, t)] for p in others]
-    )
-    kept = [
-        pltpu.make_async_copy(x_ref, xr_ref.at[pl.ds(0, rows)], keep_sem.at[0]),
-        pltpu.make_async_copy(g_ref, gr_ref.at[pl.ds(0, rows)], keep_sem.at[1]),
-    ] + [
-        pltpu.make_async_copy(gz_ref.at[p - 1], gr_ref.at[block(p, c, t)], keep_sem.at[1 + p])
+    g_own = [link(cot_ref, g_buf.at[seq_rows], net.partner())]
+    g_z = [link(cot_ref.at[ds(t, own)], gz_buf.at[dp - 1 - k], net.plane(k)) for k in others]
+    side_h = [
+        link(part_buf.at[ds(lax.rem(t + k, tp), own)], rs_buf.at[k - 1], net.tensor(k))
+        for k in sides
+    ]
+    x_t = [link(x_buf.at[mine], x_buf.at[mine], net.tensor(k)) for k in sides]
+    x_own = [link(x_buf.at[mine], x_buf.at[mine], net.partner())]
+    x_seen = []
+    for k in sides:
+        at = ds(c * tp + lax.rem(t + tp - k, tp), own)
+        x_seen.append(link(x_buf.at[at], x_buf.at[at], net.partner()))
+    x_z = [link(x_buf.at[mine], xr_ref.at[block(dp - k, c, t)], net.plane(k)) for k in others]
+    g_direct, g_relay, g_core, g_near, g_far = spread(
+        gr_ref, [gz_buf.at[p - 1] for p in others], True
+    )
+    x_direct, _, x_core, x_near, x_far = spread(
+        xr_ref, [xr_ref.at[block(p, c, t)] for p in others], False
+    )
+    x_z2 = [
+        link(x_buf.at[ds(c * tp + far, own)], xr_ref.at[block(dp - k, c, far)], net.plane(k))
+        for k in others
+    ]
+    keep_x = pltpu.make_async_copy(x_buf, xr_ref.at[pl.ds(0, rows)], keep_sem.at[0])
+    keep_g = [pltpu.make_async_copy(g_buf, gr_ref.at[pl.ds(0, rows)], keep_sem.at[1])] + [
+        pltpu.make_async_copy(gz_buf.at[p - 1], gr_ref.at[block(p, c, t)], keep_sem.at[1 + p])
         for p in others
     ]
 
     @pl.when(step == 0)
     def _():
         net.greet()
-        start(x_z + g_direct + g_core)
-        start(kept)
+        start(g_own + g_z)
+        g_buf[seq_rows, :] = cot_ref[...]
+        resid = tok_ref[...].astype(F32)
+        n1 = (resid * inverse_rms(resid) * ga_ref[...].reshape(1, -1)).astype(BF16)
+        n1_buf[...] = n1
+        qkv_ref[:, :q_width] = rotate(dot(n1, wq_ref[...]), rope_ref, 1.0).astype(BF16)
+        qkv_ref[:, q_width : q_width + kv_width] = rotate(
+            dot(n1, wk_ref[...]), rope_ref, 1.0
+        ).astype(BF16)
+        qkv_ref[:, q_width + kv_width :] = dot(n1, wv_ref[...]).astype(BF16)
+        seen = causal(length)
+        scale = HEAD_SIZE ** (-0.5)
+        for h in range(q_width // HEAD_SIZE):
+            kv = h // group
+            at_k = q_width + kv * HEAD_SIZE
+            at_v = q_width + kv_width + kv * HEAD_SIZE
+            q = qkv_ref[:, h * HEAD_SIZE : (h + 1) * HEAD_SIZE]
+            key = qkv_ref[:, at_k : at_k + HEAD_SIZE]
+            val = qkv_ref[:, at_v : at_v + HEAD_SIZE]
+            s = jnp.where(seen, dot_nt(q, key) * scale, -1e30)
+            top = jnp.max(s, axis=-1, keepdims=True)
+            lse = top + jnp.log(jnp.sum(jnp.exp(s - top), axis=-1, keepdims=True))
+            prob = jnp.exp(s - lse).astype(BF16)
+            prob_ref[h] = prob
+            att_ref[:, h * HEAD_SIZE : (h + 1) * HEAD_SIZE] = dot(prob, val).astype(BF16)
+        part_buf[...] = dot(att_ref[...], wo_ref[...]).astype(BF16)
+        start(side_h)
         moe_acc[...] = jnp.zeros_like(moe_acc)
         back_acc[...] = jnp.zeros_like(back_acc)
         dgate_ref[...] = jnp.zeros_like(dgate_ref)
-        gates = gates_of(x_ref, wr_ref, model)
+        arrived(g_own)
+
+    @pl.when(step < pairs)
+    def _():
+        dh_buf[step] = dot_nt(g_buf[...], wd_ref[...].reshape(2 * width, model))
+
+    @pl.when(step == pairs)
+    def _():
+        total = tok_ref[ds(t, own), :].astype(F32) + part_buf[ds(t, own), :].astype(F32)
+        picked = routes_ref[ds(t, own), :]
+        ids = lax.broadcasted_iota(jnp.int32, (own, EXTRA), 1)
+        chosen = picked[:, 0:1] == ids
+        for j in range(1, picked.shape[1]):
+            chosen = chosen | (picked[:, j : j + 1] == ids)
+        arrived(side_h)
+        for k in sides:
+            total = total + rs_buf[k - 1].astype(F32)
+        n2 = (total * inverse_rms(total) * gm_ref[...].reshape(1, -1)).astype(BF16)
+        x_buf[mine, :model] = n2
+        x_buf[mine, model:] = jnp.where(chosen, 1.0, 0.0).astype(BF16)
+        start(x_t + x_own + x_z)
+        h1_ref[...] = total
+        for h in range(q_width // HEAD_SIZE):
+            prob_t_ref[h] = prob_ref[h].T
+        n1t_ref[...] = n1_buf[...].T
+        for k in sides:
+            arrived(x_t[k - 1 : k])
+            start(x_seen[k - 1 : k])
+        arrived(g_z)
+        start(g_direct + g_core + keep_g)
+        arrived(x_own + x_seen)
+        keep_x.start()
+        gates = gates_of(x_buf, wr_ref, model)
         gates_ref[...] = gates
         store_split(gates, split)
 
-    @pl.when(step == 3)
+    @pl.when(step == pairs + 3)
+    def _():
+        arrived(x_z)
+        start(x_direct + x_core + x_z2)
+
+    @pl.when(step == pairs + 6)
     def _():
         arrived(g_direct)
         start(g_relay + g_near)
 
-    @pl.when(step == 5)
-    def _():
-        arrived(x_z)
-        start(x_direct + x_core)
-
-    @pl.when(step == 6)
+    @pl.when(step == pairs + 9)
     def _():
         arrived(g_relay)
         start(g_far)
-
-    @pl.when(step == 8)
-    def _():
         arrived(x_direct)
-        start(x_relay + x_near)
-
-    first = c * (2 * pl.num_programs(0)) + 2 * step
-    gate_pair = pair_of_gates(split[...], first, width)
-    wd_pair = wd_ref[...].reshape(2 * width, model)
-    dh_pair = dot_nt(g_ref[...], wd_pair)
-    lane = lax.broadcasted_iota(jnp.int32, dgate_ref.shape, 1)
-    for k in range(2):
-        lanes = slice(k * width, (k + 1) * width)
-        w_both = jnp.concatenate([wg_ref[k], wu_ref[k]], axis=1)
-        both = dot(x_ref[:, :model], w_both)
-        dh = dh_pair[:, lanes]
-        hid, ghid, dgp, dup = swiglu(both, dh, gate_pair[:, lanes])
-        ghid_ref[:, lanes] = ghid
-        dgp_ref[:, lanes] = dgp
-        dup_ref[:, lanes] = dup
-        row_sum = jnp.sum(hid * dh, axis=1, keepdims=True)
-        dgate_ref[...] += jnp.where(lane == first + k, row_sum, 0.0)
-        back_acc[...] += dot_nt(jnp.concatenate([dgp, dup], axis=1), w_both)
-    moe_acc[...] += dot(ghid_ref[...], wd_pair)
+        start(x_near)
+        arrived(x_z2)
+        start(x_far)
+
+    @pl.when(step >= pairs)
+    def _():
+        pair = step - pairs
+        first = c * (2 * pairs) + 2 * pair
+        gate_pair = pair_of_gates(split[...], first, width)
+        lane = lax.broadcasted_iota(jnp.int32, dgate_ref.shape, 1)
+        for k in range(2):
+            lanes = slice(k * width, (k + 1) * width)
+            w_both = jnp.concatenate([wg_ref[k], wu_ref[k]], axis=1)
+            both = dot(x_buf[:, :model], w_both)
+            dh = dh_buf[pair, :, lanes]
+            hid, ghid, dgp, dup = swiglu(both, dh, gate_pair[:, lanes])
+            ghid_ref[:, lanes] = ghid
+            dgp_ref[:, lanes] = dgp
+            dup_ref[:, lanes] = dup
+            row_sum = jnp.sum(hid * dh, axis=1, keepdims=True)
+            dgate_ref[...] += jnp.where(lane == first + k, row_sum, 0.0)
+            back_acc[...] += dot_nt(jnp.concatenate([dgp, dup], axis=1), w_both)
+        moe_acc[...] += dot(ghid_ref[...], wd_ref[...].reshape(2 * width, model))
 
     @pl.when(step == last)
     def _():
         moe_ref[...] = moe_acc[...].astype(BF16)
         back_ref[...] = back_acc[...].astype(BF16)
-        for copy in kept:
+        keep_x.wait()
+        for copy in keep_g:
             copy.wait()
-        arrived(g_core + g_near + g_far + x_core + x_relay)
-        start(x_far)
-        arrived(x_near + x_far)
-        for copy in x_z + g_direct + g_relay + g_core + g_near + g_far:
+        arrived(g_core + g_near + g_far + x_core + x_near + x_far)
+        sent = g_own + g_z + side_h + x_t + x_own + x_seen + x_z
+        sent = sent + g_direct + g_relay + g_core + g_near + g_far
+        for copy in sent + x_direct + x_z2 + x_core + x_near + x_far:
             copy.wait_send()
-        for copy in x_direct + x_relay + x_core + x_near + x_far:
-            copy.wait_send()
-
-
-def plane_experts(dp, tp, x, g, gz, wr, w_gate, w_up, w_down):
-    rows, model = g.shape
-    length = rows // 2
-    count, _, width = w_gate.shape
-    all_rows = rows * dp
-    others = dp - 1
-    copies = others + 2 * 8 * others
-
-    def whole(a):
-        shape = a.shape
-        return pl.BlockSpec(shape, lambda i: (0,) * len(shape), pipeline_mode=pl.Buffered(1))
-
-    by_pair = lambda shape: pl.BlockSpec((2,) + shape, lambda i: (i, 0, 0))
-    saved = pl.BlockSpec((rows, 2 * width), lambda i: (0, i))
+
+
+def whole_spec(a):
+    shape = a.shape
+    return pl.BlockSpec(shape, lambda *_: (0,) * len(shape), pipeline_mode=pl.Buffered(1))
+
+
+def front(dp, tp, arrays, weights):
+    tokens, wq, wk, wv = arrays[0], *arrays[6:9]
+    length, model = tokens.shape
+    count, _, width = weights[0].shape
+    pairs = count // 2
+    rows, own = 2 * length, length // tp
+    heads, wide = wq.shape[1] // HEAD_SIZE, model + EXTRA
+    q_width = wq.shape[1]
+    widths = q_width + wk.shape[1] + wv.shape[1]
+    others, sides = dp - 1, tp - 1
+    copies = 1 + others + sides + sides + 1 + sides + 2 * others + (8 + 6) * others
+    later = lambda i: jnp.maximum(i - pairs, 0)
+    up = lambda shape: pl.BlockSpec((2,) + shape, lambda i: (later(i), 0, 0))
+    down = pl.BlockSpec((2, width, model), lambda i: (lax.rem(i, pairs), 0, 0))
+    saved = pl.BlockSpec((rows, 2 * width), lambda i: (0, later(i)))
     shapes = [
-        ((all_rows, x.shape[1]), BF16),
-        ((all_rows, model), BF16),
+        ((rows * dp, wide), BF16),
+        ((rows * dp, model), BF16),
         ((rows, model), BF16),
         ((rows, model), BF16),
         ((rows, EXTRA), F32),
         ((rows, EXTRA), F32),
+        ((own, model), F32),
+        ((length, widths), BF16),
+        ((length, q_width), BF16),
+        ((heads, length, length), BF16),
+        ((heads, length, length), BF16),
+        ((model, length), BF16),
         ((rows, count * width), BF16),
         ((rows, count * width), BF16),
         ((rows, count * width), BF16),
     ]
     shapes = [jax.ShapeDtypeStruct(*s) for s in shapes]
+    scratch = [
+        ((rows, wide), BF16),
+        ((rows, model), BF16),
+        ((others, own, model), BF16),
+        ((length, model), BF16),
+        ((length, model), BF16),
+        ((sides, own, model), BF16),
+        ((pairs, rows, 2 * width), F32),
+        ((rows, 2 * EXTRA), BF16),
+        ((rows, model), F32),
+        ((rows, model), F32),
+    ]
     return pl.pallas_call(
-        functools.partial(plane_kernel, dp, tp),
-        grid=(count // 2,),
+        functools.partial(front_kernel, dp, tp),
+        grid=(2 * pairs,),
         out_shape=shapes,
-        in_specs=[whole(x), whole(g), whole(gz), whole(wr)]
-        + [by_pair((model, width)), by_pair((model, width)), by_pair((width, model))],
-        out_specs=[ANY, ANY] + [whole(s) for s in shapes[2:6]] + [saved] * 3,
-        scratch_shapes=[
-            pltpu.VMEM((rows, 2 * EXTRA), BF16),
-            pltpu.VMEM((rows, model), F32),
-            pltpu.VMEM((rows, model), F32),
+        in_specs=[whole_spec(a) for a in arrays] + [up((model, width)), up((model, width)), down],
+        out_specs=[ANY, ANY] + [whole_spec(s) for s in shapes[2:12]] + [saved] * 3,
+        scratch_shapes=[pltpu.VMEM(*s) for s in scratch]
+        + [
             pltpu.SemaphoreType.DMA((copies,)),
             pltpu.SemaphoreType.DMA((copies,)),
             pltpu.SemaphoreType.DMA((2 + others,)),
         ],
         compiler_params=pltpu.CompilerParams(
-            collective_id=1, has_side_effects=True, vmem_limit_bytes=VMEM_LIMIT
+            collective_id=0, has_side_effects=True, vmem_limit_bytes=VMEM_LIMIT
         ),
-        name="plane_experts",
-    )(x, g, gz, wr, w_gate, w_up, w_down)
+        name="front",
+    )(*arrays, *weights)
 
 
 def backward_kernel(
     dp,
     tp,
-    back_ref,
-    moe_ref,
-    dgate_ref,
+    back_hbm,
+    moe_hbm,
+    dgate_hbm,
     gates_ref,
     h1_ref,
-    tok_ref,
-    cot_ref,
+    tok_hbm,
+    cot_hbm,
     ga_ref,
     gm_ref,
     wr_ref,
-    wq_ref,
-    wk_ref,
-    wv_ref,
-    wo_ref,
-    qkv_ref,
-    att_ref,
-    lse_ref,
-    n1_ref,
-    rope_ref,
+    wq_hbm,
+    wk_hbm,
+    wv_hbm,
+    wo_hbm,
+    qkv_hbm,
+    att_hbm,
+    prob_hbm,
+    prob_t_hbm,
+    n1t_hbm,
+    rope_hbm,
     xr_ref,
     gr_ref,
     wg_ref,
@@ -892,6 +886,21 @@
     ghid_ref,
     dgp_ref,
     dup_ref,
+    back_ref,
+    moe_ref,
+    dgate_ref,
+    tok_ref,
+    cot_ref,
+    wq_ref,
+    wk_ref,
+    wv_ref,
+    wo_ref,
+    qkv_ref,
+    att_ref,
+    prob_ref,
+    prob_t_ref,
+    n1t_ref,
+    rope_ref,
     x_rest,
     g_rest,
     split,
@@ -929,6 +938,7 @@
     send_sem,
     recv_sem,
     keep_sem,
+    load_sem,
 ):
     step, last = pl.program_id(0), pl.num_programs(0) - 1
     net = Peers(dp, tp, send_sem, recv_sem)
@@ -969,10 +979,10 @@
             copy.start()
 
     pair_bd = [
-        link(back_ref.at[there], pair_b, net.partner()),
-        link(dgate_ref.at[there], pair_d, net.partner()),
+        link(back_hbm.at[there], pair_b, net.partner()),
+        link(dgate_hbm.at[there], pair_d, net.partner()),
     ]
-    pair_mo = [link(moe_ref.at[there], pair_m, net.partner())]
+    pair_mo = [link(moe_hbm.at[there], pair_m, net.partner())]
     side_bd = to_sides(sum_b, rs_b) + to_sides(sum_d, rs_d)
     side_mo = to_sides(sum_m, rs_m)
     share_da = share(da_buf) + share(dl_buf)
@@ -995,6 +1005,29 @@
     keep_dl = pltpu.make_async_copy(dl_buf, dl_all.at[here], keep_sem.at[0])
     plane_rows = xr_ref.shape[0] // dp
     rest = pl.ds(plane_rows, xr_ref.shape[0] - plane_rows)
+    late = [
+        (back_hbm.at[here], back_ref),
+        (dgate_hbm.at[here], dgate_ref),
+        (moe_hbm.at[here], moe_ref),
+        (cot_hbm, cot_ref),
+        (wo_hbm, wo_ref),
+        (att_hbm, att_ref),
+        (qkv_hbm, qkv_ref),
+        (prob_hbm, prob_ref),
+        (prob_t_hbm, prob_t_ref),
+        (rope_hbm, rope_ref),
+        (wq_hbm, wq_ref),
+        (wk_hbm, wk_ref),
+        (wv_hbm, wv_ref),
+        (n1t_hbm, n1t_ref),
+        (tok_hbm, tok_ref),
+    ]
+    late = [pltpu.make_async_copy(src, dst, load_sem.at[i]) for i, (src, dst) in enumerate(late)]
+
+    def loaded(first, end):
+        for copy in late[first:end]:
+            copy.wait()
+
     load_x = pltpu.make_async_copy(xr_ref.at[rest], x_rest, keep_sem.at[1])
     load_g = pltpu.make_async_copy(gr_ref.at[rest], g_rest, keep_sem.at[2])
 
@@ -1002,8 +1035,10 @@
     def _():
         load_x.start()
         load_g.start()
+        start(late[:2])
         net.greet()
         start(pair_bd)
+        start(late[2:])
         load_x.wait()
         store_split(gates_of(x_rest, wr_ref, model), split)
         load_g.wait()
@@ -1011,8 +1046,9 @@
     @pl.when(step == 1)
     def _():
         arrived(pair_bd)
-        sum_b[...] = (back_ref[here, :].astype(F32) + pair_b[...].astype(F32)).astype(BF16)
-        sum_d[...] = dgate_ref[here, :] + pair_d[...]
+        loaded(0, 2)
+        sum_b[...] = (back_ref[...].astype(F32) + pair_b[...].astype(F32)).astype(BF16)
+        sum_d[...] = dgate_ref[...] + pair_d[...]
         start(side_bd + pair_mo)
 
     def over_pair(part, pair, total):
@@ -1027,6 +1063,7 @@
     @pl.when(step == 3)
     def _():
         arrived(side_bd)
+        loaded(2, 4)
         d_n2 = sum_b[mine, :].astype(F32)
         dgate = sum_d[mine, :]
         for k in sides:
@@ -1047,17 +1084,17 @@
         da_buf[mine, :] = d_h1.astype(BF16)
         start(share_da)
         arrived(pair_mo)
-        sum_m[...] = (moe_ref[here, :].astype(F32) + pair_m[...].astype(F32)).astype(BF16)
+        sum_m[...] = (moe_ref[...].astype(F32) + pair_m[...].astype(F32)).astype(BF16)
 
     @pl.when(step == 5)
     def _():
+        loaded(4, len(late))
         arrived(share_da)
         start(side_mo + dl_z + dl_own)
         keep_dl.start()
         do_buf[...] = dot_nt(da_buf[...], wo_ref[...]).astype(BF16)
         o_part[...] = dot_tn(da_buf[...], att_ref[...]).astype(BF16).reshape(o_part.shape)
         start(o_core)
-        seen = causal(length)
         scale = HEAD_SIZE ** (-0.5)
         d_key, d_val, d_query = [], [], []
         for kv in range(kv_width // HEAD_SIZE):
@@ -1075,17 +1112,21 @@
                 at = slice(h * HEAD_SIZE, (h + 1) * HEAD_SIZE)
                 q = qkv_ref[:, at]
                 d_out = do_buf[:, at]
-                s = jnp.where(seen, dot_nt(q, key) * scale, -1e30)
-                prob = jnp.exp(s - lse_ref[:, h : h + 1])
                 delta = jnp.sum(
                     d_out.astype(F32) * att_ref[:, at].astype(F32), axis=-1, keepdims=True
                 )
-                d_s = (prob * (dot_nt(d_out, val) - delta)).astype(BF16)
+                d_s = (prob_ref[h].astype(F32) * (dot_nt(d_out, val) - delta)).astype(BF16)
                 d_query.append(dot(d_s, key) * scale)
                 dk = dk + dot_tn(d_s, q)
-                dv = dv + dot_tn(prob.astype(BF16), d_out)
+                dv = dv + dot(prob_t_ref[h], d_out)
             d_key.append(dk * scale)
             d_val.append(dv)
+        arrived(side_mo)
+        total = h1_ref[...] + sum_m[mine, :].astype(F32)
+        for k in sides:
+            total = total + rs_m[k - 1].astype(F32)
+        out_buf[mine, :] = total.astype(BF16)
+        start(share_out)
         d_buf[:, :q_width] = rotate(jnp.concatenate(d_query, axis=1), rope_ref, -1.0).astype(BF16)
         d_buf[:, q_width : q_width + kv_width] = rotate(
             jnp.concatenate(d_key, axis=1), rope_ref, -1.0
@@ -1096,7 +1137,7 @@
         part_n1 = part_n1 + dot_nt(d_buf[:, q_width + kv_width :], wv_ref[...])
         part_buf[...] = part_n1.astype(BF16)
         start(side_3)
-        q_part[...] = dot_tn(n1_ref[...], d_buf[...]).astype(BF16).reshape(q_part.shape)
+        q_part[...] = dot(n1t_ref[...], d_buf[...]).astype(BF16).reshape(q_part.shape)
         start(q_core)
 
     @pl.when(step == 6)
@@ -1104,11 +1145,6 @@
         arrived(q_core)
         over_pair(q_part, q_pair, q_sum)
         start(q_z)
-        arrived(side_mo)
-        total = h1_ref[...] + sum_m[mine, :].astype(F32)
-        for k in sides:
-            total = total + rs_m[k - 1].astype(F32)
-        out_buf[mine, :] = total.astype(BF16)
         arrived(dl_z)
         start(dl_c)
 
@@ -1134,7 +1170,7 @@
         for k in sides:
             gain = gain + gain_t[k - 1]
         gain_zs[...] = gain
-        start(plane_gain + share_out)
+        start(plane_gain)
 
     @pl.when(step == 9)
     def _():
@@ -1174,11 +1210,6 @@
         sent = sent + dl_z + dl_own + dl_c + q_core + q_z + o_core + o_z
         for copy in sent + side_gain + plane_gain + pair_gain:
             copy.wait_send()
-
-
-def whole_spec(a):
-    shape = a.shape
-    return pl.BlockSpec(shape, lambda *_: (0,) * len(shape), pipeline_mode=pl.Buffered(1))
 
 
 def backward(dp, tp, arrays, streamed, weights):
@@ -1208,7 +1239,12 @@
     ]
     shapes = [jax.ShapeDtypeStruct(*s) for s in shapes]
     full, block, slots = (length, model), (own, model), (sides, own, model)
+    copied = [arrays[i] for i in (5, 6, *range(10, len(arrays)))]
     scratch = [
+        (full, BF16),
+        (full, BF16),
+        ((length, EXTRA), F32),
+        *((a.shape, a.dtype) for a in copied),
         ((rest_rows, streamed[0].shape[1]), BF16),
         ((rest_rows, model), BF16),
         ((rest_rows, 2 * EXTRA), BF16),
@@ -1248,7 +1284,7 @@
         functools.partial(backward_kernel, dp, tp),
         grid=(count // 2,),
         out_shape=shapes,
-        in_specs=[whole_spec(a) for a in arrays]
+        in_specs=[whole_spec(a) if i in (3, 4, 7, 8, 9) else ANY for i, a in enumerate(arrays)]
         + [ANY, ANY]
         + [by_pair((model, width)), by_pair((model, width)), by_pair((width, model))],
         out_specs=[whole_spec(shapes[0]), whole_spec(shapes[1]), ANY]
@@ -1259,6 +1295,7 @@
             pltpu.SemaphoreType.DMA((copies,)),
             pltpu.SemaphoreType.DMA((copies,)),
             pltpu.SemaphoreType.DMA((3,)),
+            pltpu.SemaphoreType.DMA((3 + len(copied),)),
         ],
         compiler_params=pltpu.CompilerParams(
             collective_id=2, has_side_effects=True, vmem_limit_bytes=VMEM_LIMIT
@@ -1406,15 +1443,12 @@
     ga, gm = gain_attn, gain_moe
     wr = jnp.pad(w_router, ((0, 0), (0, EXTRA - experts)))
     heads = (w_query, key_projection, value_projection, w_out)
-    x, g, gz, h1, n1, qkv, att, lse = forward(
-        dp, tp, tokens, cotangent, routes, ga, gm, *heads, rope
-    )
-    x_all, g_all, moe, back, dgate, gates, ghid, dgp, dup = plane_experts(
-        dp, tp, x, g, gz, wr, w_gate, w_up, w_down
+    x_all, g_all, moe, back, dgate, gates, h1, *saved, ghid, dgp, dup = front(
+        dp, tp, (tokens, cotangent, routes, ga, gm, wr, *heads, rope), (w_gate, w_up, w_down)
     )
     local = (back, moe, dgate, gates, h1, tokens, cotangent, ga, gm, wr, *heads)
     output, input_grad, d_logits, qkv_grad, o_grad, gains, *rest = backward(
-        dp, tp, (*local, qkv, att, lse, n1, rope), (x_all, g_all), (w_gate, w_up, w_down)
+        dp, tp, (*local, *saved, rope), (x_all, g_all), (w_gate, w_up, w_down)
     )
     place = jnp.stack([lax.axis_index("dp"), lax.axis_index("expert")]).astype(jnp.int32)
     (

time: 212 us -> 194 us (0.915)
  Pallas kernels: 207 us -> 188 us
    pallas_call x2 -> x1, Pallas kernels: 93.4 us -> 76.8 us  [front(): pl.pallas_call(functools.partial(front_kernel, dp, tp), grid=(2 * pairs,)...]
where the time goes in v5:
time: 194 us; the launch traced here: 193 us
  Pallas kernels  188 us (97%)
  local copies, waits for them, and re-layouts  3.43 us (2%)
    pallas_call x1, Pallas kernels, backward(): pl.pallas_call(functools.partial(backward_kernel, dp, tp), grid=(count //...  86 us
    pallas_call x1, Pallas kernels, front(): pl.pallas_call(functools.partial(front_kernel, dp, tp), grid=(2 * pairs,)...  76.8 us
    pallas_call x1, Pallas kernels, weight_grads(): pl.pallas_call(weights_kernel, grid_spec=pltpu.PrefetchScalarGridSpec(num...  25.6 us

profile of v5, /device:TPU:0, one launch (start us, length us, event | category | flops | bytes accessed | tf_op | source)
XLA Modules:
  0.0 193.3 jit_solution(18001731826288555223)
XLA Ops:
  0.6 0.7 pad_add_fusion.place_ref
  1.3 1.5 copy.27.routes_ref
  2.8 1.1 copy.26
  3.9 0.8 pad.4.wr_ref
  4.8 76.8 %front.1 = (bf16[2048,1664]{1,0:T(8,128)(2,1)}, bf16[2048,1536]{1,0:T(8,128)(2,1)}, bf16[512,1536]{1,0:T(8,128)(2,1)}, bf16[512,1536]{1,0:T(8,128)(2,1)}, f32[51...) custom-call(bf16[256,1536]{1,0:T(8,128)(2,1)} %tok_hbm.1, ...), custom_call_target="tpu_custom_call" | custom-call | tf_op jit(solution)/shard_map/front/pallas_call | solution.py:833
  81.6 86.0 %backward.1 = (bf16[256,1536]{1,0:T(8,128)(2,1)}, bf16[256,1536]{1,0:T(8,128)(2,1)}, bf16[2048,128]{1,0:T(8,128)(2,1)}, f32[192,640]{1,0:T(8,128)}, f32[192,384]...) custom-call(bf16[512,1536]{1,0:T(8,128)(2,1)} %get-tuple-element.50., ...), custom_call_target="tpu_custom_call" | custom-call | tf_op jit(solution)/shard_map/backward/pallas_call | solution.py:1283
  167.6 25.6 %weight_grads.1 = (f32[20,384,128]{2,1,0:T(8,128)}, f32[20,384,128]{2,1,0:T(8,128)}, f32[20,128,384]{2,1,0:T(8,128)}, f32[192,384]{1,0:T(8,128)}, f32[192,128]{1...) custom-call(s32[2]{0:T(128)} %pad_add_fusion.place_ref, ...), custom_call_target="tpu_custom_call" | custom-call | tf_op jit(solution)/shard_map/weight_grads/pallas_call | solution.py:1397

commit v6 on v5

--- a/solution.py
+++ b/solution.py
@@ -393,6 +393,7 @@
 ANY = pl.BlockSpec(memory_space=pl.ANY)
 EXTRA = 128
 VMEM_LIMIT = 60 * 2**20
+STAGE_PLACES = (1, 5, 9, 11, 14, 16, 18)
 F32, BF16 = jnp.float32, jnp.bfloat16
 
 
@@ -478,14 +479,20 @@
         copy.wait_recv()
 
 
-def rotate(u, rope_ref, sign):
+def rotate(u, rope_ref, scale=1.0, sign=1.0):
     width = u.shape[1]
     tiles = []
     for at in range(0, width, 128):
         v = u[:, at : at + 128]
         side = pltpu.roll(v, 96, 1) * rope_ref[1] + pltpu.roll(v, 32, 1) * rope_ref[2]
-        tiles.append(v * rope_ref[0] + sign * side)
+        turned = v * rope_ref[0] + side if sign > 0 else v * rope_ref[0] - side
+        tiles.append(turned if scale == 1.0 else turned * scale)
     return tiles[0] if len(tiles) == 1 else jnp.concatenate(tiles, axis=1)
+
+
+def stack_heads(u, kv, group):
+    heads = [kv * group + j for j in range(group)]
+    return jnp.concatenate([u[:, h * HEAD_SIZE : (h + 1) * HEAD_SIZE] for h in heads], axis=0)
 
 
 def inverse_rms(u):
@@ -498,8 +505,13 @@
     return col <= row
 
 
-def gates_of(x_ref, wr_ref, model):
-    logits = dot(x_ref[:, :model], wr_ref[...])
+def pad_router(wr_ref, wr_buf):
+    wr_buf[...] = jnp.zeros_like(wr_buf)
+    wr_buf[: wr_ref.shape[0], :] = wr_ref[...]
+
+
+def gates_of(x_ref, wr_buf, model):
+    logits = dot_nt(x_ref[:, :model], wr_buf[...])
     chosen = x_ref[:, model:].astype(F32) > 0.5
     top = jnp.max(jnp.where(chosen, logits, -jnp.inf), axis=1, keepdims=True)
     weight = jnp.where(chosen, jnp.exp(jnp.where(chosen, logits - top, 0.0)), 0.0)
@@ -554,17 +566,22 @@
     dgate_ref,
     gates_ref,
     h1_ref,
-    qkv_ref,
+    kv_ref,
     att_ref,
+    qs_ref,
+    as_ref,
     prob_ref,
     prob_t_ref,
     n1t_ref,
     ghid_ref,
     dgp_ref,
     dup_ref,
+    place_ref,
     x_buf,
     g_buf,
     gz_buf,
+    wr_buf,
+    routes_buf,
     n1_buf,
     part_buf,
     rs_buf,
@@ -666,31 +683,34 @@
         resid = tok_ref[...].astype(F32)
         n1 = (resid * inverse_rms(resid) * ga_ref[...].reshape(1, -1)).astype(BF16)
         n1_buf[...] = n1
-        qkv_ref[:, :q_width] = rotate(dot(n1, wq_ref[...]), rope_ref, 1.0).astype(BF16)
-        qkv_ref[:, q_width : q_width + kv_width] = rotate(
-            dot(n1, wk_ref[...]), rope_ref, 1.0
-        ).astype(BF16)
-        qkv_ref[:, q_width + kv_width :] = dot(n1, wv_ref[...]).astype(BF16)
+        q_all = rotate(dot(n1, wq_ref[...]), rope_ref, HEAD_SIZE ** (-0.5)).astype(BF16)
+        kv_ref[:, :kv_width] = rotate(dot(n1, wk_ref[...]), rope_ref).astype(BF16)
+        kv_ref[:, kv_width:] = dot(n1, wv_ref[...]).astype(BF16)
         seen = causal(length)
-        scale = HEAD_SIZE ** (-0.5)
-        for h in range(q_width // HEAD_SIZE):
-            kv = h // group
-            at_k = q_width + kv * HEAD_SIZE
-            at_v = q_width + kv_width + kv * HEAD_SIZE
-            q = qkv_ref[:, h * HEAD_SIZE : (h + 1) * HEAD_SIZE]
-            key = qkv_ref[:, at_k : at_k + HEAD_SIZE]
-            val = qkv_ref[:, at_v : at_v + HEAD_SIZE]
-            s = jnp.where(seen, dot_nt(q, key) * scale, -1e30)
-            top = jnp.max(s, axis=-1, keepdims=True)
-            lse = top + jnp.log(jnp.sum(jnp.exp(s - top), axis=-1, keepdims=True))
-            prob = jnp.exp(s - lse).astype(BF16)
-            prob_ref[h] = prob
-            att_ref[:, h * HEAD_SIZE : (h + 1) * HEAD_SIZE] = dot(prob, val).astype(BF16)
+        for kv in range(kv_width // HEAD_SIZE):
+            key = kv_ref[:, kv * HEAD_SIZE : (kv + 1) * HEAD_SIZE]
+            val = kv_ref[:, kv_width + kv * HEAD_SIZE : kv_width + (kv + 1) * HEAD_SIZE]
+            q = stack_heads(q_all, kv, group)
+            qs_ref[kv] = q
+            s = dot_nt(q, key).reshape(group, length, length)
+            s = jnp.where(seen[None], s, -1e30)
+            up_to = jnp.exp(s - jnp.max(s, axis=-1, keepdims=True))
+            prob = up_to * (1.0 / jnp.sum(up_to, axis=-1, keepdims=True))
+            prob = prob.reshape(group * length, length).astype(BF16)
+            prob_ref[kv] = prob
+            att = dot(prob, val).astype(BF16)
+            as_ref[kv] = att
+            for j in range(group):
+                h = kv * group + j
+                att_ref[:, h * HEAD_SIZE : (h + 1) * HEAD_SIZE] = att[j * length : (j + 1) * length]
         part_buf[...] = dot(att_ref[...], wo_ref[...]).astype(BF16)
         start(side_h)
         moe_acc[...] = jnp.zeros_like(moe_acc)
         back_acc[...] = jnp.zeros_like(back_acc)
         dgate_ref[...] = jnp.zeros_like(dgate_ref)
+        pad_router(wr_ref, wr_buf)
+        place_ref[0] = z
+        place_ref[1] = c
         arrived(g_own)
 
     @pl.when(step < pairs)
@@ -700,7 +720,8 @@
     @pl.when(step == pairs)
     def _():
         total = tok_ref[ds(t, own), :].astype(F32) + part_buf[ds(t, own), :].astype(F32)
-        picked = routes_ref[ds(t, own), :]
+        routes_buf[...] = routes_ref[...].T
+        picked = routes_buf[ds(t, own), :]
         ids = lax.broadcasted_iota(jnp.int32, (own, EXTRA), 1)
         chosen = picked[:, 0:1] == ids
         for j in range(1, picked.shape[1]):
@@ -713,8 +734,8 @@
         x_buf[mine, model:] = jnp.where(chosen, 1.0, 0.0).astype(BF16)
         start(x_t + x_own + x_z)
         h1_ref[...] = total
-        for h in range(q_width // HEAD_SIZE):
-            prob_t_ref[h] = prob_ref[h].T
+        for kv in range(kv_width // HEAD_SIZE):
+            prob_t_ref[kv] = prob_ref[kv].T
         n1t_ref[...] = n1_buf[...].T
         for k in sides:
             arrived(x_t[k - 1 : k])
@@ -723,7 +744,7 @@
         start(g_direct + g_core + keep_g)
         arrived(x_own + x_seen)
         keep_x.start()
-        gates = gates_of(x_buf, wr_ref, model)
+        gates = gates_of(x_buf, wr_buf, model)
         gates_ref[...] = gates
         store_split(gates, split)
 
@@ -786,14 +807,13 @@
 
 
 def front(dp, tp, arrays, weights):
-    tokens, wq, wk, wv = arrays[0], *arrays[6:9]
+    tokens, wq, wk = arrays[0], arrays[6], arrays[7]
     length, model = tokens.shape
     count, _, width = weights[0].shape
     pairs = count // 2
     rows, own = 2 * length, length // tp
-    heads, wide = wq.shape[1] // HEAD_SIZE, model + EXTRA
-    q_width = wq.shape[1]
-    widths = q_width + wk.shape[1] + wv.shape[1]
+    wide, q_width = model + EXTRA, wq.shape[1]
+    kv_heads, group = wk.shape[1] // HEAD_SIZE, q_width // wk.shape[1]
     others, sides = dp - 1, tp - 1
     copies = 1 + others + sides + sides + 1 + sides + 2 * others + (8 + 6) * others
     later = lambda i: jnp.maximum(i - pairs, 0)
@@ -808,20 +828,25 @@
         ((rows, EXTRA), F32),
         ((rows, EXTRA), F32),
         ((own, model), F32),
-        ((length, widths), BF16),
+        ((length, 2 * wk.shape[1]), BF16),
         ((length, q_width), BF16),
-        ((heads, length, length), BF16),
-        ((heads, length, length), BF16),
+        ((kv_heads, group * length, HEAD_SIZE), BF16),
+        ((kv_heads, group * length, HEAD_SIZE), BF16),
+        ((kv_heads, group * length, length), BF16),
+        ((kv_heads, length, group * length), BF16),
         ((model, length), BF16),
         ((rows, count * width), BF16),
         ((rows, count * width), BF16),
         ((rows, count * width), BF16),
     ]
+    shapes.append(((2,), jnp.int32))
     shapes = [jax.ShapeDtypeStruct(*s) for s in shapes]
     scratch = [
         ((rows, wide), BF16),
         ((rows, model), BF16),
         ((others, own, model), BF16),
+        ((EXTRA, model), BF16),
+        ((length, arrays[2].shape[0]), jnp.int32),
         ((length, model), BF16),
         ((length, model), BF16),
         ((sides, own, model), BF16),
@@ -835,7 +860,10 @@
         grid=(2 * pairs,),
         out_shape=shapes,
         in_specs=[whole_spec(a) for a in arrays] + [up((model, width)), up((model, width)), down],
-        out_specs=[ANY, ANY] + [whole_spec(s) for s in shapes[2:12]] + [saved] * 3,
+        out_specs=[ANY, ANY]
+        + [whole_spec(s) for s in shapes[2:14]]
+        + [saved] * 3
+        + [pl.BlockSpec(memory_space=pltpu.SMEM)],
         scratch_shapes=[pltpu.VMEM(*s) for s in scratch]
         + [
             pltpu.SemaphoreType.DMA((copies,)),
@@ -866,14 +894,17 @@
     wk_hbm,
     wv_hbm,
     wo_hbm,
-    qkv_hbm,
+    kv_hbm,
     att_hbm,
+    qs_hbm,
+    as_hbm,
     prob_hbm,
     prob_t_hbm,
     n1t_hbm,
     rope_hbm,
     xr_ref,
     gr_ref,
+    own_ref,
     wg_ref,
     wu_ref,
     wd_ref,
@@ -883,7 +914,7 @@
     qkv_grad_ref,
     o_grad_ref,
     gains_ref,
-    ghid_ref,
+    down_ref,
     dgp_ref,
     dup_ref,
     back_ref,
@@ -895,14 +926,19 @@
     wk_ref,
     wv_ref,
     wo_ref,
-    qkv_ref,
+    kv_ref,
     att_ref,
+    qs_ref,
+    as_ref,
     prob_ref,
     prob_t_ref,
     n1t_ref,
     rope_ref,
     x_rest,
     g_rest,
+    wr_buf,
+    g_plane,
+    gt_buf,
     split,
     pair_b,
     pair_m,
@@ -1012,7 +1048,9 @@
         (cot_hbm, cot_ref),
         (wo_hbm, wo_ref),
         (att_hbm, att_ref),
-        (qkv_hbm, qkv_ref),
+        (kv_hbm, kv_ref),
+        (qs_hbm, qs_ref),
+        (as_hbm, as_ref),
         (prob_hbm, prob_ref),
         (prob_t_hbm, prob_t_ref),
         (rope_hbm, rope_ref),
@@ -1030,21 +1068,28 @@
 
     load_x = pltpu.make_async_copy(xr_ref.at[rest], x_rest, keep_sem.at[1])
     load_g = pltpu.make_async_copy(gr_ref.at[rest], g_rest, keep_sem.at[2])
+    load_own = pltpu.make_async_copy(
+        gr_ref.at[pl.ds(0, plane_rows), columns(z)], g_plane, keep_sem.at[3]
+    )
 
     @pl.when(step == 0)
     def _():
         load_x.start()
         load_g.start()
+        load_own.start()
         start(late[:2])
         net.greet()
         start(pair_bd)
+        load_x.wait()
+        pad_router(wr_ref, wr_buf)
+        store_split(gates_of(x_rest, wr_buf, model), split)
+        load_g.wait()
+        load_own.wait()
         start(late[2:])
-        load_x.wait()
-        store_split(gates_of(x_rest, wr_ref, model), split)
-        load_g.wait()
-
-    @pl.when(step == 1)
-    def _():
+        gt_buf[:, :plane_rows] = g_plane[...].T
+        gt_buf[:, plane_rows:] = g_rest[:, columns(z)].T
+
+    def pair_sum():
         arrived(pair_bd)
         loaded(0, 2)
         sum_b[...] = (back_ref[...].astype(F32) + pair_b[...].astype(F32)).astype(BF16)
@@ -1060,8 +1105,7 @@
             value = value + came[k - 1].astype(F32)
         out[...] = value
 
-    @pl.when(step == 3)
-    def _():
+    def moe_backward():
         arrived(side_bd)
         loaded(2, 4)
         d_n2 = sum_b[mine, :].astype(F32)
@@ -1072,7 +1116,7 @@
         gates = gates_ref[ds(c * tp + t, own), :]
         d_logits = gates * (dgate - jnp.sum(gates * dgate, axis=1, keepdims=True))
         dl_buf[mine, :] = d_logits.astype(BF16)
-        d_n2 = d_n2 + dot_nt(d_logits.astype(BF16), wr_ref[...])
+        d_n2 = d_n2 + dot(d_logits.astype(BF16), wr_buf[...])
         h1 = h1_ref[...]
         r2 = inverse_rms(h1)
         weighted = d_n2 * gm_ref[...].reshape(1, -1)
@@ -1086,8 +1130,7 @@
         arrived(pair_mo)
         sum_m[...] = (moe_ref[...].astype(F32) + pair_m[...].astype(F32)).astype(BF16)
 
-    @pl.when(step == 5)
-    def _():
+    def attention_backward():
         loaded(4, len(late))
         arrived(share_da)
         start(side_mo + dl_z + dl_own)
@@ -1102,34 +1145,24 @@
                 arrived(o_core)
                 over_pair(o_part, o_pair, o_sum)
                 start(o_z)
-            at_k = q_width + kv * HEAD_SIZE
-            at_v = q_width + kv_width + kv * HEAD_SIZE
-            key = qkv_ref[:, at_k : at_k + HEAD_SIZE]
-            val = qkv_ref[:, at_v : at_v + HEAD_SIZE]
-            dk = jnp.zeros((length, HEAD_SIZE), F32)
-            dv = jnp.zeros((length, HEAD_SIZE), F32)
-            for h in range(kv * group, (kv + 1) * group):
-                at = slice(h * HEAD_SIZE, (h + 1) * HEAD_SIZE)
-                q = qkv_ref[:, at]
-                d_out = do_buf[:, at]
-                delta = jnp.sum(
-                    d_out.astype(F32) * att_ref[:, at].astype(F32), axis=-1, keepdims=True
-                )
-                d_s = (prob_ref[h].astype(F32) * (dot_nt(d_out, val) - delta)).astype(BF16)
-                d_query.append(dot(d_s, key) * scale)
-                dk = dk + dot_tn(d_s, q)
-                dv = dv + dot(prob_t_ref[h], d_out)
-            d_key.append(dk * scale)
-            d_val.append(dv)
+            key = kv_ref[:, kv * HEAD_SIZE : (kv + 1) * HEAD_SIZE]
+            val = kv_ref[:, kv_width + kv * HEAD_SIZE : kv_width + (kv + 1) * HEAD_SIZE]
+            d_out = stack_heads(do_buf, kv, group)
+            delta = jnp.sum(d_out.astype(F32) * as_ref[kv].astype(F32), axis=-1, keepdims=True)
+            d_s = (prob_ref[kv].astype(F32) * (dot_nt(d_out, val) - delta)).astype(BF16)
+            d_q = dot(d_s, key) * scale
+            d_query += [d_q[j * length : (j + 1) * length] for j in range(group)]
+            d_key.append(dot_tn(d_s, qs_ref[kv]))
+            d_val.append(dot(prob_t_ref[kv], d_out))
         arrived(side_mo)
         total = h1_ref[...] + sum_m[mine, :].astype(F32)
         for k in sides:
             total = total + rs_m[k - 1].astype(F32)
         out_buf[mine, :] = total.astype(BF16)
         start(share_out)
-        d_buf[:, :q_width] = rotate(jnp.concatenate(d_query, axis=1), rope_ref, -1.0).astype(BF16)
+        d_buf[:, :q_width] = rotate(jnp.concatenate(d_query, axis=1), rope_ref, sign=-1.0).astype(BF16)
         d_buf[:, q_width : q_width + kv_width] = rotate(
-            jnp.concatenate(d_key, axis=1), rope_ref, -1.0
+            jnp.concatenate(d_key, axis=1), rope_ref, sign=-1.0
         ).astype(BF16)
         d_buf[:, q_width + kv_width :] = jnp.concatenate(d_val, axis=1).astype(BF16)
         part_n1 = dot_nt(d_buf[:, :q_width], wq_ref[...])
@@ -1140,16 +1173,14 @@
         q_part[...] = dot(n1t_ref[...], d_buf[...]).astype(BF16).reshape(q_part.shape)
         start(q_core)
 
-    @pl.when(step == 6)
-    def _():
+    def send_parts():
         arrived(q_core)
         over_pair(q_part, q_pair, q_sum)
         start(q_z)
         arrived(dl_z)
         start(dl_c)
 
-    @pl.when(step == 7)
-    def _():
+    def input_gradient():
         arrived(side_3)
         d_n1 = part_buf[mine, :].astype(F32)
         for k in sides:
@@ -1163,8 +1194,7 @@
         in_buf[mine, :] = d_x.astype(BF16)
         start(side_gain + share_in)
 
-    @pl.when(step == 8)
-    def _():
+    def gain_over_planes():
         arrived(side_gain)
         gain = gain_buf[...]
         for k in sides:
@@ -1172,8 +1202,7 @@
         gain_zs[...] = gain
         start(plane_gain)
 
-    @pl.when(step == 9)
-    def _():
+    def gain_over_pair():
         arrived(plane_gain)
         gain = gain_zs[:, columns(z)]
         for k in others:
@@ -1181,17 +1210,32 @@
         gain_c[0] = gain
         start(pair_gain)
 
+    stages = (pair_sum, moe_backward, attention_backward, send_parts, input_gradient, gain_over_planes, gain_over_pair)
+
+    def stages_at(half):
+        for stage, place in zip(stages, STAGE_PLACES):
+            if place % 2 == half:
+                pl.when(step == place // 2)(stage)
+
+    stages_at(0)
     first = c * (2 * pl.num_programs(0)) + 2 * step
     wd_pair = wd_ref[...].reshape(2 * width, model)
     gate_pair = pair_of_gates(split[...], first, width)
     dh_pair = dot_nt(g_rest[...], wd_pair)
+    hidden = []
     for k in range(2):
+        if k == 1:
+            stages_at(1)
         lanes = slice(k * width, (k + 1) * width)
         both = dot(x_rest[:, :model], jnp.concatenate([wg_ref[k], wu_ref[k]], axis=1))
         _, ghid, dgp, dup = swiglu(both, dh_pair[:, lanes], gate_pair[:, lanes])
-        ghid_ref[:, lanes] = ghid
+        hidden.append(ghid)
         dgp_ref[:, lanes] = dgp
         dup_ref[:, lanes] = dup
+    down = dot(gt_buf[:, :plane_rows], own_ref[...])
+    down = (down + dot(gt_buf[:, plane_rows:], jnp.concatenate(hidden, axis=1))).T
+    for k in range(2):
+        down_ref[k] = down[k * width : (k + 1) * width]
 
     @pl.when(step == last)
     def _():
@@ -1212,7 +1256,7 @@
             copy.wait_send()
 
 
-def backward(dp, tp, arrays, streamed, weights):
+def backward(dp, tp, arrays, streamed, own_hid, weights):
     tokens = arrays[5]
     wq, wk, wv = arrays[10:13]
     all_rows, model = streamed[1].shape
@@ -1233,7 +1277,7 @@
         ((part // 2, wide), F32),
         ((part // 2, q_width), F32),
         ((8, part), F32),
-        ((rest_rows, count * width), BF16),
+        ((count, width, part), F32),
         ((rest_rows, count * width), BF16),
         ((rest_rows, count * width), BF16),
     ]
@@ -1247,6 +1291,9 @@
         *((a.shape, a.dtype) for a in copied),
         ((rest_rows, streamed[0].shape[1]), BF16),
         ((rest_rows, model), BF16),
+        ((EXTRA, model), BF16),
+        ((all_rows - rest_rows, part), BF16),
+        ((part, all_rows), BF16),
         ((rest_rows, 2 * EXTRA), BF16),
         (full, BF16),
         (full, BF16),
@@ -1285,39 +1332,37 @@
         grid=(count // 2,),
         out_shape=shapes,
         in_specs=[whole_spec(a) if i in (3, 4, 7, 8, 9) else ANY for i, a in enumerate(arrays)]
-        + [ANY, ANY]
+        + [ANY, ANY, pl.BlockSpec((own_hid.shape[0], 2 * width), lambda i: (0, i))]
         + [by_pair((model, width)), by_pair((model, width)), by_pair((width, model))],
         out_specs=[whole_spec(shapes[0]), whole_spec(shapes[1]), ANY]
         + [whole_spec(s) for s in shapes[3:6]]
-        + [saved] * 3,
+        + [by_pair((width, part)), saved, saved],
         scratch_shapes=[pltpu.VMEM(*s) for s in scratch]
         + [
             pltpu.SemaphoreType.DMA((copies,)),
             pltpu.SemaphoreType.DMA((copies,)),
-            pltpu.SemaphoreType.DMA((3,)),
+            pltpu.SemaphoreType.DMA((4,)),
             pltpu.SemaphoreType.DMA((3 + len(copied),)),
         ],
         compiler_params=pltpu.CompilerParams(
             collective_id=2, has_side_effects=True, vmem_limit_bytes=VMEM_LIMIT
         ),
         name="backward",
-    )(*arrays, *streamed, *weights)
+    )(*arrays, *streamed, own_hid, *weights)
 
 
 def weights_kernel(
     place_ref,
     x_ref,
-    g_ref,
     dl_ref,
     qkv_grad_ref,
     o_grad_ref,
     gains_ref,
     out_in_ref,
     in_in_ref,
-    ghid_ref,
     dgp_ref,
     dup_ref,
-    ghid_rest,
+    down_ref,
     dgp_rest,
     dup_rest,
     gate_grad_ref,
@@ -1333,17 +1378,15 @@
     out_ref,
     in_ref,
     xt_buf,
-    gt_buf,
 ):
     step = pl.program_id(0)
     c = place_ref[1]
     width = gate_grad_ref.shape[2]
-    plane_rows = ghid_ref.shape[0]
+    plane_rows = dgp_ref.shape[0]
 
     @pl.when(step == 0)
     def _():
         xt_buf[...] = x_ref[...].T
-        gt_buf[...] = g_ref[...].T
         q_width, kv_width = query_ref.shape[1], key_ref.shape[1]
         half = query_ref.shape[0]
         query_ref[...] = qkv_grad_ref[:, :q_width]
@@ -1358,20 +1401,19 @@
         ga_grad_ref[...] = gains[0:1, :]
         gm_grad_ref[...] = gains[1:2, :]
 
-    def contract(left, own, rest):
-        return dot(left[:, :plane_rows], own[...]) + dot(left[:, plane_rows:], rest[...])
-
-    gate_both = contract(xt_buf, dgp_ref, dgp_rest)
-    up_both = contract(xt_buf, dup_ref, dup_rest)
-    down_both = contract(gt_buf, ghid_ref, ghid_rest).T
+    def contract(own, rest):
+        return dot(xt_buf[:, :plane_rows], own[...]) + dot(xt_buf[:, plane_rows:], rest[...])
+
+    gate_both = contract(dgp_ref, dgp_rest)
+    up_both = contract(dup_ref, dup_rest)
+    down_grad_ref[...] = down_ref[...]
     for k in range(2):
         lanes = slice(k * width, (k + 1) * width)
         gate_grad_ref[k] = gate_both[:, lanes]
         up_grad_ref[k] = up_both[:, lanes]
-        down_grad_ref[k] = down_both[lanes, :]
-
-
-def weight_grads(place, x, g, sides, own, rest, count, kv_width, experts):
+
+
+def weight_grads(place, x, sides, own, rest, count, kv_width, experts):
     rows = x.shape[0]
     _, qkv_grad, o_grad, gains, output, _ = sides
     width = own[0].shape[1] // count
@@ -1399,18 +1441,19 @@
         grid_spec=pltpu.PrefetchScalarGridSpec(
             num_scalar_prefetch=1,
             grid=(count // 2,),
-            in_specs=[columns, columns]
+            in_specs=[columns]
             + [whole_spec(a) for a in sides]
             + [saved(a) for a in own]
-            + [saved(a) for a in rest],
+            + [by_pair((width, part))]
+            + [saved(a) for a in rest[1:]],
             out_specs=[by_pair((part, width)), by_pair((part, width)), by_pair((width, part))]
             + [whole_spec(s) for s in shapes[3:]],
-            scratch_shapes=[pltpu.VMEM((part, rows), BF16), pltpu.VMEM((part, rows), BF16)],
+            scratch_shapes=[pltpu.VMEM((part, rows), BF16)],
         ),
         out_shape=shapes,
         compiler_params=pltpu.CompilerParams(vmem_limit_bytes=VMEM_LIMIT),
         name="weight_grads",
-    )(place, x, g, *sides, *own, *rest)
+    )(place, x, *sides, *own, *rest)
 
 
 def rope_rows(length):
@@ -1441,16 +1484,15 @@
     experts = w_router.shape[1]
     rope = jnp.asarray(rope_rows(tokens.shape[0]))
     ga, gm = gain_attn, gain_moe
-    wr = jnp.pad(w_router, ((0, 0), (0, EXTRA - experts)))
+    wr = w_router.T
     heads = (w_query, key_projection, value_projection, w_out)
-    x_all, g_all, moe, back, dgate, gates, h1, *saved, ghid, dgp, dup = front(
-        dp, tp, (tokens, cotangent, routes, ga, gm, wr, *heads, rope), (w_gate, w_up, w_down)
+    x_all, g_all, moe, back, dgate, gates, h1, *saved, ghid, dgp, dup, place = front(
+        dp, tp, (tokens, cotangent, routes.T, ga, gm, wr, *heads, rope), (w_gate, w_up, w_down)
     )
     local = (back, moe, dgate, gates, h1, tokens, cotangent, ga, gm, wr, *heads)
     output, input_grad, d_logits, qkv_grad, o_grad, gains, *rest = backward(
-        dp, tp, (*local, *saved, rope), (x_all, g_all), (w_gate, w_up, w_down)
-    )
-    place = jnp.stack([lax.axis_index("dp"), lax.axis_index("expert")]).astype(jnp.int32)
+        dp, tp, (*local, *saved, rope), (x_all, g_all), ghid, (w_gate, w_up, w_down)
+    )
     (
         gate_grad,
         up_grad,
@@ -1467,9 +1509,8 @@
     ) = weight_grads(
         place,
         x_all,
-        g_all,
         (d_logits, qkv_grad, o_grad, gains, output, input_grad),
-        (ghid, dgp, dup),
+        (dgp, dup),
         rest,
         w_gate.shape[0],
         key_projection.shape[1],

time: 194 us -> 187 us (0.964)
  local copies, waits for them, and re-layouts: 3.43 us -> 0 us
  Pallas kernels: 188 us -> 185 us
    pallas_call x1, Pallas kernels: 25.6 us -> 21.6 us  [weight_grads(): pl.pallas_call(weights_kernel, grid_spec=pltpu.PrefetchScalarGridSpec(num...]
    unnamed x2 -> x0, local copies, waits for them, and re-layouts: 2.61 us -> none
where the time goes in v6:
time: 187 us; the launch traced here: 186 us
  Pallas kernels  185 us (99%)
    pallas_call x1, Pallas kernels, backward(): pl.pallas_call(functools.partial(backward_kernel, dp, tp), grid=(count //...  86.8 us
    pallas_call x1, Pallas kernels, front(): pl.pallas_call(functools.partial(front_kernel, dp, tp), grid=(2 * pairs,)...  77 us
    pallas_call x1, Pallas kernels, weight_grads(): pl.pallas_call(weights_kernel, grid_spec=pltpu.PrefetchScalarGridSpec(num...  21.6 us

profile of v6, /device:TPU:0, one launch (start us, length us, event | category | flops | bytes accessed | tf_op | source)
XLA Modules:
  0.0 186.2 jit_solution(12925072825165329009)
XLA Ops:
  0.6 77.0 %front.1 = (bf16[2048,1664]{1,0:T(8,128)(2,1)}, bf16[2048,1536]{1,0:T(8,128)(2,1)}, bf16[512,1536]{1,0:T(8,128)(2,1)}, bf16[512,1536]{1,0:T(8,128)(2,1)}, f32[51...) custom-call(bf16[256,1536]{1,0:T(8,128)(2,1)} %tok_hbm.1, ...), custom_call_target="tpu_custom_call" | custom-call | tf_op jit(solution)/shard_map/front/pallas_call | solution.py:858
  77.6 86.8 %backward.1 = (bf16[256,1536]{1,0:T(8,128)(2,1)}, bf16[256,1536]{1,0:T(8,128)(2,1)}, bf16[2048,128]{1,0:T(8,128)(2,1)}, f32[192,640]{1,0:T(8,128)}, f32[192,384]...) custom-call(bf16[512,1536]{1,0:T(8,128)(2,1)} %get-tuple-element.53., ...), custom_call_target="tpu_custom_call" | custom-call | tf_op jit(solution)/shard_map/backward/pallas_call | solution.py:1330
  164.4 21.6 %weight_grads.1 = (f32[20,384,128]{2,1,0:T(8,128)}, f32[20,384,128]{2,1,0:T(8,128)}, f32[20,128,384]{2,1,0:T(8,128)}, f32[192,384]{1,0:T(8,128)}, f32[192,128]{1...) custom-call(s32[2]{0:T(128)} %get-tuple-element.51.place_ref, ...), custom_call_target="tpu_custom_call" | custom-call | tf_op jit(solution)/shard_map/weight_grads/pallas_call | solution.py:1439

commit v7 on v6

--- a/solution.py
+++ b/solution.py
@@ -392,8 +392,8 @@
 VMEM = pl.BlockSpec(memory_space=pltpu.VMEM)
 ANY = pl.BlockSpec(memory_space=pl.ANY)
 EXTRA = 128
-VMEM_LIMIT = 60 * 2**20
-STAGE_PLACES = (1, 5, 9, 11, 14, 16, 18)
+VMEM_LIMIT = 63 * 2**20
+STAGE_PLACES = (1, 5, 9, 10, 14, 16, 18)
 F32, BF16 = jnp.float32, jnp.bfloat16
 
 
@@ -510,9 +510,20 @@
     wr_buf[: wr_ref.shape[0], :] = wr_ref[...]
 
 
-def gates_of(x_ref, wr_buf, model):
-    logits = dot_nt(x_ref[:, :model], wr_buf[...])
-    chosen = x_ref[:, model:].astype(F32) > 0.5
+def chosen_of(routes_ref, sequences):
+    masks = []
+    for i in sequences:
+        picked = routes_ref[i]
+        ids = lax.broadcasted_iota(jnp.int32, (EXTRA, picked.shape[1]), 0)
+        chosen = ids == picked[0:1, :]
+        for j in range(1, picked.shape[0]):
+            chosen = chosen | (ids == picked[j : j + 1, :])
+        masks.append(jnp.where(chosen, 1.0, 0.0).T)
+    return jnp.concatenate(masks, axis=0) > 0.5
+
+
+def gates_of(x_ref, chosen, wr_buf):
+    logits = dot_nt(x_ref[...], wr_buf[...])
     top = jnp.max(jnp.where(chosen, logits, -jnp.inf), axis=1, keepdims=True)
     weight = jnp.where(chosen, jnp.exp(jnp.where(chosen, logits - top, 0.0)), 0.0)
     return weight / jnp.sum(weight, axis=1, keepdims=True)
@@ -574,8 +585,8 @@
     prob_t_ref,
     n1t_ref,
     ghid_ref,
-    dgp_ref,
-    dup_ref,
+    dgu_ref,
+    mask_ref,
     place_ref,
     x_buf,
     g_buf,
@@ -669,6 +680,11 @@
         link(x_buf.at[ds(c * tp + far, own)], xr_ref.at[block(dp - k, c, far)], net.plane(k))
         for k in others
     ]
+    r_own = [link(routes_ref, routes_buf.at[c], net.partner())]
+    r_z = [link(routes_ref, routes_buf.at[(dp - k) * 2 + c], net.plane(k)) for k in others]
+    r_core = [
+        link(routes_buf.at[p * 2 + c], routes_buf.at[p * 2 + c], net.partner()) for p in others
+    ]
     keep_x = pltpu.make_async_copy(x_buf, xr_ref.at[pl.ds(0, rows)], keep_sem.at[0])
     keep_g = [pltpu.make_async_copy(g_buf, gr_ref.at[pl.ds(0, rows)], keep_sem.at[1])] + [
         pltpu.make_async_copy(gz_buf.at[p - 1], gr_ref.at[block(p, c, t)], keep_sem.at[1 + p])
@@ -678,8 +694,9 @@
     @pl.when(step == 0)
     def _():
         net.greet()
-        start(g_own + g_z)
+        start(r_own + r_z + g_own + g_z)
         g_buf[seq_rows, :] = cot_ref[...]
+        routes_buf[c] = routes_ref[...]
         resid = tok_ref[...].astype(F32)
         n1 = (resid * inverse_rms(resid) * ga_ref[...].reshape(1, -1)).astype(BF16)
         n1_buf[...] = n1
@@ -717,22 +734,29 @@
     def _():
         dh_buf[step] = dot_nt(g_buf[...], wd_ref[...].reshape(2 * width, model))
 
+    @pl.when(step == pairs // 2)
+    def _():
+        arrived(r_z)
+        start(r_core)
+
+    @pl.when(step == pairs - 1)
+    def _():
+        arrived(r_core)
+        for i in range(2, 2 * dp):
+            masked = chosen_of(routes_buf, range(i, i + 1))
+            mask_ref[(i - 2) * length : (i - 1) * length, :] = jnp.where(masked, 1.0, 0.0).astype(BF16)
+
     @pl.when(step == pairs)
     def _():
         total = tok_ref[ds(t, own), :].astype(F32) + part_buf[ds(t, own), :].astype(F32)
-        routes_buf[...] = routes_ref[...].T
-        picked = routes_buf[ds(t, own), :]
-        ids = lax.broadcasted_iota(jnp.int32, (own, EXTRA), 1)
-        chosen = picked[:, 0:1] == ids
-        for j in range(1, picked.shape[1]):
-            chosen = chosen | (picked[:, j : j + 1] == ids)
         arrived(side_h)
         for k in sides:
             total = total + rs_buf[k - 1].astype(F32)
         n2 = (total * inverse_rms(total) * gm_ref[...].reshape(1, -1)).astype(BF16)
-        x_buf[mine, :model] = n2
-        x_buf[mine, model:] = jnp.where(chosen, 1.0, 0.0).astype(BF16)
+        x_buf[mine, :] = n2
         start(x_t + x_own + x_z)
+        arrived(r_own)
+        chosen = chosen_of(routes_buf, range(2))
         h1_ref[...] = total
         for kv in range(kv_width // HEAD_SIZE):
             prob_t_ref[kv] = prob_ref[kv].T
@@ -744,7 +768,7 @@
         start(g_direct + g_core + keep_g)
         arrived(x_own + x_seen)
         keep_x.start()
-        gates = gates_of(x_buf, wr_buf, model)
+        gates = gates_of(x_buf, chosen, wr_buf)
         gates_ref[...] = gates
         store_split(gates, split)
 
@@ -773,18 +797,19 @@
         first = c * (2 * pairs) + 2 * pair
         gate_pair = pair_of_gates(split[...], first, width)
         lane = lax.broadcasted_iota(jnp.int32, dgate_ref.shape, 1)
+        w_pair = jnp.concatenate([wg_ref[0], wu_ref[0], wg_ref[1], wu_ref[1]], axis=1)
+        both_pair = dot(x_buf[...], w_pair)
         for k in range(2):
             lanes = slice(k * width, (k + 1) * width)
-            w_both = jnp.concatenate([wg_ref[k], wu_ref[k]], axis=1)
-            both = dot(x_buf[:, :model], w_both)
             dh = dh_buf[pair, :, lanes]
+            both = both_pair[:, 2 * k * width : 2 * (k + 1) * width]
             hid, ghid, dgp, dup = swiglu(both, dh, gate_pair[:, lanes])
             ghid_ref[:, lanes] = ghid
-            dgp_ref[:, lanes] = dgp
-            dup_ref[:, lanes] = dup
+            dgu_ref[:, 2 * k * width : (2 * k + 1) * width] = dgp
+            dgu_ref[:, (2 * k + 1) * width : 2 * (k + 1) * width] = dup
             row_sum = jnp.sum(hid * dh, axis=1, keepdims=True)
             dgate_ref[...] += jnp.where(lane == first + k, row_sum, 0.0)
-            back_acc[...] += dot_nt(jnp.concatenate([dgp, dup], axis=1), w_both)
+        back_acc[...] += dot_nt(dgu_ref[...], w_pair)
         moe_acc[...] += dot(ghid_ref[...], wd_ref[...].reshape(2 * width, model))
 
     @pl.when(step == last)
@@ -795,7 +820,7 @@
         for copy in keep_g:
             copy.wait()
         arrived(g_core + g_near + g_far + x_core + x_near + x_far)
-        sent = g_own + g_z + side_h + x_t + x_own + x_seen + x_z
+        sent = g_own + g_z + side_h + x_t + x_own + x_seen + x_z + r_own + r_z + r_core
         sent = sent + g_direct + g_relay + g_core + g_near + g_far
         for copy in sent + x_direct + x_z2 + x_core + x_near + x_far:
             copy.wait_send()
@@ -812,16 +837,17 @@
     count, _, width = weights[0].shape
     pairs = count // 2
     rows, own = 2 * length, length // tp
-    wide, q_width = model + EXTRA, wq.shape[1]
+    q_width = wq.shape[1]
     kv_heads, group = wk.shape[1] // HEAD_SIZE, q_width // wk.shape[1]
     others, sides = dp - 1, tp - 1
-    copies = 1 + others + sides + sides + 1 + sides + 2 * others + (8 + 6) * others
+    copies = 1 + others + sides + sides + 1 + sides + 2 * others + (8 + 6) * others + 1 + 2 * others
     later = lambda i: jnp.maximum(i - pairs, 0)
     up = lambda shape: pl.BlockSpec((2,) + shape, lambda i: (later(i), 0, 0))
     down = pl.BlockSpec((2, width, model), lambda i: (lax.rem(i, pairs), 0, 0))
     saved = pl.BlockSpec((rows, 2 * width), lambda i: (0, later(i)))
+    saved_both = pl.BlockSpec((rows, 4 * width), lambda i: (0, later(i)))
     shapes = [
-        ((rows * dp, wide), BF16),
+        ((rows * dp, model), BF16),
         ((rows * dp, model), BF16),
         ((rows, model), BF16),
         ((rows, model), BF16),
@@ -836,17 +862,17 @@
         ((kv_heads, length, group * length), BF16),
         ((model, length), BF16),
         ((rows, count * width), BF16),
-        ((rows, count * width), BF16),
-        ((rows, count * width), BF16),
+        ((rows, 2 * count * width), BF16),
+        ((rows * others, EXTRA), BF16),
+        ((2,), jnp.int32),
     ]
-    shapes.append(((2,), jnp.int32))
     shapes = [jax.ShapeDtypeStruct(*s) for s in shapes]
     scratch = [
-        ((rows, wide), BF16),
+        ((rows, model), BF16),
         ((rows, model), BF16),
         ((others, own, model), BF16),
         ((EXTRA, model), BF16),
-        ((length, arrays[2].shape[0]), jnp.int32),
+        ((2 * dp, *arrays[2].shape), jnp.int32),
         ((length, model), BF16),
         ((length, model), BF16),
         ((sides, own, model), BF16),
@@ -862,8 +888,7 @@
         in_specs=[whole_spec(a) for a in arrays] + [up((model, width)), up((model, width)), down],
         out_specs=[ANY, ANY]
         + [whole_spec(s) for s in shapes[2:14]]
-        + [saved] * 3
-        + [pl.BlockSpec(memory_space=pltpu.SMEM)],
+        + [saved, saved_both, whole_spec(shapes[16]), pl.BlockSpec(memory_space=pltpu.SMEM)],
         scratch_shapes=[pltpu.VMEM(*s) for s in scratch]
         + [
             pltpu.SemaphoreType.DMA((copies,)),
@@ -905,6 +930,7 @@
     xr_ref,
     gr_ref,
     own_ref,
+    mask_ref,
     wg_ref,
     wu_ref,
     wd_ref,
@@ -915,8 +941,7 @@
     o_grad_ref,
     gains_ref,
     down_ref,
-    dgp_ref,
-    dup_ref,
+    dgu_ref,
     back_ref,
     moe_ref,
     dgate_ref,
@@ -1082,7 +1107,8 @@
         start(pair_bd)
         load_x.wait()
         pad_router(wr_ref, wr_buf)
-        store_split(gates_of(x_rest, wr_buf, model), split)
+        chosen = mask_ref[...].astype(F32) > 0.5
+        store_split(gates_of(x_rest, chosen, wr_buf), split)
         load_g.wait()
         load_own.wait()
         start(late[2:])
@@ -1159,7 +1185,6 @@
         for k in sides:
             total = total + rs_m[k - 1].astype(F32)
         out_buf[mine, :] = total.astype(BF16)
-        start(share_out)
         d_buf[:, :q_width] = rotate(jnp.concatenate(d_query, axis=1), rope_ref, sign=-1.0).astype(BF16)
         d_buf[:, q_width : q_width + kv_width] = rotate(
             jnp.concatenate(d_key, axis=1), rope_ref, sign=-1.0
@@ -1179,6 +1204,7 @@
         start(q_z)
         arrived(dl_z)
         start(dl_c)
+        start(share_out)
 
     def input_gradient():
         arrived(side_3)
@@ -1230,8 +1256,8 @@
         both = dot(x_rest[:, :model], jnp.concatenate([wg_ref[k], wu_ref[k]], axis=1))
         _, ghid, dgp, dup = swiglu(both, dh_pair[:, lanes], gate_pair[:, lanes])
         hidden.append(ghid)
-        dgp_ref[:, lanes] = dgp
-        dup_ref[:, lanes] = dup
+        dgu_ref[:, 2 * k * width : (2 * k + 1) * width] = dgp
+        dgu_ref[:, (2 * k + 1) * width : 2 * (k + 1) * width] = dup
     down = dot(gt_buf[:, :plane_rows], own_ref[...])
     down = (down + dot(gt_buf[:, plane_rows:], jnp.concatenate(hidden, axis=1))).T
     for k in range(2):
@@ -1256,7 +1282,7 @@
             copy.wait_send()
 
 
-def backward(dp, tp, arrays, streamed, own_hid, weights):
+def backward(dp, tp, arrays, streamed, own_hid, mask, weights):
     tokens = arrays[5]
     wq, wk, wv = arrays[10:13]
     all_rows, model = streamed[1].shape
@@ -1269,7 +1295,7 @@
     others, sides = dp - 1, tp - 1
     copies = 3 + 9 * sides + (2 * others + 1) + 2 * (1 + others) + sides + others + 1
     by_pair = lambda shape: pl.BlockSpec((2,) + shape, lambda i: (i, 0, 0))
-    saved = pl.BlockSpec((rest_rows, 2 * width), lambda i: (0, i))
+    saved = pl.BlockSpec((rest_rows, 4 * width), lambda i: (0, i))
     shapes = [
         ((length, model), BF16),
         ((length, model), BF16),
@@ -1278,8 +1304,7 @@
         ((part // 2, q_width), F32),
         ((8, part), F32),
         ((count, width, part), F32),
-        ((rest_rows, count * width), BF16),
-        ((rest_rows, count * width), BF16),
+        ((rest_rows, 2 * count * width), BF16),
     ]
     shapes = [jax.ShapeDtypeStruct(*s) for s in shapes]
     full, block, slots = (length, model), (own, model), (sides, own, model)
@@ -1332,11 +1357,11 @@
         grid=(count // 2,),
         out_shape=shapes,
         in_specs=[whole_spec(a) if i in (3, 4, 7, 8, 9) else ANY for i, a in enumerate(arrays)]
-        + [ANY, ANY, pl.BlockSpec((own_hid.shape[0], 2 * width), lambda i: (0, i))]
+        + [ANY, ANY, pl.BlockSpec((own_hid.shape[0], 2 * width), lambda i: (0, i)), whole_spec(mask)]
         + [by_pair((model, width)), by_pair((model, width)), by_pair((width, model))],
         out_specs=[whole_spec(shapes[0]), whole_spec(shapes[1]), ANY]
         + [whole_spec(s) for s in shapes[3:6]]
-        + [by_pair((width, part)), saved, saved],
+        + [by_pair((width, part)), saved],
         scratch_shapes=[pltpu.VMEM(*s) for s in scratch]
         + [
             pltpu.SemaphoreType.DMA((copies,)),
@@ -1348,7 +1373,7 @@
             collective_id=2, has_side_effects=True, vmem_limit_bytes=VMEM_LIMIT
         ),
         name="backward",
-    )(*arrays, *streamed, own_hid, *weights)
+    )(*arrays, *streamed, own_hid, mask, *weights)
 
 
 def weights_kernel(
@@ -1360,11 +1385,9 @@
     gains_ref,
     out_in_ref,
     in_in_ref,
-    dgp_ref,
-    dup_ref,
+    dgu_ref,
     down_ref,
-    dgp_rest,
-    dup_rest,
+    dgu_rest,
     gate_grad_ref,
     up_grad_ref,
     down_grad_ref,
@@ -1382,7 +1405,7 @@
     step = pl.program_id(0)
     c = place_ref[1]
     width = gate_grad_ref.shape[2]
-    plane_rows = dgp_ref.shape[0]
+    plane_rows = dgu_ref.shape[0]
 
     @pl.when(step == 0)
     def _():
@@ -1401,26 +1424,23 @@
         ga_grad_ref[...] = gains[0:1, :]
         gm_grad_ref[...] = gains[1:2, :]
 
-    def contract(own, rest):
-        return dot(xt_buf[:, :plane_rows], own[...]) + dot(xt_buf[:, plane_rows:], rest[...])
-
-    gate_both = contract(dgp_ref, dgp_rest)
-    up_both = contract(dup_ref, dup_rest)
     down_grad_ref[...] = down_ref[...]
     for k in range(2):
-        lanes = slice(k * width, (k + 1) * width)
-        gate_grad_ref[k] = gate_both[:, lanes]
-        up_grad_ref[k] = up_both[:, lanes]
-
-
-def weight_grads(place, x, sides, own, rest, count, kv_width, experts):
+        lanes = slice(2 * k * width, 2 * (k + 1) * width)
+        both = dot(xt_buf[:, :plane_rows], dgu_ref[:, lanes])
+        both = both + dot(xt_buf[:, plane_rows:], dgu_rest[:, lanes])
+        gate_grad_ref[k] = both[:, :width]
+        up_grad_ref[k] = both[:, width:]
+
+
+def weight_grads(place, x, sides, own, down, rest, kv_width, experts):
     rows = x.shape[0]
     _, qkv_grad, o_grad, gains, output, _ = sides
-    width = own[0].shape[1] // count
+    count, width, _ = down.shape
     part = gains.shape[1]
     q_width, half = o_grad.shape[1], part // 2
     by_pair = lambda shape: pl.BlockSpec((2,) + shape, lambda i, p: (i, 0, 0))
-    saved = lambda a: pl.BlockSpec((a.shape[0], 2 * width), lambda i, p: (0, i))
+    saved = lambda a: pl.BlockSpec((a.shape[0], 4 * width), lambda i, p: (0, i))
     columns = pl.BlockSpec((rows, part), lambda i, p: (0, p[0]), pipeline_mode=pl.Buffered(1))
     shapes = [
         (count, part, width),
@@ -1443,9 +1463,7 @@
             grid=(count // 2,),
             in_specs=[columns]
             + [whole_spec(a) for a in sides]
-            + [saved(a) for a in own]
-            + [by_pair((width, part))]
-            + [saved(a) for a in rest[1:]],
+            + [saved(own), by_pair((width, part)), saved(rest)],
             out_specs=[by_pair((part, width)), by_pair((part, width)), by_pair((width, part))]
             + [whole_spec(s) for s in shapes[3:]],
             scratch_shapes=[pltpu.VMEM((part, rows), BF16)],
@@ -1453,7 +1471,7 @@
         out_shape=shapes,
         compiler_params=pltpu.CompilerParams(vmem_limit_bytes=VMEM_LIMIT),
         name="weight_grads",
-    )(place, x, *sides, *own, *rest)
+    )(place, x, *sides, own, down, rest)
 
 
 def rope_rows(length):
@@ -1486,12 +1504,12 @@
     ga, gm = gain_attn, gain_moe
     wr = w_router.T
     heads = (w_query, key_projection, value_projection, w_out)
-    x_all, g_all, moe, back, dgate, gates, h1, *saved, ghid, dgp, dup, place = front(
+    x_all, g_all, moe, back, dgate, gates, h1, *saved, ghid, dgu, mask, place = front(
         dp, tp, (tokens, cotangent, routes.T, ga, gm, wr, *heads, rope), (w_gate, w_up, w_down)
     )
     local = (back, moe, dgate, gates, h1, tokens, cotangent, ga, gm, wr, *heads)
-    output, input_grad, d_logits, qkv_grad, o_grad, gains, *rest = backward(
-        dp, tp, (*local, *saved, rope), (x_all, g_all), ghid, (w_gate, w_up, w_down)
+    output, input_grad, d_logits, qkv_grad, o_grad, gains, down, dgu_rest = backward(
+        dp, tp, (*local, *saved, rope), (x_all, g_all), ghid, mask, (w_gate, w_up, w_down)
     )
     (
         gate_grad,
@@ -1510,9 +1528,9 @@
         place,
         x_all,
         (d_logits, qkv_grad, o_grad, gains, output, input_grad),
-        (dgp, dup),
-        rest,
-        w_gate.shape[0],
+        dgu,
+        down,
+        dgu_rest,
         key_projection.shape[1],
         experts,
     )

time: 187 us -> 186 us (level)
  no operation moved by 1% of the time
where the time goes in v7:
time: 186 us
  Pallas kernels  185 us (99%)
    pallas_call x1, Pallas kernels, backward(): pl.pallas_call(functools.partial(backward_kernel, dp, tp), grid=(count //...  87.4 us
    pallas_call x1, Pallas kernels, front(): pl.pallas_call(functools.partial(front_kernel, dp, tp), grid=(2 * pairs,)...  75.3 us
    pallas_call x1, Pallas kernels, weight_grads(): pl.pallas_call(weights_kernel, grid_spec=pltpu.PrefetchScalarGridSpec(num...  22.2 us

profile of v7, /device:TPU:0, one launch (start us, length us, event | category | flops | bytes accessed | tf_op | source)
XLA Modules:
  0.0 185.7 jit_solution(4425333647292363020)
XLA Ops:
  0.6 75.3 %front.1 = (bf16[2048,1536]{1,0:T(8,128)(2,1)}, bf16[2048,1536]{1,0:T(8,128)(2,1)}, bf16[512,1536]{1,0:T(8,128)(2,1)}, bf16[512,1536]{1,0:T(8,128)(2,1)}, f32[51...) custom-call(bf16[256,1536]{1,0:T(8,128)(2,1)} %tok_hbm.1, ...), custom_call_target="tpu_custom_call" | custom-call | tf_op jit(solution)/shard_map/front/pallas_call | solution.py:884
  75.9 87.4 %backward.1 = (bf16[256,1536]{1,0:T(8,128)(2,1)}, bf16[256,1536]{1,0:T(8,128)(2,1)}, bf16[2048,128]{1,0:T(8,128)(2,1)}, f32[192,640]{1,0:T(8,128)}, f32[192,384]...) custom-call(bf16[512,1536]{1,0:T(8,128)(2,1)} %get-tuple-element.52.back_hbm, ...), custom_call_target="tpu_custom_call" | custom-call | tf_op jit(solution)/shard_map/backward/pallas_call | solution.py:1355
  163.4 22.2 %weight_grads.1 = (f32[20,384,128]{2,1,0:T(8,128)}, f32[20,384,128]{2,1,0:T(8,128)}, f32[20,128,384]{2,1,0:T(8,128)}, f32[192,384]{1,0:T(8,128)}, f32[192,128]{1...) custom-call(s32[2]{0:T(128)} %get-tuple-element.50.place_ref, ...), custom_call_target="tpu_custom_call" | custom-call | tf_op jit(solution)/shard_map/weight_grads/pallas_call | solution.py:1459
